TPU v7x, 128 devices: a whole 4x4x4 slice. The times are simulated.
128 devices in a mesh: vx: 8 (over x, z_hi), vy: 16 (over z_lo, y, core).
Axes of the slice: x: 4, y: 4, z: 4 (z_hi: 2, z_lo: 2; z = z_hi * 2 + z_lo), core: 2. Of those that a mesh axis runs over, the one named last changes fastest.
Arguments:
- tokens: bfloat16 [128, 1, 1024, 1024], P(('vx', 'vy')), may hold values from -256 to 256
- var_embed: bfloat16 [91, 1024], replicated, may hold values from -2 to 2
- query: bfloat16 [1024], replicated, may hold values from -6 to 6
- key_weight: bfloat16 [1024, 1024], P('vy'), may hold values from -1 to 1
- value_weight: bfloat16 [1024, 1024], P('vy'), may hold values from -0.1875 to 0.1875
- out_weight: bfloat16 [1024, 1024], P('vy'), may hold values from -0.1875 to 0.1875
- var_slot: int32 [91], replicated, may hold values from 0 to 127, as said below
Outputs:
- aggregated: bfloat16 [1, 1024, 1024], P(None, ('vx', 'vy'))
Inputs may be any that keep to these rules, and one draw needn't show every extreme that they name: `var_slot`: distinct slot numbers; at least one device's slot holds a variable.
All inputs are finite; a program needn't handle non-finite values.
Results may differ from a plain program's by a relative error of at most 0.0096.
Values may be sent and summed in bfloat16 or wider, within the bound.
A program may use at most 64 MiB of HBM per device.

v0:
```python
import math

import jax
import jax.numpy as jnp
from jax import lax
from jax.sharding import PartitionSpec as P

HEADS = 16


def side_by_side(arrays, axis, dim, along):
    widths = [a.shape[along] for a in arrays]
    both = jnp.concatenate(arrays, axis=along)
    result = lax.all_gather(both, axis, axis=dim, tiled=True)
    return tuple(jnp.split(result, [sum(widths[:k]) for k in range(1, len(widths))], axis=along))


def split_up(array, dim, size):
    lengths = array.shape
    pieces = array.reshape(*lengths[:dim], size, lengths[dim] // size, *lengths[dim + 1 :])
    return jnp.moveaxis(pieces, dim, 0)


def joined_along(pieces, dim):
    pieces = jnp.moveaxis(pieces, 0, dim)
    lengths = pieces.shape
    return pieces.reshape(*lengths[:dim], lengths[dim] * lengths[dim + 1], *lengths[dim + 2 :])


def joined_exchange(array, axis, axes, splits, concats):
    sizes = [lax.axis_size(a) for a in axes]
    pieces = split_up(array, splits[0], sizes[0])
    pieces = jnp.moveaxis(split_up(pieces, splits[1] + 1, sizes[1]), 0, 1)
    inside = pieces.shape[2:]
    pieces = pieces.reshape(-1, *inside)
    pieces = lax.all_to_all(pieces, axis, split_axis=0, concat_axis=0, tiled=True)
    pieces = joined_along(pieces.reshape(*sizes, *inside), concats[0] + 1)
    return joined_along(pieces, concats[1])


def attend(keys, values, query_matrix, scale, heads):
    scores = (
        jnp.einsum("vbpd,dh->vbph", keys, query_matrix, preferred_element_type=jnp.float32) * scale
    )
    highest = jnp.max(scores, axis=0, keepdims=True)
    exponent = jnp.exp(scores - highest)
    weights = (exponent / jnp.sum(exponent, axis=0, keepdims=True)).astype(jnp.bfloat16)
    shaped = values.reshape(values.shape[:3] + (heads, values.shape[3] // heads))
    context = jnp.einsum("vbph,vbphe->bphe", weights, shaped, preferred_element_type=jnp.float32)
    return context.astype(jnp.bfloat16).reshape(values.shape[1:])


def shards(tokens, var_embed, query, key_weight, value_weight, out_weight, var_slot):
    slot_dev, batch, patches, width = tokens.shape
    heads = HEADS
    scale = 1.0 / math.sqrt(width // heads)
    count_x = lax.axis_size("vx")
    count_y = lax.axis_size("vy")
    position = lax.axis_index("vx") * count_y + lax.axis_index("vy")
    local_slots = position * slot_dev + jnp.arange(slot_dev, dtype=jnp.int32)
    slot_match = (local_slots[:, None] == var_slot[None, :]).astype(jnp.bfloat16)
    embed_rows = jnp.dot(slot_match, var_embed, preferred_element_type=jnp.float32)
    mixed = (tokens.astype(jnp.float32) + embed_rows[:, None, None, :]).astype(jnp.bfloat16)
    key_full, value_full = side_by_side((key_weight, value_weight), "vy", 0, 1)
    stacked = jnp.stack((key_full, value_full))
    head_of = jnp.arange(width, dtype=jnp.int32) // (width // heads)
    query_matrix = jnp.where(
        head_of[:, None] == jnp.arange(heads, dtype=jnp.int32)[None, :],
        query[:, None],
        jnp.zeros((), jnp.bfloat16),
    )
    outgoing = mixed[None]
    slot_owner = var_slot // slot_dev
    slot_pos = (
        slot_owner % count_y * count_x * slot_dev
        + slot_owner // count_y * slot_dev
        + var_slot % slot_dev
    )
    selected = jnp.take(
        joined_exchange(outgoing, ("vx", "vy"), ("vx", "vy"), (3, 3), (1, 1)), slot_pos, axis=1
    )
    projected = jnp.einsum(
        "vbpd,cde->cvbpe", selected[0], stacked, preferred_element_type=jnp.float32
    ).astype(jnp.bfloat16)
    keys = projected[0]
    values = projected[1]
    context = attend(keys, values, query_matrix, scale, heads)
    flattened = context.reshape(-1, width)
    result = jnp.dot(
        flattened,
        lax.all_gather(out_weight, "vy", axis=0, tiled=True),
        preferred_element_type=jnp.float32,
    )
    return result.astype(jnp.bfloat16).reshape(batch, -1, width)


def solution(mesh):
    placed = (
        P(("vx", "vy"), None, None, None),
        P(),
        P(),
        P("vy", None),
        P("vy", None),
        P("vy", None),
        P(),
    )
    return jax.shard_map(
        shards, mesh=mesh, in_specs=placed, out_specs=P(None, ("vx", "vy"), None), check_vma=False
    )
```

profile of v0, /device:TPU:0, one launch (start us, length us, event | category | flops | bytes accessed | tf_op | source)
XLA Modules:
  0.0 115.2 jit_solution(9693294114337851187)
XLA Ops:
  6.5 0.0 copy-start
  6.5 0.0 all-gather.3.cloned.1.call-start
  6.5 1.8 %pad_maximum_fusion = bf16[64,2048]{1,0:T(8,128)(2,1)} fusion(bf16[64,1024]{1,0:T(8,128)(2,1)} %param.11, bf16[64,1024]{1,0:T(8,128)(2,1)} %param.10), kind=kLoop, calls=%fused_computation.25 | loop fusion | flops 524288 | bytes 524288 | tf_op jit(solution)/shard_map/concatenate | solution.py:13
  8.3 0.0 all-gather.3.cloned.1.call-update
  8.3 0.0 copy-done
  8.3 0.8 fusion.27
  9.1 3.5 %fusion.5 = bf16[128,1,1,1,8,1024]{5,4,3,2,1,0:T(8,128)(2,1)} fusion(bf16[1,1,1024,1024]{3,2,1,0:T(8,128)(2,1)} %param.7, f32[1024]{0:T(1024)S(1)} %bitcast.59), kind=kLoop, calls=%fused_computation.9 | loop fusion | flops 3145728 | bytes 4198400 | tf_op jit(solution)/shard_map/reshape;transpose;transpose;reshape;transpose;reshape;broadcast_in_dim | solution.py:35
  12.7 0.0 copy-start.3
  12.7 11.2 %all-to-all-start = ((bf16[128,1,1,1,8,1024]{5,4,3,2,1,0:T(8,128)(2,1)}), bf16[128,1,1,1,8,1024]{5,4,3,2,1,0:T(8,128)(2,1)S(1)}, u32[]{:S(2)}, u32[]{:S(2)}) async-start(bf16[128,1,1,1,8,1024]{5,4,3,2,1,0:T(8,128)(2,1)} %fusion.5), calls=%async_computation | async-start | bytes 4194304 | tf_op jit(solution)/shard_map/all_to_all | solution.py:36
  23.8 0.0 all-gather.5.cloned.1.call-start
  23.9 0.7 all-gather.5.cloned.1.call-update
  24.6 0.0 copy-done.3
  24.6 29.6 %all-to-all-done = bf16[128,1,1,1,8,1024]{5,4,3,2,1,0:T(8,128)(2,1)S(1)} async-done(((bf16[128,1,1,1,8,1024]{5,4,3,2,1,0:T(8,128)(2,1)}), bf16[128,1,1,1,8,1024]{5,4,3,2,1,0:T(8,128)(2,1)S(1)}, u32[]{:S(2)}, u32[]{:S(2)}) %all-to-all-start) | async-done | bytes 2097184 | tf_op jit(solution)/shard_map/all_to_all | solution.py:36
  54.2 1.6 %copy.15 = bf16[16,1,8,1,1,8,1024]{6,5,2,0,4,3,1:T(8,128)(2,1)} copy(bf16[16,1,8,1,1,8,1024]{6,5,0,2,4,3,1:T(8,128)(2,1)S(1)} %bitcast.55) | data formatting | bytes 4194304 | tf_op jit(solution)/shard_map/transpose | solution.py:25
  55.8 2.3 %gather_fusion = bf16[91,8,1024]{2,1,0:T(8,128)(2,1)S(1)} fusion(bf16[128,8,1024]{2,1,0:T(8,128)(2,1)} %bitcast.56, s32[1024]{0:T(1024)S(1)} %pad_clamp_fusion), kind=kCustom, calls=%fused_computation | custom fusion | bytes 2982252 | tf_op jit(solution)/shard_map/jit(_take)/gather | solution.py:79
  58.1 0.2 broadcast_select_fusion
  58.4 12.0 %all-gather.3.cloned.1.call-done = bf16[1024,2048]{1,0:T(8,128)(2,1)} async-done(((bf16[64,2048]{1,0:T(8,128)(2,1)}), bf16[1024,2048]{1,0:T(8,128)(2,1)}) %all-gather.3.cloned.1.call-update) | async-done | bytes 4194320 | tf_op jit(solution)/shard_map/all_gather | solution.py:14
  70.4 2.7 %slice_bitcast_fusion.1 = (bf16[1,1024,1024]{2,1,0:T(8,128)(2,1)S(1)}, bf16[1,1024,1024]{2,1,0:T(8,128)(2,1)S(1)}) fusion(bf16[1024,2048]{1,0:T(8,128)(2,1)} %all-gather.3.cloned.1.call-done), kind=kLoop, calls=%fused_computation.11 | loop fusion | bytes 8388608 | tf_op jit(solution)/shard_map/stack | solution.py:65
  73.1 4.5 %convert_bitcast_fusion = bf16[2,91,1,8,1024]{4,1,3,0,2:T(8,128)(2,1)S(1)} fusion(bf16[1,1024,1024]{2,1,0:T(8,128)(2,1)S(1)} %get-tuple-element.8, bf16[1,1024,1024]{2,1,0:T(8,128)(2,1)S(1)} %get-tuple-element.7, bf16[91,8,1024]{2,1,0:T(8,128)(2,1)S(1)} %broadcast_select_fusion), kind=kOutput, calls=%fused_computation.8 | convolution fusion | flops 3063332864 | bytes 8667136 | tf_op jit(solution)/shard_map/vbpd,cde->cvbpe/dot_general | solution.py:82
  77.6 0.0 copy-start.2
  77.6 1.6 %copy-done.2 = bf16[2,91,1,8,1024]{4,1,3,0,2:T(8,128)(2,1)} copy-done((bf16[2,91,1,8,1024]{4,1,3,0,2:T(8,128)(2,1)}, bf16[2,91,1,8,1024]{4,1,3,0,2:T(8,128)(2,1)S(1)}, u32[]{:S(2)}) %copy-start.2) | copy-done | bytes 2981912
  79.2 0.1 slice.11
  79.4 0.0 copy-start.4
  79.4 2.5 %copy.17 = bf16[1,91,1,8,1024]{1,4,3,2,0:T(8,128)(2,1)} copy(bf16[1,91,1,8,1024]{4,1,3,0,2:T(8,128)(2,1)S(1)} %slice.11) | data formatting | bytes 2981888 | tf_op jit(solution)/shard_map/slice | solution.py:86
  81.9 0.0 copy-done.4
  81.9 0.0 copy-start.1
  81.9 2.3 %fusion.14 = bf16[91,8,16,1]{0,2,1,3:T(8,128)(2,1)S(1)} fusion(bf16[2,91,1,8,1024]{4,1,3,0,2:T(8,128)(2,1)} %copy-done.2, s32[1024]{0:T(1024)S(1)} %add_select_fusion, bf16[1024]{0:T(1024)(128)(2,1)S(1)} %copy-done.4), kind=kOutput, calls=%fused_computation.22 | convolution fusion | flops 23934900 | bytes 1602304 | tf_op jit(solution)/shard_map/div | solution.py:47
  84.2 0.0 copy-done.1
  84.2 1.2 %fusion.16 = f32[8,16,1,64]{3,2,1,0:T(1,128)S(1)} fusion(bf16[91,8,16,64]{0,3,2,1:T(8,128)(2,1)S(1)} %bitcast.57, bf16[91,8,16,1]{0,2,1,3:T(8,128)(2,1)S(1)} %fusion.14), kind=kOutput, calls=%fused_computation.26 | convolution fusion | flops 1490944 | bytes 1547008 | tf_op jit(solution)/shard_map/vbph,vbphe->bphe/dot_general | solution.py:49
  85.4 0.1 reshape_reshape.3
  85.5 20.2 %all-gather.5.cloned.1.call-done = bf16[1024,1024]{1,0:T(8,128)(2,1)} async-done(((bf16[64,1024]{1,0:T(8,128)(2,1)}), bf16[1024,1024]{1,0:T(8,128)(2,1)}) %all-gather.5.cloned.1.call-update) | async-done | bytes 2097168 | tf_op jit(solution)/shard_map/all_gather | solution.py:91
  105.7 2.6 %fusion.15 = bf16[1,8,1024]{2,1,0:T(8,128)(2,1)} fusion(bf16[8,1024]{1,0:T(8,128)(2,1)S(1)} %reshape_reshape.3, bf16[1024,1024]{1,0:T(8,128)(2,1)} %all-gather.5.cloned.1.call-done), kind=kOutput, calls=%fused_computation.24 | convolution fusion | flops 16785408 | bytes 2129920 | tf_op jit(solution)/shard_map/dot_general | solution.py:89
  (4 shorter events, 0.0 us)
Async XLA Ops:
  6.5 1.8 %copy-start = (bf16[91,1024]{1,0:T(8,128)(2,1)S(1)}, bf16[91,1024]{1,0:T(8,128)(2,1)}, u32[]{:S(2)}) copy-start(bf16[91,1024]{1,0:T(8,128)(2,1)} %param.8) | copy-start | bytes 559108
  6.5 63.9 %all-gather.3.cloned.1.call-start = ((), (), s32[]{:S(2)}) async-start(), calls=%async_computation.1 | async-start | bytes 4456448 | tf_op jit(solution)/shard_map/all_gather | solution.py:14
  12.7 11.9 %copy-start.3 = (s32[91]{0:T(128)S(1)}, s32[91]{0:T(128)}, u32[]{:S(2)}) copy-start(s32[91]{0:T(128)} %param.13) | copy-start | bytes 1096
  12.7 41.6 %all-to-all-start = ((bf16[128,1,1,1,8,1024]{5,4,3,2,1,0:T(8,128)(2,1)}), bf16[128,1,1,1,8,1024]{5,4,3,2,1,0:T(8,128)(2,1)S(1)}, u32[]{:S(2)}, u32[]{:S(2)}) async-start(bf16[128,1,1,1,8,1024]{5,4,3,2,1,0:T(8,128)(2,1)} %fusion.5), calls=%async_computation | async-start | bytes 4194304 | tf_op jit(solution)/shard_map/all_to_all | solution.py:36
  23.8 81.9 %all-gather.5.cloned.1.call-start = ((), (), s32[]{:S(2)}) async-start(), calls=%async_computation.2 | async-start | bytes 2228224 | tf_op jit(solution)/shard_map/all_gather | solution.py:91
  77.6 1.6 %copy-start.2 = (bf16[2,91,1,8,1024]{4,1,3,0,2:T(8,128)(2,1)}, bf16[2,91,1,8,1024]{4,1,3,0,2:T(8,128)(2,1)S(1)}, u32[]{:S(2)}) copy-start(bf16[2,91,1,8,1024]{4,1,3,0,2:T(8,128)(2,1)S(1)} %convert_bitcast_fusion) | copy-start | bytes 8945668
  79.4 2.5 %copy-start.4 = (bf16[1024]{0:T(1024)(128)(2,1)S(1)}, bf16[1024]{0:T(1024)(128)(2,1)}, u32[]{:S(2)}) copy-start(bf16[1024]{0:T(1024)(128)(2,1)} %param.9) | copy-start | bytes 6148
  81.9 2.3 %copy-start.1 = (bf16[1,91,1,8,1024]{1,4,3,2,0:T(8,128)(2,1)S(1)}, bf16[1,91,1,8,1024]{1,4,3,2,0:T(8,128)(2,1)}, u32[]{:S(2)}) copy-start(bf16[1,91,1,8,1024]{1,4,3,2,0:T(8,128)(2,1)} %copy.17) | copy-start | bytes 4472836
Sparse Core Ops, SparseCore 0:
  9.0 61.3 all-gather.2
  72.1 33.5 all-gather.4
where the time goes:
time: 117 us; the launch traced here: 115 us
  waiting for transfers between devices  62.5 us (53%)
  between operations  13.5 us (12%)
  matrix products  11.4 us (10%)
  starting transfers between devices  11.2 us (10%)
  local copies, waits for them, and re-layouts  11 us (9%)
  other arithmetic  5.52 us (5%)
    all_to_all x1, waiting for transfers between devices, joined_exchange(): lax.all_to_all(pieces, axis, split_axis=0, concat_axis=0, tiled=True)  29.6 us
    all_gather x1, waiting for transfers between devices, shards(): lax.all_gather(out_weight, 'vy', axis=0, tiled=True)  20.2 us
    all_gather x1, waiting for transfers between devices, side_by_side(): result = lax.all_gather(both, axis, axis=dim, tiled=True)  12 us
    all_to_all x1, starting transfers between devices, joined_exchange(): lax.all_to_all(pieces, axis, split_axis=0, concat_axis=0, tiled=True)  11.2 us
    dot_general x1, matrix products, shards(): jnp.einsum('vbpd,cde->cvbpe', selected[0], stacked, preferred_element_typ...  4.51 us
    another operation x1, other arithmetic, joined_exchange(): pieces = pieces.reshape(-1, *inside)  3.51 us
    another operation x1, local copies, waits for them, and re-layouts, shards(): stacked = jnp.stack((key_full, value_full))  2.66 us
    slice x2, local copies, waits for them, and re-layouts, shards(): values = projected[1]  2.65 us
  transfers between devices with their start and end apart: 3, of which 3 were waited for; matrix products, arithmetic and copies ran while one was open for 19% of the time, Pallas kernels for 0%

commit v1 on v0

v1 whole, which is shorter than its diff:
```python
import functools

import jax
import jax.numpy as jnp
from jax import lax
from jax.experimental import pallas as pl
from jax.experimental.pallas import tpu as pltpu
from jax.sharding import PartitionSpec as P

MESH = pl.DeviceIdType.MESH
F32, BF16 = jnp.float32, jnp.bfloat16
HEADS = 16
D = 1024
BIG = -1e30

NAT = ("x", "z", "y")
PARTS = ((0, 512, ("x", "y", "z")), (512, 512, ("y", "x", "z")))
SEND_SEMS = 200
DIRECT_OPP = False


def device_of(x, y, z, c):
    return (x * 2 + z // 2, (z % 2) * 8 + y * 2 + c)


class Copies:
    def __init__(self, send, recv, local):
        self.send, self.recv, self.local = send, recv, local
        self.n, self.k, self.open = 0, 0, []

    def remote(self, src, dst, device):
        copy = pltpu.make_async_remote_copy(
            src_ref=src,
            dst_ref=dst,
            send_sem=self.send.at[self.n],
            recv_sem=self.recv.at[self.n],
            device_id=device,
            device_id_type=MESH,
        )
        self.n += 1
        copy.start()
        self.open.append(copy)
        return copy

    def here(self, src, dst):
        copy = pltpu.make_async_copy(src, dst, self.local.at[self.k])
        self.k += 1
        copy.start()
        return copy


def lanes_iota(rows):
    return lax.broadcasted_iota(jnp.int32, (rows, 128), 1)


def hilo(a):
    lane = lanes_iota(a.shape[0])
    high = a.astype(BF16).astype(F32)
    low = pltpu.roll(a - high, 16, axis=1)
    both = jnp.where(lane < 16, high, jnp.where(lane < 32, low, 0.0))
    return both.astype(BF16)


def fold(rows):
    lane = lanes_iota(rows.shape[0])
    rows = jnp.where(lane < 32, rows, 0.0)
    q = rows.shape[0] // 4
    out = rows[:q]
    for g in range(1, 4):
        out = out + pltpu.roll(rows[g * q : (g + 1) * q], 32 * g, axis=1)
    return out


def unfold(packed):
    pieces = [packed]
    for g in range(1, 4):
        pieces.append(pltpu.roll(packed, 128 - 32 * g, axis=1))
    return jnp.concatenate(pieces, axis=0)


def pack_stats(m, l):
    lane = lanes_iota(m.shape[0])
    return jnp.where(lane < 16, m, jnp.where(lane < 32, pltpu.roll(l, 16, axis=1), 0.0))


def merge_stats(stats):
    m = functools.reduce(jnp.maximum, stats)
    scales = [jnp.exp(s - m) for s in stats]
    l = sum(a * pltpu.roll(s, 112, axis=1) for a, s in zip(scales, stats))
    return m, l, scales


def pick(ref, axis, index, lanes, ndim):
    where = [slice(None)] * (ndim + 2)
    where[axis] = index
    where[-1] = lanes
    got = ref[tuple(where)]
    return got.reshape(-1, got.shape[-1])


def kernel(tok, emb, query, wk, wv, wo, vslot, out, wk_v, tokv, mixed, gv, go, V, Pacc, wx, st0, qk_o, qk_p, qkc,
           qkg, qkt, e2, er, used, sc, *rest):
    ssem, rsem, lsem = rest[-3:]
    per_part = [rest[i * 17 : (i + 1) * 17] for i in range(len(PARTS))]
    names = ("s1", "r1", "s2", "r2", "s3", "r3", "m1", "m2", "ts1", "tr1", "ts2", "tr2", "ts3", "tr3", "ax1", "ax2", "ax3")
    T = [dict(zip(names, p)) for p in per_part]
    cp = Copies(ssem, rsem, lsem)

    vx, vy = lax.axis_index("vx"), lax.axis_index("vy")
    x, z = vx // 2, (vx % 2) * 2 + vy // 8
    y, c = (vy // 2) % 4, vy % 2
    zl = z % 2
    zmate = z + 1 - 2 * zl
    me = {"x": x, "y": y, "z": z}

    def peer(dim, offset):
        at = dict(me)
        at[dim] = (me[dim] + offset) % 4
        return device_of(at["x"], at["y"], at["z"], c)

    other = device_of(x, y, z, 1 - c)
    chips = [device_of(x, y, zmate, c)]
    for o in (1, 2, 3):
        chips.append(device_of(x, (y + o) % 4, z, c))
        chips.append(device_of(x, (y + o) % 4, zmate, c))

    load_wk = cp.here(wk, wk_v)
    load_tok = cp.here(tok.at[:, c], tokv.at[0])

    barrier = pltpu.get_barrier_semaphore()
    partners = [other] + [peer(d, o) for d in ("x", "y", "z") for o in (1, 2, 3)]
    partners += [device_of(x, (y + o) % 4, zmate, c) for o in (1, 2, 3)]
    for p in partners:
        pl.semaphore_signal(barrier, inc=1, device_id=p, device_id_type=MESH)

    def row_of(yy, zz, cc):
        return pl.multiple_of(((zz * 4 + yy) * 2 + cc) * 64, 64)

    load_wv = cp.here(wv, gv.at[pl.ds(row_of(y, zl, c), 64), :])
    load_wo = cp.here(wo, go.at[pl.ds(row_of(y, zl, c), 64), :])

    head_lane = lax.broadcasted_iota(jnp.int32, (HEADS, D), 1) // 64
    head_row = lax.broadcasted_iota(jnp.int32, (HEADS, D), 0)
    own_head = head_lane == head_row
    q_matrix = jnp.where(own_head, query[...].astype(F32), 0.0).astype(BF16)
    load_wk.wait()
    nt = (((1,), (1,)), ((), ()))
    qk = lax.dot_general(q_matrix, wk_v[...], nt, preferred_element_type=F32) * 0.125
    qk_hi = qk.astype(BF16)
    qk_lo = (qk - qk_hi.astype(F32)).astype(BF16)
    qk_both = jnp.concatenate([qk_hi, qk_lo], axis=0)
    qk_o[...] = qk_both

    ones = own_head.astype(F32).astype(BF16)
    e2[...] = jnp.concatenate([ones, ones, jnp.zeros((96, D), BF16)], axis=0)
    position = vx * 16 + vy
    partner_pos = position + 1 - 2 * c
    n_vars = vslot.shape[1]
    row8 = lax.broadcasted_iota(jnp.int32, (8, n_vars), 0)
    slot_id = jnp.where(row8 == 0, position, jnp.where(row8 == 1, partner_pos, -1))
    match = (vslot[...] == slot_id).astype(F32)
    er[...] = jnp.dot(match.astype(BF16), emb[...], preferred_element_type=F32)
    used[...] = jnp.broadcast_to(jnp.sum(match, axis=1, keepdims=True), (8, 128))

    pl.semaphore_wait(barrier, len(partners))

    qk_copy = cp.remote(qk_o, qk_p, other)
    tok_copy = cp.remote(tok.at[:, 1 - c], tokv.at[1], other)

    class Gather:
        def __init__(self, src, g, local):
            self.src, self.g = src, g
            local.wait()
            own = row_of(y, zl, c)
            self.from_left = self.put(own, 64, peer("y", 1))
            self.from_right = self.put(own, 64, peer("y", 3))
            self.own_z = self.halves(y)
            self.core = {0: self.put(own, 64, other)}
            self.core_z, self.z = {}, {}

        def put(self, row, rows, device):
            ref = self.g.at[pl.ds(row, rows), :]
            return cp.remote(ref, ref, device)

        def halves(self, yy):
            row = row_of(yy, zl, c)
            return (self.put(row, 32, peer("z", 1)), self.put(pl.multiple_of(row + 32, 32), 32, peer("z", 3)))

        def y_arrived(self):
            self.from_left.wait_recv()
            left = (y + 3) % 4
            self.opp_a = self.put(row_of(left, zl, c), 32, peer("y", 1))
            self.from_right.wait_recv()
            right = (y + 1) % 4
            self.opp_b = self.put(pl.multiple_of(row_of(right, zl, c) + 32, 32), 32, peer("y", 3))

        def y_to_z(self):
            for o in (3, 1):
                self.z[o] = self.halves((y + o) % 4)

        def y_to_core(self):
            for o in (3, 1):
                self.core[o] = self.put(row_of((y + o) % 4, zl, c), 64, other)

        def opp_arrived(self):
            self.opp_a.wait_recv()
            self.opp_b.wait_recv()

        def opp_to_z(self):
            self.z[2] = self.halves((y + 2) % 4)

        def opp_to_core(self):
            self.core[2] = self.put(row_of((y + 2) % 4, zl, c), 64, other)

        def z_arrived(self, o):
            pair = self.own_z if o == 0 else self.z[o]
            pair[0].wait_recv()
            pair[1].wait_recv()
            self.core_z[o] = self.put(row_of((y + o) % 4, 1 - zl, c), 64, other)

        def complete(self, o):
            self.core[o].wait_recv()
            self.core_z[o].wait_recv()

    A = Gather(wv, gv, load_wv)

    qk_copy.wait_recv()
    qk_other = qk_p[...]
    first = jnp.where(c == 0, qk_both.astype(F32), qk_other.astype(F32))
    second = jnp.where(c == 0, qk_other.astype(F32), qk_both.astype(F32))
    qkc[...] = jnp.concatenate([first, second], axis=1).astype(BF16)
    chip = zl * 4 + y
    qk_copies = [cp.remote(qkc, qkg.at[chip], p) for p in chips]

    def mix(k):
        def step(i, carry):
            t = tokv[k, pl.ds(i * 8, 8)].astype(F32).reshape(64, D)
            mixed[pl.ds(pl.multiple_of(k * 512 + i * 64, 64), 64), :] = (t + er[k : k + 1, :]).astype(BF16)
            return carry

        lax.fori_loop(0, 8, step, 0)

    load_tok.wait()
    mix(0)
    tok_copy.wait_recv()
    mix(1)

    A.y_arrived()
    A.y_to_z()
    A.y_to_core()
    B = Gather(wo, go, load_wo) if False else None

    for k in qk_copies:
        k.wait_recv()
    qkg[chip] = qkc[...]
    qkt[...] = jnp.concatenate(
        [jnp.concatenate([qkg[i] for i in range(8)], axis=1), jnp.zeros((96, D), BF16)], axis=0
    )

    def score(i, carry):
        rows = pl.multiple_of(i * 128, 128)
        d = lax.dot_general(mixed[pl.ds(rows, 128), :], qkt[...], nt, preferred_element_type=F32)
        sc[i] = d + pltpu.roll(d, 112, axis=1)
        return carry

    lax.fori_loop(0, 8, score, 0)
    use0, use1 = used[0:1, :], used[1:2, :]

    def pair(i, carry):
        s0 = jnp.where(use0 > 0, sc[i], BIG)
        s1 = jnp.where(use1 > 0, sc[4 + i], BIG)
        m = jnp.maximum(s0, s1)
        w0 = use0 * jnp.exp(s0 - m)
        w1 = use1 * jnp.exp(s1 - m)
        st0[i] = pack_stats(m, w0 + w1).reshape(4, 4, 8, 128)
        rows = pl.ds(pl.multiple_of(i * 128, 128), 128)
        wx[0, rows, :] = jnp.dot(hilo(w0), e2[...], preferred_element_type=F32)
        wx[1, rows, :] = jnp.dot(hilo(w1), e2[...], preferred_element_type=F32)
        return carry

    lax.fori_loop(0, 4, pair, 0)

    for t, (l0, w, dims) in zip(T, PARTS):
        axis = NAT.index(dims[0])
        t["sc1"] = []
        for o in (1, 2, 3):
            rows = pick(st0, axis, (me[dims[0]] + o) % 4, slice(None), 3)
            t["ts1"][o - 1] = fold(rows)
            t["sc1"].append(cp.remote(t["ts1"].at[o - 1], t["tr1"].at[o - 1], peer(dims[0], o)))

    def expand(a, l0, w):
        return jnp.dot(hilo(a), e2[:, l0 : l0 + w], preferred_element_type=F32)

    def stats1():
        for t, (l0, w, dims) in zip(T, PARTS):
            for k in t["sc1"]:
                k.wait_recv()
            own = pick(st0, NAT.index(dims[0]), me[dims[0]], slice(None), 3)
            m, l, scales = merge_stats([own] + [unfold(t["tr1"][o]) for o in range(3)])
            for k, a in enumerate(scales):
                t["ax1"][k] = expand(a, l0, w)
            left = [d for d in NAT if d != dims[0]]
            axis = left.index(dims[1])
            t["st1"] = pack_stats(m, l).reshape(4, 4, 8, 128)
            stats = t["st1"]
            pieces = [(stats[i] if axis == 0 else stats[:, i]).reshape(32, 128) for i in range(4)]
            t["own1"] = choose(pieces, me[dims[1]])
            t["sc2"] = []
            for o in (1, 2, 3):
                t["ts2"][o - 1] = fold(choose(pieces, (me[dims[1]] + o) % 4))
                t["sc2"].append(cp.remote(t["ts2"].at[o - 1], t["tr2"].at[o - 1], peer(dims[1], o)))

    def choose(pieces, index):
        got = pieces[3]
        for i in (2, 1, 0):
            got = jnp.where(index == i, pieces[i], got)
        return got

    def stats2():
        for t, (l0, w, dims) in zip(T, PARTS):
            for k in t["sc2"]:
                k.wait_recv()
            m, l, scales = merge_stats([t["own1"]] + [unfold(t["tr2"][o]) for o in range(3)])
            for k, a in enumerate(scales):
                t["ax2"][k] = expand(a, l0, w)
            stats = pack_stats(m, l)
            pieces = [stats[8 * i : 8 * i + 8] for i in range(4)]
            t["own2"] = choose(pieces, me[dims[2]])
            t["sc3"] = []
            for o in (1, 2, 3):
                t["ts3"][o - 1] = choose(pieces, (me[dims[2]] + o) % 4)
                t["sc3"].append(cp.remote(t["ts3"].at[o - 1], t["tr3"].at[o - 1], peer(dims[2], o)))

    def stats3():
        for t, (l0, w, dims) in zip(T, PARTS):
            for k in t["sc3"]:
                k.wait_recv()
            m, l, scales = merge_stats([t["own2"]] + [t["tr3"][o] for o in range(3)])
            for k, a in enumerate(scales):
                t["ax3"][k] = expand(a / l, l0, w)

    def offsets(o):
        yy = (y + o) % 4
        return pl.multiple_of(yy * 128, 128), pl.multiple_of((4 + yy) * 128, 128)

    def left_rows(start, rows, a, b):
        at = pl.ds(pl.multiple_of(start, rows), rows)
        return jnp.concatenate([mixed[at, pl.ds(a, 128)], mixed[at, pl.ds(b, 128)]], axis=1)

    def group(o, fresh):
        a, b = offsets(o)

        def step(i, carry):
            rhs = jnp.concatenate([gv[pl.ds(a, 128), :], gv[pl.ds(b, 128), :]], axis=0)
            r = jnp.dot(left_rows(i * 256, 256, a, b), rhs, preferred_element_type=F32)
            at = pl.ds(pl.multiple_of(i * 256, 256), 256)
            V[at, :] = r if fresh else V[at, :] + r
            return carry

        lax.fori_loop(0, 4, step, 0)

    def last_group(o, l0, w):
        a, b = offsets(o)
        cols = slice(l0, l0 + w)

        def step(i, carry):
            rhs = jnp.concatenate([gv[pl.ds(a, 128), cols], gv[pl.ds(b, 128), cols]], axis=0)
            total = None
            for k in range(2):
                r = jnp.dot(left_rows(k * 512 + i * 128, 128, a, b), rhs, preferred_element_type=F32)
                at = pl.ds(pl.multiple_of(k * 512 + i * 128, 128), 128)
                part = (V[at, cols] + r) * wx[k, pl.ds(pl.multiple_of(i * 128, 128), 128), cols]
                total = part if total is None else total + part
            Pacc[i, :, :, :, cols] = total.reshape(4, 4, 8, w)
            return carry

        lax.fori_loop(0, 4, step, 0)

    A.opp_arrived()
    A.opp_to_z()
    A.opp_to_core()
    A.z_arrived(0)
    B = Gather(wo, go, load_wo)
    A.complete(0)
    group(0, True)
    stats1()
    A.z_arrived(3)
    A.z_arrived(1)
    A.complete(3)
    group(3, False)
    B.y_arrived()
    B.y_to_core()
    stats2()
    A.complete(1)
    group(1, False)
    A.z_arrived(2)
    stats3()
    A.complete(2)

    for t, (l0, w, dims) in zip(T, PARTS):
        last_group(2, l0, w)
        axis = NAT.index(dims[0])
        t["c1"] = []
        for o in (2, 1, 3):
            t["s1"][o - 1] = pick(Pacc, axis, (me[dims[0]] + o) % 4, slice(l0, l0 + w), 3).astype(BF16)
            t["c1"].append(cp.remote(t["s1"].at[o - 1], t["r1"].at[o - 1], peer(dims[0], o)))
    B.opp_arrived()
    B.opp_to_core()
    B.y_to_z()
    B.opp_to_z()
    B.z_arrived(0)

    for t, (l0, w, dims) in zip(T, PARTS):
        own = pick(Pacc, NAT.index(dims[0]), me[dims[0]], slice(l0, l0 + w), 3)
        total = t["ax1"][0] * own
        for k in t["c1"]:
            k.wait_recv()
        for o in range(3):
            total = total + t["ax1"][o + 1] * t["r1"][o].astype(F32)
        t["m1"][...] = total.reshape(4, 4, 8, w)
        left = [d for d in NAT if d != dims[0]]
        axis = left.index(dims[1])
        t["c2"] = []
        for o in (2, 1, 3):
            t["s2"][o - 1] = pick(t["m1"], axis, (me[dims[1]] + o) % 4, slice(None), 2).astype(BF16)
            t["c2"].append(cp.remote(t["s2"].at[o - 1], t["r2"].at[o - 1], peer(dims[1], o)))

    for t, (l0, w, dims) in zip(T, PARTS):
        left = [d for d in NAT if d != dims[0]]
        own = pick(t["m1"], left.index(dims[1]), me[dims[1]], slice(None), 2)
        total = t["ax2"][0] * own
        for k in t["c2"]:
            k.wait_recv()
        for o in range(3):
            total = total + t["ax2"][o + 1] * t["r2"][o].astype(F32)
        t["m2"][...] = total.reshape(4, 8, w)
        t["c3"] = []
        for o in (2, 1, 3):
            t["s3"][o - 1] = t["m2"][(me[dims[2]] + o) % 4]
            t["c3"].append(cp.remote(t["s3"].at[o - 1], t["r3"].at[o - 1], peer(dims[2], o)))

    for o in (3, 1, 2):
        B.z_arrived(o)
    context = []
    for t, (l0, w, dims) in sorted(zip(T, PARTS), key=lambda tp: tp[1][0]):
        total = t["ax3"][0] * t["m2"][me[dims[2]]]
        for k in t["c3"]:
            k.wait_recv()
        for o in range(3):
            total = total + t["ax3"][o + 1] * t["r3"][o]
        context.append(total)
    for o in (0, 3, 1, 2):
        B.complete(o)
    context = jnp.concatenate(context, axis=1).astype(BF16)
    out[...] = jnp.dot(context, go[...], preferred_element_type=F32).astype(BF16)
    for k in cp.open:
        k.wait_send()


def shards(tokens, var_embed, query, key_weight, value_weight, out_weight, var_slot):
    vm = pl.BlockSpec(memory_space=pltpu.VMEM)
    hbm = pl.BlockSpec(memory_space=pl.ANY)
    V = pltpu.VMEM
    part = []
    for _, w, _ in PARTS:
        part += [
            V((3, 128, w), BF16), V((3, 128, w), BF16),
            V((3, 32, w), BF16), V((3, 32, w), BF16),
            V((3, 8, w), F32), V((3, 8, w), F32),
            V((4, 4, 8, w), F32), V((4, 8, w), F32),
            V((3, 32, 128), F32), V((3, 32, 128), F32),
            V((3, 8, 128), F32), V((3, 8, 128), F32),
            V((3, 8, 128), F32), V((3, 8, 128), F32),
            V((4, 128, w), F32), V((4, 32, w), F32), V((4, 8, w), F32),
        ]
    result = pl.pallas_call(
        kernel,
        out_shape=jax.ShapeDtypeStruct((8, D), BF16),
        in_specs=[hbm, vm, vm, hbm, hbm, hbm, vm],
        out_specs=vm,
        scratch_shapes=[
            V((64, D), BF16), V((2, 64, 8, D), BF16), V((1024, D), BF16), V((D, D), BF16), V((D, D), BF16),
            V((1024, D), F32), V((4, 4, 4, 8, D), F32), V((2, 512, D), F32), V((4, 4, 4, 8, 128), F32),
            V((32, 64), BF16), V((32, 64), BF16), V((32, 128), BF16), V((8, 32, 128), BF16), V((128, D), BF16),
            V((128, D), BF16), V((8, D), F32), V((8, 128), F32), V((8, 128, 128), F32),
            *part,
            pltpu.SemaphoreType.DMA((SEND_SEMS,)), pltpu.SemaphoreType.DMA((SEND_SEMS,)), pltpu.SemaphoreType.DMA((8,)),
        ],
        compiler_params=pltpu.CompilerParams(
            collective_id=0, has_side_effects=True, vmem_limit_bytes=60 * 1024 * 1024
        ),
    )(
        tokens.reshape(64, 2, 8, D), var_embed, query.reshape(1, D), key_weight, value_weight, out_weight,
        var_slot.reshape(1, -1),
    )
    return result.reshape(1, 8, D)


def solution(mesh):
    placed = (
        P(("vx", "vy"), None, None, None), P(), P(), P("vy", None), P("vy", None), P("vy", None), P(),
    )
    return jax.shard_map(
        shards, mesh=mesh, in_specs=placed, out_specs=P(None, ("vx", "vy"), None), check_vma=False
    )
```

time: 117 us -> 54.2 us (0.46); the launches traced: 115 us -> 54 us
  waiting for transfers between devices: 62.5 us -> 0 us
  Pallas kernels: 0 us -> 51.4 us
  between operations: 13.5 us -> 0.01 us
  matrix products: 11.4 us -> 0 us
  starting transfers between devices: 11.2 us -> 0 us
  local copies, waits for them, and re-layouts: 11 us -> 2.6 us
  other arithmetic: 5.52 us -> 0 us
    pallas_call x0 -> x1, Pallas kernels: none -> 51.4 us  [shards(): pl.pallas_call(kernel, out_shape=jax.ShapeDtypeStruct((8, D), BF16), in_s...]
    all_gather x2 -> x0, waiting for transfers between devices: 32.2 us -> none  [the longest x1 20.2 us: shards(): lax.all_gather(out_weight, 'vy', axis=0, tiled=True)]
    all_to_all x1 -> x0, waiting for transfers between devices: 29.6 us -> none  [joined_exchange(): lax.all_to_all(pieces, axis, split_axis=0, concat_axis=0, tiled=True)]
    all_to_all x1 -> x0, starting transfers between devices: 11.2 us -> none  [joined_exchange(): lax.all_to_all(pieces, axis, split_axis=0, concat_axis=0, tiled=True)]
    dot_general x4 -> x0, matrix products: 9.06 us -> none  [the longest x1 4.51 us: shards(): jnp.einsum('vbpd,cde->cvbpe', selected[0], stacked, preferred_element_typ...]
    another operation x1 -> x0, other arithmetic: 3.51 us -> none  [joined_exchange(): pieces = pieces.reshape(-1, *inside)]
    another operation x2 -> x0, local copies, waits for them, and re-layouts: 2.78 us -> none  [the longest x1 2.66 us: shards(): stacked = jnp.stack((key_full, value_full))]
    slice x2 -> x0, local copies, waits for them, and re-layouts: 2.65 us -> none  [shards(): values = projected[1]]
  transfers between devices with their start and end apart: 3 -> 0, of which waited for: 3 -> 0; matrix products, arithmetic and copies ran while one was open for 19% -> 0% of each run, Pallas kernels for 0% -> 0%
where the time goes in v1:
time: 54.2 us; the launch traced here: 54 us
  Pallas kernels  51.4 us (95%)
  local copies, waits for them, and re-layouts  2.6 us (5%)
    pallas_call x1, Pallas kernels, shards(): pl.pallas_call(kernel, out_shape=jax.ShapeDtypeStruct((8, D), BF16), in_s...  51.4 us
    unnamed x1, local copies, waits for them, and re-layouts  1.32 us
    reshape x1, local copies, waits for them, and re-layouts, shards(): query.reshape(1, D)  1.28 us

profile of v1, /device:TPU:0, one launch (start us, length us, event | category | flops | bytes accessed | tf_op | source)
XLA Modules:
  0.0 54.0 jit_solution(16713264280839294477)
XLA Ops:
  0.0 1.3 %reshape.13.query = bf16[1,1024]{1,0:T(2,128)(2,1)} reshape(bf16[1024]{0:T(1024)(128)(2,1)} %param.9) | data formatting | bytes 4096 | tf_op jit(solution)/shard_map/reshape | solution.py:493
  1.3 51.4 %shard_map.73 = bf16[8,1024]{1,0:T(8,128)(2,1)} custom-call(bf16[64,2,8,1024]{3,2,1,0:T(8,128)(2,1)} %bitcast.3, bf16[91,1024]{1,0:T(8,128)(2,1)} %emb.1, bf16[1,1024]{1,0:T(2,128)(2,1)} %reshape.13.query, bf16[64,1024]{1,0:T(8,128)(2,1)} %wk.1, bf16[64,1024]{1,0:T(8,128)(2,1)} %wv.1, bf16[64,1024]{1,0:T(8,128)(2,1)} %wo.1, s32[1,91]{1,0:T(1,128)} %bitcast.5), custom_call_target="tpu_custom_call" | custom-call | tf_op jit(solution)/shard_map/pallas_call | solution.py:476
  52.7 1.3 %copy.9 = bf16[1,8,1024]{2,1,0:T(8,128)(2,1)} copy(bf16[1,8,1024]{2,1,0:T(8,128)(2,1)} %bitcast.4) | data formatting | bytes 32768

commit v2 on v1

--- a/solution.py
+++ b/solution.py
@@ -1,3 +1,4 @@
+import contextlib
 import functools
 
 import jax
@@ -16,7 +17,10 @@
 NAT = ("x", "z", "y")
 PARTS = ((0, 512, ("x", "y", "z")), (512, 512, ("y", "x", "z")))
 SEND_SEMS = 200
-DIRECT_OPP = False
+
+
+def scope(name):
+    return contextlib.nullcontext()
 
 
 def device_of(x, y, z, c):
@@ -98,8 +102,8 @@
     return got.reshape(-1, got.shape[-1])
 
 
-def kernel(tok, emb, query, wk, wv, wo, vslot, out, wk_v, tokv, mixed, gv, go, V, Pacc, wx, st0, qk_o, qk_p, qkc,
-           qkg, qkt, e2, er, used, sc, *rest):
+def kernel(tok, emb_h, query, wk, wv, wo, vslot, out, emb, wk_v, tokv, mixed, gv, go, V, Pacc, wx, st0, qk_o, qkg, qkt,
+           e2, er, used, sc, *rest):
     ssem, rsem, lsem = rest[-3:]
     per_part = [rest[i * 17 : (i + 1) * 17] for i in range(len(PARTS))]
     names = ("s1", "r1", "s2", "r2", "s3", "r3", "m1", "m2", "ts1", "tr1", "ts2", "tr2", "ts3", "tr3", "ax1", "ax2", "ax3")
@@ -119,19 +123,17 @@
         return device_of(at["x"], at["y"], at["z"], c)
 
     other = device_of(x, y, z, 1 - c)
-    chips = [device_of(x, y, zmate, c)]
+    group_peers = [other, device_of(x, y, zmate, c), device_of(x, y, zmate, 1 - c)]
     for o in (1, 2, 3):
-        chips.append(device_of(x, (y + o) % 4, z, c))
-        chips.append(device_of(x, (y + o) % 4, zmate, c))
-
-    load_wk = cp.here(wk, wk_v)
-    load_tok = cp.here(tok.at[:, c], tokv.at[0])
+        group_peers += [device_of(x, (y + o) % 4, zz, cc) for zz in (z, zmate) for cc in (c, 1 - c)]
 
     barrier = pltpu.get_barrier_semaphore()
-    partners = [other] + [peer(d, o) for d in ("x", "y", "z") for o in (1, 2, 3)]
-    partners += [device_of(x, (y + o) % 4, zmate, c) for o in (1, 2, 3)]
+    partners = group_peers + [peer("x", o) for o in (1, 2, 3)] + [device_of(x, y, (zmate + 2) % 4, c), peer("z", 2)]
     for p in partners:
         pl.semaphore_signal(barrier, inc=1, device_id=p, device_id_type=MESH)
+    load_wk = cp.here(wk, wk_v.at[pl.ds(0, 64), :])
+    load_emb = cp.here(emb_h, emb)
+    load_tok = cp.here(tok.at[:, c], tokv.at[0])
 
     def row_of(yy, zz, cc):
         return pl.multiple_of(((zz * 4 + yy) * 2 + cc) * 64, 64)
@@ -142,14 +144,15 @@
     head_lane = lax.broadcasted_iota(jnp.int32, (HEADS, D), 1) // 64
     head_row = lax.broadcasted_iota(jnp.int32, (HEADS, D), 0)
     own_head = head_lane == head_row
-    q_matrix = jnp.where(own_head, query[...].astype(F32), 0.0).astype(BF16)
-    load_wk.wait()
+    wk_v[64:128, :] = jnp.zeros((64, D), BF16)
+    q8 = query[...].astype(F32)
+    q_row = jnp.concatenate([q8[k : k + 1, :] for k in range(8)], axis=1)
+    q_matrix = jnp.where(own_head, q_row, 0.0).astype(BF16)
+    with scope("w_wk"):
+        load_wk.wait()
     nt = (((1,), (1,)), ((), ()))
     qk = lax.dot_general(q_matrix, wk_v[...], nt, preferred_element_type=F32) * 0.125
-    qk_hi = qk.astype(BF16)
-    qk_lo = (qk - qk_hi.astype(F32)).astype(BF16)
-    qk_both = jnp.concatenate([qk_hi, qk_lo], axis=0)
-    qk_o[...] = qk_both
+    qk_o[...] = qk[:8] + pltpu.roll(qk[8:], 64, axis=1)
 
     ones = own_head.astype(F32).astype(BF16)
     e2[...] = jnp.concatenate([ones, ones, jnp.zeros((96, D), BF16)], axis=0)
@@ -159,78 +162,84 @@
     row8 = lax.broadcasted_iota(jnp.int32, (8, n_vars), 0)
     slot_id = jnp.where(row8 == 0, position, jnp.where(row8 == 1, partner_pos, -1))
     match = (vslot[...] == slot_id).astype(F32)
+    load_emb.wait()
     er[...] = jnp.dot(match.astype(BF16), emb[...], preferred_element_type=F32)
     used[...] = jnp.broadcast_to(jnp.sum(match, axis=1, keepdims=True), (8, 128))
 
-    pl.semaphore_wait(barrier, len(partners))
-
-    qk_copy = cp.remote(qk_o, qk_p, other)
-    tok_copy = cp.remote(tok.at[:, 1 - c], tokv.at[1], other)
+    with scope("w_barrier"):
+        pl.semaphore_wait(barrier, len(partners))
+
+    mine = (zl * 4 + y) * 2 + c
+    qk_copies = [cp.remote(qk_o, qkg.at[mine], p) for p in group_peers]
 
     class Gather:
-        def __init__(self, src, g, local):
-            self.src, self.g = src, g
+        def __init__(self, g, local):
+            self.g = g
             local.wait()
-            own = row_of(y, zl, c)
-            self.from_left = self.put(own, 64, peer("y", 1))
-            self.from_right = self.put(own, 64, peer("y", 3))
-            self.own_z = self.halves(y)
-            self.core = {0: self.put(own, 64, other)}
-            self.core_z, self.z = {}, {}
-
-        def put(self, row, rows, device):
-            ref = self.g.at[pl.ds(row, rows), :]
+            self.y, self.z, self.core = {}, {}, {}
+
+        def put(self, o, half, zz, device):
+            rows = 64 if half is None else 32
+            start = row_of((y + o) % 4, zz, c) + (half or 0) * 32
+            ref = self.g.at[pl.ds(pl.multiple_of(start, 32), rows), :]
             return cp.remote(ref, ref, device)
 
-        def halves(self, yy):
-            row = row_of(yy, zl, c)
-            return (self.put(row, 32, peer("z", 1)), self.put(pl.multiple_of(row + 32, 32), 32, peer("z", 3)))
-
-        def y_arrived(self):
-            self.from_left.wait_recv()
-            left = (y + 3) % 4
-            self.opp_a = self.put(row_of(left, zl, c), 32, peer("y", 1))
-            self.from_right.wait_recv()
-            right = (y + 1) % 4
-            self.opp_b = self.put(pl.multiple_of(row_of(right, zl, c) + 32, 32), 32, peer("y", 3))
-
-        def y_to_z(self):
-            for o in (3, 1):
-                self.z[o] = self.halves((y + o) % 4)
-
-        def y_to_core(self):
-            for o in (3, 1):
-                self.core[o] = self.put(row_of((y + o) % 4, zl, c), 64, other)
-
-        def opp_arrived(self):
-            self.opp_a.wait_recv()
-            self.opp_b.wait_recv()
-
-        def opp_to_z(self):
-            self.z[2] = self.halves((y + 2) % 4)
-
-        def opp_to_core(self):
-            self.core[2] = self.put(row_of((y + 2) % 4, zl, c), 64, other)
-
-        def z_arrived(self, o):
-            pair = self.own_z if o == 0 else self.z[o]
-            pair[0].wait_recv()
-            pair[1].wait_recv()
-            self.core_z[o] = self.put(row_of((y + o) % 4, 1 - zl, c), 64, other)
+        def to_y(self):
+            self.y[3, 0] = self.put(0, 0, zl, peer("y", 1))
+            self.y[1, 1] = self.put(0, 1, zl, peer("y", 3))
+            self.y[3, 1] = self.put(0, 1, zl, peer("y", 1))
+            self.y[1, 0] = self.put(0, 0, zl, peer("y", 3))
+
+        def to_opposite(self, half):
+            self.y[2, half] = self.put(3 if half == 0 else 1, half, zl, peer("y", 1 if half == 0 else 3))
+
+        def to_z(self, o, half):
+            self.z[o, half] = self.put(o, half, zl, peer("z", 1 if half == 0 else 3))
+
+        def to_core(self, o, half, far):
+            self.core.setdefault(o, []).append(self.put(o, half, 1 - zl if far else zl, other))
+
+        def wait_y(self, o, half):
+            self.y[o, half].wait_recv()
+
+        def wait_z(self, o, half):
+            self.z[o, half].wait_recv()
 
         def complete(self, o):
-            self.core[o].wait_recv()
-            self.core_z[o].wait_recv()
-
-    A = Gather(wv, gv, load_wv)
-
-    qk_copy.wait_recv()
-    qk_other = qk_p[...]
-    first = jnp.where(c == 0, qk_both.astype(F32), qk_other.astype(F32))
-    second = jnp.where(c == 0, qk_other.astype(F32), qk_both.astype(F32))
-    qkc[...] = jnp.concatenate([first, second], axis=1).astype(BF16)
-    chip = zl * 4 + y
-    qk_copies = [cp.remote(qkc, qkg.at[chip], p) for p in chips]
+            for k in self.core[o]:
+                k.wait_recv()
+
+        def y_wave(self, first):
+            for o, half in ((3, 0), (1, 1)) if first else ((3, 1), (1, 0)):
+                self.wait_y(o, half)
+                if first:
+                    self.to_opposite(half)
+                self.to_z(o, half)
+                self.to_core(o, half, False)
+
+        def opposite(self):
+            for half in (0, 1):
+                self.wait_y(2, half)
+                self.to_z(2, half)
+            self.to_core(2, None, False)
+
+        def z_both(self, o):
+            self.wait_z(o, 0)
+            self.wait_z(o, 1)
+            self.to_core(o, None, True)
+
+        def z_wave(self, first):
+            for o, half in ((3, 0), (1, 1)) if first else ((3, 1), (1, 0)):
+                self.wait_z(o, half)
+                self.to_core(o, half, True)
+
+    with scope("gatherA"):
+        A = Gather(gv, load_wv)
+        A.to_y()
+        A.to_z(0, 0)
+        A.to_z(0, 1)
+        tok_copy = cp.remote(tok.at[:, 1 - c], tokv.at[1], other)
+        A.to_core(0, None, False)
 
     def mix(k):
         def step(i, carry):
@@ -240,45 +249,68 @@
 
         lax.fori_loop(0, 8, step, 0)
 
-    load_tok.wait()
-    mix(0)
-    tok_copy.wait_recv()
-    mix(1)
-
-    A.y_arrived()
-    A.y_to_z()
-    A.y_to_core()
-    B = Gather(wo, go, load_wo) if False else None
-
-    for k in qk_copies:
-        k.wait_recv()
-    qkg[chip] = qkc[...]
-    qkt[...] = jnp.concatenate(
-        [jnp.concatenate([qkg[i] for i in range(8)], axis=1), jnp.zeros((96, D), BF16)], axis=0
-    )
-
-    def score(i, carry):
-        rows = pl.multiple_of(i * 128, 128)
-        d = lax.dot_general(mixed[pl.ds(rows, 128), :], qkt[...], nt, preferred_element_type=F32)
-        sc[i] = d + pltpu.roll(d, 112, axis=1)
+    def score(k):
+        rows = slice(k * 512, k * 512 + 512)
+        d = lax.dot_general(mixed[rows, :], qkt[...], nt, preferred_element_type=F32)
+        d = d + pltpu.roll(d, 112, axis=1)
+        sc[rows, :] = jnp.where(used[k : k + 1, :] > 0, d, BIG)
+
+    def pair_stats(i, carry):
+        low, high = pl.ds(pl.multiple_of(i * 128, 128), 128), pl.ds(pl.multiple_of(512 + i * 128, 128), 128)
+        s0, s1 = sc[low, :], sc[high, :]
+        m = jnp.maximum(s0, s1)
+        w0 = used[0:1, :] * jnp.exp(s0 - m)
+        w1 = used[1:2, :] * jnp.exp(s1 - m)
+        st0[i] = pack_stats(m, w0 + w1).reshape(4, 4, 8, 128)
+        sc[low, :] = w0
+        sc[high, :] = w1
         return carry
 
-    lax.fori_loop(0, 8, score, 0)
-    use0, use1 = used[0:1, :], used[1:2, :]
-
-    def pair(i, carry):
-        s0 = jnp.where(use0 > 0, sc[i], BIG)
-        s1 = jnp.where(use1 > 0, sc[4 + i], BIG)
-        m = jnp.maximum(s0, s1)
-        w0 = use0 * jnp.exp(s0 - m)
-        w1 = use1 * jnp.exp(s1 - m)
-        st0[i] = pack_stats(m, w0 + w1).reshape(4, 4, 8, 128)
-        rows = pl.ds(pl.multiple_of(i * 128, 128), 128)
-        wx[0, rows, :] = jnp.dot(hilo(w0), e2[...], preferred_element_type=F32)
-        wx[1, rows, :] = jnp.dot(hilo(w1), e2[...], preferred_element_type=F32)
+    def pair_expand(i, carry):
+        for k in range(2):
+            rows = pl.ds(pl.multiple_of(i * 128, 128), 128)
+            w = sc[pl.ds(pl.multiple_of(k * 512 + i * 128, 128), 128), :]
+            wx[k, rows, :] = jnp.dot(hilo(w), e2[...], preferred_element_type=F32)
         return carry
 
-    lax.fori_loop(0, 4, pair, 0)
+    with scope("mix0"):
+        load_tok.wait()
+        mix(0)
+    with scope("A_y1"):
+        A.y_wave(True)
+    with scope("A_z0"):
+        A.z_both(0)
+    with scope("w_tok"):
+        tok_copy.wait_recv()
+    with scope("mix1"):
+        mix(1)
+    with scope("w_qk"):
+        for k in qk_copies:
+            k.wait_recv()
+    with scope("qkt"):
+        qkg[mine] = qk_o[...]
+        left = lax.broadcasted_iota(jnp.int32, (8, 128), 1) < 64
+        columns = []
+        for k in range(8):
+            a, b = qkg[2 * k], qkg[2 * k + 1]
+            top = jnp.where(left, a, pltpu.roll(b, 64, axis=1))
+            bottom = jnp.where(left, pltpu.roll(a, 64, axis=1), b)
+            columns.append(jnp.concatenate([top, bottom], axis=0))
+        q_keys = jnp.concatenate(columns, axis=1)
+        q_high = q_keys.astype(BF16)
+        q_low = (q_keys - q_high.astype(F32)).astype(BF16)
+        qkt[...] = jnp.concatenate([q_high, q_low, jnp.zeros((96, D), BF16)], axis=0)
+    with scope("score0"):
+        score(0)
+    with scope("A_y2"):
+        A.y_wave(False)
+    with scope("gatherB"):
+        B = Gather(go, load_wo)
+        B.to_y()
+    with scope("score1"):
+        score(1)
+    with scope("pair_stats"):
+        lax.fori_loop(0, 4, pair_stats, 0)
 
     for t, (l0, w, dims) in zip(T, PARTS):
         axis = NAT.index(dims[0])
@@ -359,62 +391,88 @@
 
         lax.fori_loop(0, 4, step, 0)
 
-    def last_group(o, l0, w):
+    def last_rows(o, l0, w, i):
         a, b = offsets(o)
         cols = slice(l0, l0 + w)
-
+        rhs = jnp.concatenate([gv[pl.ds(a, 128), cols], gv[pl.ds(b, 128), cols]], axis=0)
+        total = None
+        for k in range(2):
+            r = jnp.dot(left_rows(k * 512 + i * 128, 128, a, b), rhs, preferred_element_type=F32)
+            at = pl.ds(pl.multiple_of(k * 512 + i * 128, 128), 128)
+            part = (V[at, cols] + r) * wx[k, pl.ds(pl.multiple_of(i * 128, 128), 128), cols]
+            total = part if total is None else total + part
+        return total
+
+    def last_group(o, l0, w):
         def step(i, carry):
-            rhs = jnp.concatenate([gv[pl.ds(a, 128), cols], gv[pl.ds(b, 128), cols]], axis=0)
-            total = None
-            for k in range(2):
-                r = jnp.dot(left_rows(k * 512 + i * 128, 128, a, b), rhs, preferred_element_type=F32)
-                at = pl.ds(pl.multiple_of(k * 512 + i * 128, 128), 128)
-                part = (V[at, cols] + r) * wx[k, pl.ds(pl.multiple_of(i * 128, 128), 128), cols]
-                total = part if total is None else total + part
-            Pacc[i, :, :, :, cols] = total.reshape(4, 4, 8, w)
+            Pacc[i, :, :, :, l0 : l0 + w] = last_rows(o, l0, w, i).reshape(4, 4, 8, w)
             return carry
 
         lax.fori_loop(0, 4, step, 0)
 
-    A.opp_arrived()
-    A.opp_to_z()
-    A.opp_to_core()
-    A.z_arrived(0)
-    B = Gather(wo, go, load_wo)
-    A.complete(0)
-    group(0, True)
-    stats1()
-    A.z_arrived(3)
-    A.z_arrived(1)
-    A.complete(3)
-    group(3, False)
-    B.y_arrived()
-    B.y_to_core()
-    stats2()
-    A.complete(1)
-    group(1, False)
-    A.z_arrived(2)
-    stats3()
-    A.complete(2)
-
-    for t, (l0, w, dims) in zip(T, PARTS):
+    with scope("pair_expand"):
+        lax.fori_loop(0, 4, pair_expand, 0)
+    with scope("A_opp"):
+        A.opposite()
+    with scope("A_z1"):
+        A.z_wave(True)
+    with scope("A_c0"):
+        A.complete(0)
+    with scope("g0"):
+        group(0, True)
+    with scope("A_z2"):
+        A.z_wave(False)
+        B.to_z(0, 0)
+        B.to_z(0, 1)
+        B.to_core(0, None, False)
+    with scope("stats1"):
+        stats1()
+    with scope("A_c3"):
+        A.complete(3)
+    with scope("g3"):
+        group(3, False)
+    with scope("A_zo"):
+        A.z_both(2)
+    with scope("B_y"):
+        B.y_wave(True)
+        B.y_wave(False)
+    with scope("A_c1"):
+        A.complete(1)
+    with scope("g1"):
+        group(1, False)
+    with scope("B_o"):
+        B.opposite()
+    with scope("A_c2"):
+        A.complete(2)
+
+    t, (l0, w, dims) = T[1], PARTS[1]
+    with scope("last1"):
         last_group(2, l0, w)
-        axis = NAT.index(dims[0])
         t["c1"] = []
         for o in (2, 1, 3):
-            t["s1"][o - 1] = pick(Pacc, axis, (me[dims[0]] + o) % 4, slice(l0, l0 + w), 3).astype(BF16)
+            t["s1"][o - 1] = pick(Pacc, NAT.index(dims[0]), (me[dims[0]] + o) % 4, slice(l0, l0 + w), 3).astype(BF16)
             t["c1"].append(cp.remote(t["s1"].at[o - 1], t["r1"].at[o - 1], peer(dims[0], o)))
-    B.opp_arrived()
-    B.opp_to_core()
-    B.y_to_z()
-    B.opp_to_z()
-    B.z_arrived(0)
-
-    for t, (l0, w, dims) in zip(T, PARTS):
+    t, (l0, w, dims) = T[0], PARTS[0]
+    with scope("last0"):
+        t["c1"] = []
+        for o in (2, 1, 3):
+            t["s1"][o - 1] = last_rows(2, l0, w, (x + o) % 4).astype(BF16)
+            t["c1"].append(cp.remote(t["s1"].at[o - 1], t["r1"].at[o - 1], peer("x", o)))
+        Pacc[x, :, :, :, l0 : l0 + w] = last_rows(2, l0, w, x).reshape(4, 4, 8, w)
+    with scope("stats2"):
+        stats2()
+    with scope("B_z"):
+        B.z_both(0)
+        B.z_wave(True)
+        B.z_wave(False)
+        B.z_both(2)
+
+    for t, (l0, w, dims) in list(zip(T, PARTS))[::-1]:
         own = pick(Pacc, NAT.index(dims[0]), me[dims[0]], slice(l0, l0 + w), 3)
         total = t["ax1"][0] * own
-        for k in t["c1"]:
-            k.wait_recv()
+        with scope("w_c1"):
+            for k in t["c1"]:
+                k.wait_recv()
         for o in range(3):
             total = total + t["ax1"][o + 1] * t["r1"][o].astype(F32)
         t["m1"][...] = total.reshape(4, 4, 8, w)
@@ -425,12 +483,13 @@
             t["s2"][o - 1] = pick(t["m1"], axis, (me[dims[1]] + o) % 4, slice(None), 2).astype(BF16)
             t["c2"].append(cp.remote(t["s2"].at[o - 1], t["r2"].at[o - 1], peer(dims[1], o)))
 
-    for t, (l0, w, dims) in zip(T, PARTS):
+    for t, (l0, w, dims) in list(zip(T, PARTS))[::-1]:
         left = [d for d in NAT if d != dims[0]]
         own = pick(t["m1"], left.index(dims[1]), me[dims[1]], slice(None), 2)
         total = t["ax2"][0] * own
-        for k in t["c2"]:
-            k.wait_recv()
+        with scope("w_c2"):
+            for k in t["c2"]:
+                k.wait_recv()
         for o in range(3):
             total = total + t["ax2"][o + 1] * t["r2"][o].astype(F32)
         t["m2"][...] = total.reshape(4, 8, w)
@@ -439,22 +498,26 @@
             t["s3"][o - 1] = t["m2"][(me[dims[2]] + o) % 4]
             t["c3"].append(cp.remote(t["s3"].at[o - 1], t["r3"].at[o - 1], peer(dims[2], o)))
 
-    for o in (3, 1, 2):
-        B.z_arrived(o)
+    with scope("stats3"):
+        stats3()
     context = []
     for t, (l0, w, dims) in sorted(zip(T, PARTS), key=lambda tp: tp[1][0]):
         total = t["ax3"][0] * t["m2"][me[dims[2]]]
-        for k in t["c3"]:
-            k.wait_recv()
+        with scope("w_c3"):
+            for k in t["c3"]:
+                k.wait_recv()
         for o in range(3):
             total = total + t["ax3"][o + 1] * t["r3"][o]
         context.append(total)
-    for o in (0, 3, 1, 2):
-        B.complete(o)
-    context = jnp.concatenate(context, axis=1).astype(BF16)
-    out[...] = jnp.dot(context, go[...], preferred_element_type=F32).astype(BF16)
-    for k in cp.open:
-        k.wait_send()
+    with scope("B_c"):
+        for o in (0, 3, 1, 2):
+            B.complete(o)
+    with scope("tail"):
+        context = jnp.concatenate(context, axis=1).astype(BF16)
+        out[...] = jnp.dot(context, go[...], preferred_element_type=F32).astype(BF16)
+    with scope("w_sends"):
+        for k in cp.open:
+            k.wait_send()
 
 
 def shards(tokens, var_embed, query, key_weight, value_weight, out_weight, var_slot):
@@ -476,13 +539,13 @@
     result = pl.pallas_call(
         kernel,
         out_shape=jax.ShapeDtypeStruct((8, D), BF16),
-        in_specs=[hbm, vm, vm, hbm, hbm, hbm, vm],
+        in_specs=[hbm, hbm, vm, hbm, hbm, hbm, vm],
         out_specs=vm,
         scratch_shapes=[
-            V((64, D), BF16), V((2, 64, 8, D), BF16), V((1024, D), BF16), V((D, D), BF16), V((D, D), BF16),
+            V((91, D), BF16), V((128, D), BF16), V((2, 64, 8, D), BF16), V((1024, D), BF16), V((D, D), BF16), V((D, D), BF16),
             V((1024, D), F32), V((4, 4, 4, 8, D), F32), V((2, 512, D), F32), V((4, 4, 4, 8, 128), F32),
-            V((32, 64), BF16), V((32, 64), BF16), V((32, 128), BF16), V((8, 32, 128), BF16), V((128, D), BF16),
-            V((128, D), BF16), V((8, D), F32), V((8, 128), F32), V((8, 128, 128), F32),
+            V((8, 128), F32), V((16, 8, 128), F32), V((128, D), BF16),
+            V((128, D), BF16), V((8, D), F32), V((8, 128), F32), V((1024, 128), F32),
             *part,
             pltpu.SemaphoreType.DMA((SEND_SEMS,)), pltpu.SemaphoreType.DMA((SEND_SEMS,)), pltpu.SemaphoreType.DMA((8,)),
         ],
@@ -490,7 +553,7 @@
             collective_id=0, has_side_effects=True, vmem_limit_bytes=60 * 1024 * 1024
         ),
     )(
-        tokens.reshape(64, 2, 8, D), var_embed, query.reshape(1, D), key_weight, value_weight, out_weight,
+        tokens.reshape(64, 2, 8, D), var_embed, query.reshape(8, 128), key_weight, value_weight, out_weight,
         var_slot.reshape(1, -1),
     )
     return result.reshape(1, 8, D)

time: 54.2 us -> 47.5 us (0.88)
  Pallas kernels: 51.4 us -> 46 us
  local copies, waits for them, and re-layouts: 2.6 us -> 1.32 us
    pallas_call x1, Pallas kernels: 51.4 us -> 46 us  [shards(): pl.pallas_call(kernel, out_shape=jax.ShapeDtypeStruct((8, D), BF16), in_s...]
    reshape x1 -> x0, local copies, waits for them, and re-layouts: 1.28 us -> none  [shards(): query.reshape(1, D)]
where the time goes in v2:
time: 47.5 us; the launch traced here: 47.3 us
  Pallas kernels  46 us (97%)
  local copies, waits for them, and re-layouts  1.32 us (3%)
    pallas_call x1, Pallas kernels, shards(): pl.pallas_call(kernel, out_shape=jax.ShapeDtypeStruct((8, D), BF16), in_s...  46 us
    unnamed x1, local copies, waits for them, and re-layouts  1.32 us

profile of v2, /device:TPU:0, one launch (start us, length us, event | category | flops | bytes accessed | tf_op | source)
XLA Modules:
  0.0 47.3 jit_solution(1286504881788110886)
XLA Ops:
  0.0 46.0 %shard_map.73 = bf16[8,1024]{1,0:T(8,128)(2,1)} custom-call(bf16[64,2,8,1024]{3,2,1,0:T(8,128)(2,1)} %bitcast.4, bf16[91,1024]{1,0:T(8,128)(2,1)} %emb_h.1, bf16[8,128]{1,0:T(8,128)(2,1)} %bitcast.6, bf16[64,1024]{1,0:T(8,128)(2,1)} %wk.1, bf16[64,1024]{1,0:T(8,128)(2,1)} %wv.1, bf16[64,1024]{1,0:T(8,128)(2,1)} %wo.1, s32[1,91]{1,0:T(1,128)} %bitcast.7), custom_call_target="tpu_custom_call" | custom-call | tf_op jit(solution)/shard_map/pallas_call | solution.py:539
  46.0 1.3 %copy.9 = bf16[1,8,1024]{2,1,0:T(8,128)(2,1)} copy(bf16[1,8,1024]{2,1,0:T(8,128)(2,1)} %bitcast.5) | data formatting | bytes 32768

commit v3 on v2

--- a/solution.py
+++ b/solution.py
@@ -15,8 +15,8 @@
 BIG = -1e30
 
 NAT = ("x", "z", "y")
-PARTS = ((0, 512, ("x", "y", "z")), (512, 512, ("y", "x", "z")))
-SEND_SEMS = 200
+PARTS = ((640, 384, ("y", "z", "x")), (0, 384, ("x", "y", "z")), (384, 256, ("z", "x", "y")))
+SEND_SEMS = 160
 
 
 def scope(name):
@@ -57,12 +57,10 @@
     return lax.broadcasted_iota(jnp.int32, (rows, 128), 1)
 
 
-def hilo(a):
-    lane = lanes_iota(a.shape[0])
-    high = a.astype(BF16).astype(F32)
-    low = pltpu.roll(a - high, 16, axis=1)
-    both = jnp.where(lane < 16, high, jnp.where(lane < 32, low, 0.0))
-    return both.astype(BF16)
+def expand(a, l0, w):
+    half = lanes_iota(a.shape[0]) // 64
+    tiles = [jnp.take_along_axis(a, half + 2 * t, axis=1, mode="promise_in_bounds") for t in range(l0 // 128, (l0 + w) // 128)]
+    return jnp.concatenate(tiles, axis=1)
 
 
 def fold(rows):
@@ -102,8 +100,8 @@
     return got.reshape(-1, got.shape[-1])
 
 
-def kernel(tok, emb_h, query, wk, wv, wo, vslot, out, emb, wk_v, tokv, mixed, gv, go, V, Pacc, wx, st0, qk_o, qkg, qkt,
-           e2, er, used, sc, *rest):
+def kernel(tok, emb_h, query, wk, wv, wo, vslot, out, emb, wk_v, tokv, mixed, gv, go, V, Pacc, st0, qk_o, qkg, qkt,
+           er, used, sc, *rest):
     ssem, rsem, lsem = rest[-3:]
     per_part = [rest[i * 17 : (i + 1) * 17] for i in range(len(PARTS))]
     names = ("s1", "r1", "s2", "r2", "s3", "r3", "m1", "m2", "ts1", "tr1", "ts2", "tr2", "ts3", "tr3", "ax1", "ax2", "ax3")
@@ -154,8 +152,6 @@
     qk = lax.dot_general(q_matrix, wk_v[...], nt, preferred_element_type=F32) * 0.125
     qk_o[...] = qk[:8] + pltpu.roll(qk[8:], 64, axis=1)
 
-    ones = own_head.astype(F32).astype(BF16)
-    e2[...] = jnp.concatenate([ones, ones, jnp.zeros((96, D), BF16)], axis=0)
     position = vx * 16 + vy
     partner_pos = position + 1 - 2 * c
     n_vars = vslot.shape[1]
@@ -264,13 +260,6 @@
         st0[i] = pack_stats(m, w0 + w1).reshape(4, 4, 8, 128)
         sc[low, :] = w0
         sc[high, :] = w1
-        return carry
-
-    def pair_expand(i, carry):
-        for k in range(2):
-            rows = pl.ds(pl.multiple_of(i * 128, 128), 128)
-            w = sc[pl.ds(pl.multiple_of(k * 512 + i * 128, 128), 128), :]
-            wx[k, rows, :] = jnp.dot(hilo(w), e2[...], preferred_element_type=F32)
         return carry
 
     with scope("mix0"):
@@ -300,15 +289,16 @@
         q_high = q_keys.astype(BF16)
         q_low = (q_keys - q_high.astype(F32)).astype(BF16)
         qkt[...] = jnp.concatenate([q_high, q_low, jnp.zeros((96, D), BF16)], axis=0)
+    with scope("A_y2"):
+        A.y_wave(False)
+        B = Gather(go, load_wo)
+        B.to_y()
     with scope("score0"):
         score(0)
-    with scope("A_y2"):
-        A.y_wave(False)
-    with scope("gatherB"):
-        B = Gather(go, load_wo)
-        B.to_y()
     with scope("score1"):
         score(1)
+    with scope("A_opp"):
+        A.opposite()
     with scope("pair_stats"):
         lax.fori_loop(0, 4, pair_stats, 0)
 
@@ -319,9 +309,6 @@
             rows = pick(st0, axis, (me[dims[0]] + o) % 4, slice(None), 3)
             t["ts1"][o - 1] = fold(rows)
             t["sc1"].append(cp.remote(t["ts1"].at[o - 1], t["tr1"].at[o - 1], peer(dims[0], o)))
-
-    def expand(a, l0, w):
-        return jnp.dot(hilo(a), e2[:, l0 : l0 + w], preferred_element_type=F32)
 
     def stats1():
         for t, (l0, w, dims) in zip(T, PARTS):
@@ -399,7 +386,7 @@
         for k in range(2):
             r = jnp.dot(left_rows(k * 512 + i * 128, 128, a, b), rhs, preferred_element_type=F32)
             at = pl.ds(pl.multiple_of(k * 512 + i * 128, 128), 128)
-            part = (V[at, cols] + r) * wx[k, pl.ds(pl.multiple_of(i * 128, 128), 128), cols]
+            part = (V[at, cols] + r) * expand(sc[at, :], l0, w)
             total = part if total is None else total + part
         return total
 
@@ -410,64 +397,63 @@
 
         lax.fori_loop(0, 4, step, 0)
 
-    with scope("pair_expand"):
-        lax.fori_loop(0, 4, pair_expand, 0)
-    with scope("A_opp"):
-        A.opposite()
     with scope("A_z1"):
         A.z_wave(True)
-    with scope("A_c0"):
-        A.complete(0)
-    with scope("g0"):
-        group(0, True)
     with scope("A_z2"):
         A.z_wave(False)
         B.to_z(0, 0)
         B.to_z(0, 1)
         B.to_core(0, None, False)
-    with scope("stats1"):
-        stats1()
+    with scope("A_c0"):
+        A.complete(0)
+    with scope("g0"):
+        group(0, True)
+    with scope("B_y"):
+        B.y_wave(True)
+        B.y_wave(False)
     with scope("A_c3"):
         A.complete(3)
     with scope("g3"):
         group(3, False)
     with scope("A_zo"):
         A.z_both(2)
-    with scope("B_y"):
-        B.y_wave(True)
-        B.y_wave(False)
     with scope("A_c1"):
         A.complete(1)
     with scope("g1"):
         group(1, False)
+    with scope("A_c2"):
+        A.complete(2)
+
+    def send1(t, l0, w, dims, o):
+        index = (me[dims[0]] + o) % 4
+        t["s1"][o - 1] = pick(Pacc, NAT.index(dims[0]), index, slice(l0, l0 + w), 3).astype(BF16)
+        t["c1"].append(cp.remote(t["s1"].at[o - 1], t["r1"].at[o - 1], peer(dims[0], o)))
+
+    for t in T:
+        t["c1"] = []
+    with scope("last1"):
+        last_group(2, 512, 512)
+        for o in (2, 1, 3):
+            send1(T[0], *PARTS[0], o)
     with scope("B_o"):
         B.opposite()
-    with scope("A_c2"):
-        A.complete(2)
-
-    t, (l0, w, dims) = T[1], PARTS[1]
-    with scope("last1"):
-        last_group(2, l0, w)
-        t["c1"] = []
+    with scope("last0"):
         for o in (2, 1, 3):
-            t["s1"][o - 1] = pick(Pacc, NAT.index(dims[0]), (me[dims[0]] + o) % 4, slice(l0, l0 + w), 3).astype(BF16)
-            t["c1"].append(cp.remote(t["s1"].at[o - 1], t["r1"].at[o - 1], peer(dims[0], o)))
-    t, (l0, w, dims) = T[0], PARTS[0]
-    with scope("last0"):
-        t["c1"] = []
+            index = (x + o) % 4
+            Pacc[index, :, :, :, 0:512] = last_rows(2, 0, 512, index).reshape(4, 4, 8, 512)
+            send1(T[1], *PARTS[1], o)
+        Pacc[x, :, :, :, 0:512] = last_rows(2, 0, 512, x).reshape(4, 4, 8, 512)
         for o in (2, 1, 3):
-            t["s1"][o - 1] = last_rows(2, l0, w, (x + o) % 4).astype(BF16)
-            t["c1"].append(cp.remote(t["s1"].at[o - 1], t["r1"].at[o - 1], peer("x", o)))
-        Pacc[x, :, :, :, l0 : l0 + w] = last_rows(2, l0, w, x).reshape(4, 4, 8, w)
-    with scope("stats2"):
-        stats2()
+            send1(T[2], *PARTS[2], o)
+    with scope("stats1"):
+        stats1()
     with scope("B_z"):
         B.z_both(0)
         B.z_wave(True)
         B.z_wave(False)
         B.z_both(2)
 
-    for t, (l0, w, dims) in list(zip(T, PARTS))[::-1]:
+    for t, (l0, w, dims) in zip(T, PARTS):
         own = pick(Pacc, NAT.index(dims[0]), me[dims[0]], slice(l0, l0 + w), 3)
         total = t["ax1"][0] * own
         with scope("w_c1"):
@@ -483,7 +469,10 @@
             t["s2"][o - 1] = pick(t["m1"], axis, (me[dims[1]] + o) % 4, slice(None), 2).astype(BF16)
             t["c2"].append(cp.remote(t["s2"].at[o - 1], t["r2"].at[o - 1], peer(dims[1], o)))
 
-    for t, (l0, w, dims) in list(zip(T, PARTS))[::-1]:
+    with scope("stats2"):
+        stats2()
+
+    for t, (l0, w, dims) in zip(T, PARTS):
         left = [d for d in NAT if d != dims[0]]
         own = pick(t["m1"], left.index(dims[1]), me[dims[1]], slice(None), 2)
         total = t["ax2"][0] * own
@@ -543,9 +532,8 @@
         out_specs=vm,
         scratch_shapes=[
             V((91, D), BF16), V((128, D), BF16), V((2, 64, 8, D), BF16), V((1024, D), BF16), V((D, D), BF16), V((D, D), BF16),
-            V((1024, D), F32), V((4, 4, 4, 8, D), F32), V((2, 512, D), F32), V((4, 4, 4, 8, 128), F32),
-            V((8, 128), F32), V((16, 8, 128), F32), V((128, D), BF16),
-            V((128, D), BF16), V((8, D), F32), V((8, 128), F32), V((1024, 128), F32),
+            V((1024, D), F32), V((4, 4, 4, 8, D), F32), V((4, 4, 4, 8, 128), F32),
+            V((8, 128), F32), V((16, 8, 128), F32), V((128, D), BF16), V((8, D), F32), V((8, 128), F32), V((1024, 128), F32),
             *part,
             pltpu.SemaphoreType.DMA((SEND_SEMS,)), pltpu.SemaphoreType.DMA((SEND_SEMS,)), pltpu.SemaphoreType.DMA((8,)),
         ],

time: 47.5 us -> 44.3 us (0.933)
  Pallas kernels: 46 us -> 42.8 us
    pallas_call x1, Pallas kernels: 46 us -> 42.8 us  [shards(): pl.pallas_call(kernel, out_shape=jax.ShapeDtypeStruct((8, D), BF16), in_s...]
where the time goes in v3:
time: 44.3 us; the launch traced here: 44.1 us
  Pallas kernels  42.8 us (97%)
  local copies, waits for them, and re-layouts  1.32 us (3%)
    pallas_call x1, Pallas kernels, shards(): pl.pallas_call(kernel, out_shape=jax.ShapeDtypeStruct((8, D), BF16), in_s...  42.8 us
    unnamed x1, local copies, waits for them, and re-layouts  1.32 us

profile of v3, /device:TPU:0, one launch (start us, length us, event | category | flops | bytes accessed | tf_op | source)
XLA Modules:
  0.0 44.1 jit_solution(12060793316539415841)
XLA Ops:
  0.0 42.8 %shard_map.73 = bf16[8,1024]{1,0:T(8,128)(2,1)} custom-call(bf16[64,2,8,1024]{3,2,1,0:T(8,128)(2,1)} %bitcast.4, bf16[91,1024]{1,0:T(8,128)(2,1)} %emb_h.1, bf16[8,128]{1,0:T(8,128)(2,1)} %bitcast.6, bf16[64,1024]{1,0:T(8,128)(2,1)} %wk.1, bf16[64,1024]{1,0:T(8,128)(2,1)} %wv.1, bf16[64,1024]{1,0:T(8,128)(2,1)} %wo.1, s32[1,91]{1,0:T(1,128)} %bitcast.7), custom_call_target="tpu_custom_call" | custom-call | tf_op jit(solution)/shard_map/pallas_call | solution.py:528
  42.8 1.3 %copy.9 = bf16[1,8,1024]{2,1,0:T(8,128)(2,1)} copy(bf16[1,8,1024]{2,1,0:T(8,128)(2,1)} %bitcast.5) | data formatting | bytes 32768

commit v4 on v3

--- a/solution.py
+++ b/solution.py
@@ -15,8 +15,9 @@
 BIG = -1e30
 
 NAT = ("x", "z", "y")
-PARTS = ((640, 384, ("y", "z", "x")), (0, 384, ("x", "y", "z")), (384, 256, ("z", "x", "y")))
-SEND_SEMS = 160
+PARTS = ((0, 512, ("x", "y", "z")), (512, 256, ("y", "z", "x")), (768, 256, ("z", "x", "y")))
+BLOCK = 256
+SEND_SEMS = 200
 
 
 def scope(name):
@@ -136,8 +137,9 @@
     def row_of(yy, zz, cc):
         return pl.multiple_of(((zz * 4 + yy) * 2 + cc) * 64, 64)
 
-    load_wv = cp.here(wv, gv.at[pl.ds(row_of(y, zl, c), 64), :])
-    load_wo = cp.here(wo, go.at[pl.ds(row_of(y, zl, c), 64), :])
+    own_rows = pl.ds(row_of(y, zl, c), 64)
+    load_wv = [cp.here(wv.at[:, BLOCK * b : BLOCK * b + BLOCK], gv.at[b, own_rows, :]) for b in range(4)]
+    load_wo = cp.here(wo, go.at[own_rows, :])
 
     head_lane = lax.broadcasted_iota(jnp.int32, (HEADS, D), 1) // 64
     head_row = lax.broadcasted_iota(jnp.int32, (HEADS, D), 0)
@@ -181,61 +183,43 @@
             return cp.remote(ref, ref, device)
 
         def to_y(self):
-            self.y[3, 0] = self.put(0, 0, zl, peer("y", 1))
-            self.y[1, 1] = self.put(0, 1, zl, peer("y", 3))
-            self.y[3, 1] = self.put(0, 1, zl, peer("y", 1))
-            self.y[1, 0] = self.put(0, 0, zl, peer("y", 3))
-
-        def to_opposite(self, half):
-            self.y[2, half] = self.put(3 if half == 0 else 1, half, zl, peer("y", 1 if half == 0 else 3))
-
-        def to_z(self, o, half):
-            self.z[o, half] = self.put(o, half, zl, peer("z", 1 if half == 0 else 3))
-
-        def to_core(self, o, half, far):
-            self.core.setdefault(o, []).append(self.put(o, half, 1 - zl if far else zl, other))
-
-        def wait_y(self, o, half):
-            self.y[o, half].wait_recv()
-
-        def wait_z(self, o, half):
-            self.z[o, half].wait_recv()
-
-        def complete(self, o):
-            for k in self.core[o]:
-                k.wait_recv()
-
-        def y_wave(self, first):
-            for o, half in ((3, 0), (1, 1)) if first else ((3, 1), (1, 0)):
-                self.wait_y(o, half)
-                if first:
-                    self.to_opposite(half)
-                self.to_z(o, half)
-                self.to_core(o, half, False)
-
-        def opposite(self):
-            for half in (0, 1):
-                self.wait_y(2, half)
-                self.to_z(2, half)
-            self.to_core(2, None, False)
-
-        def z_both(self, o):
-            self.wait_z(o, 0)
-            self.wait_z(o, 1)
-            self.to_core(o, None, True)
-
-        def z_wave(self, first):
-            for o, half in ((3, 0), (1, 1)) if first else ((3, 1), (1, 0)):
-                self.wait_z(o, half)
-                self.to_core(o, half, True)
+            for o in (1, 3, 2):
+                self.y[4 - o] = self.put(0, None, zl, peer("y", o))
+
+        def to_z(self, o):
+            self.z[o] = [self.put(o, half, zl, peer("z", 1 + 2 * half)) for half in (0, 1)]
+
+        def to_core(self, o, far):
+            self.core.setdefault(o, []).append(self.put(o, None, 1 - zl if far else zl, other))
+
+        def start(self):
+            self.to_y()
+            self.to_z(0)
+            self.to_core(0, False)
+
+        def from_y(self, *order):
+            for o in order:
+                self.y[o].wait_recv()
+                self.to_z(o)
+                self.to_core(o, False)
+
+        def from_z(self, *order):
+            for o in order:
+                for k in self.z[o]:
+                    k.wait_recv()
+                self.to_core(o, True)
+
+        def complete(self, *order):
+            for o in order:
+                for k in self.core[o]:
+                    k.wait_recv()
 
     with scope("gatherA"):
-        A = Gather(gv, load_wv)
-        A.to_y()
-        A.to_z(0, 0)
-        A.to_z(0, 1)
+        A = [Gather(gv.at[b], load_wv[b]) for b in range(4)]
+        A[0].start()
         tok_copy = cp.remote(tok.at[:, 1 - c], tokv.at[1], other)
-        A.to_core(0, None, False)
+        for b in range(1, 4):
+            A[b].start()
 
     def mix(k):
         def step(i, carry):
@@ -265,14 +249,20 @@
     with scope("mix0"):
         load_tok.wait()
         mix(0)
-    with scope("A_y1"):
-        A.y_wave(True)
-    with scope("A_z0"):
-        A.z_both(0)
+    with scope("y0"):
+        A[0].from_y(3, 1)
+    with scope("z00"):
+        A[0].from_z(0)
     with scope("w_tok"):
         tok_copy.wait_recv()
     with scope("mix1"):
         mix(1)
+    with scope("o0"):
+        A[0].from_y(2)
+    with scope("z01"):
+        A[1].from_z(0)
+    with scope("y1"):
+        A[1].from_y(3, 1)
     with scope("w_qk"):
         for k in qk_copies:
             k.wait_recv()
@@ -289,18 +279,31 @@
         q_high = q_keys.astype(BF16)
         q_low = (q_keys - q_high.astype(F32)).astype(BF16)
         qkt[...] = jnp.concatenate([q_high, q_low, jnp.zeros((96, D), BF16)], axis=0)
-    with scope("A_y2"):
-        A.y_wave(False)
+    with scope("score0"):
+        score(0)
+    with scope("o1"):
+        A[1].from_y(2)
+    with scope("y2"):
+        A[2].from_z(0)
+        A[2].from_y(3, 1)
+    with scope("zy0"):
+        A[0].from_z(3, 1)
+    with scope("score1"):
+        score(1)
+    with scope("o2"):
+        A[2].from_y(2)
+    with scope("y3"):
+        A[3].from_z(0)
+        A[3].from_y(3, 1)
+    with scope("pair_stats"):
+        lax.fori_loop(0, 4, pair_stats, 0)
+    with scope("zo0"):
+        A[0].from_z(2)
+    with scope("o3"):
+        A[3].from_y(2)
+    with scope("gatherB"):
         B = Gather(go, load_wo)
         B.to_y()
-    with scope("score0"):
-        score(0)
-    with scope("score1"):
-        score(1)
-    with scope("A_opp"):
-        A.opposite()
-    with scope("pair_stats"):
-        lax.fori_loop(0, 4, pair_stats, 0)
 
     for t, (l0, w, dims) in zip(T, PARTS):
         axis = NAT.index(dims[0])
@@ -362,113 +365,125 @@
         yy = (y + o) % 4
         return pl.multiple_of(yy * 128, 128), pl.multiple_of((4 + yy) * 128, 128)
 
-    def left_rows(start, rows, a, b):
+    def left_cols(start, rows, groups):
         at = pl.ds(pl.multiple_of(start, rows), rows)
-        return jnp.concatenate([mixed[at, pl.ds(a, 128)], mixed[at, pl.ds(b, 128)]], axis=1)
-
-    def group(o, fresh):
-        a, b = offsets(o)
+        return jnp.concatenate([mixed[at, pl.ds(a, 128)] for o in groups for a in offsets(o)], axis=1)
+
+    def right_rows(b, groups):
+        return jnp.concatenate([gv[b, pl.ds(a, 128), :] for o in groups for a in offsets(o)], axis=0)
+
+    def early(b, groups):
+        cols = slice(BLOCK * b, BLOCK * b + BLOCK)
 
         def step(i, carry):
-            rhs = jnp.concatenate([gv[pl.ds(a, 128), :], gv[pl.ds(b, 128), :]], axis=0)
-            r = jnp.dot(left_rows(i * 256, 256, a, b), rhs, preferred_element_type=F32)
             at = pl.ds(pl.multiple_of(i * 256, 256), 256)
-            V[at, :] = r if fresh else V[at, :] + r
+            V[at, cols] = jnp.dot(left_cols(i * 256, 256, groups), right_rows(b, groups), preferred_element_type=F32)
             return carry
 
         lax.fori_loop(0, 4, step, 0)
 
-    def last_rows(o, l0, w, i):
-        a, b = offsets(o)
-        cols = slice(l0, l0 + w)
-        rhs = jnp.concatenate([gv[pl.ds(a, 128), cols], gv[pl.ds(b, 128), cols]], axis=0)
+    def late_rows(b, groups, i):
+        cols = slice(BLOCK * b, BLOCK * b + BLOCK)
         total = None
         for k in range(2):
-            r = jnp.dot(left_rows(k * 512 + i * 128, 128, a, b), rhs, preferred_element_type=F32)
-            at = pl.ds(pl.multiple_of(k * 512 + i * 128, 128), 128)
-            part = (V[at, cols] + r) * expand(sc[at, :], l0, w)
+            start = k * 512 + i * 128
+            at = pl.ds(pl.multiple_of(start, 128), 128)
+            r = jnp.dot(left_cols(start, 128, groups), right_rows(b, groups), preferred_element_type=F32)
+            if len(groups) < 4:
+                r = r + V[at, cols]
+            part = r * expand(sc[at, :], BLOCK * b, BLOCK)
             total = part if total is None else total + part
-        return total
-
-    def last_group(o, l0, w):
+        Pacc[i, :, :, :, cols] = total.reshape(4, 4, 8, BLOCK)
+
+    def late(b, groups):
         def step(i, carry):
-            Pacc[i, :, :, :, l0 : l0 + w] = last_rows(o, l0, w, i).reshape(4, 4, 8, w)
+            late_rows(b, groups, i)
             return carry
 
         lax.fori_loop(0, 4, step, 0)
 
-    with scope("A_z1"):
-        A.z_wave(True)
-    with scope("A_z2"):
-        A.z_wave(False)
-        B.to_z(0, 0)
-        B.to_z(0, 1)
-        B.to_core(0, None, False)
-    with scope("A_c0"):
-        A.complete(0)
-    with scope("g0"):
-        group(0, True)
-    with scope("B_y"):
-        B.y_wave(True)
-        B.y_wave(False)
-    with scope("A_c3"):
-        A.complete(3)
-    with scope("g3"):
-        group(3, False)
-    with scope("A_zo"):
-        A.z_both(2)
-    with scope("A_c1"):
-        A.complete(1)
-    with scope("g1"):
-        group(1, False)
-    with scope("A_c2"):
-        A.complete(2)
-
-    def send1(t, l0, w, dims, o):
+    ALL = (0, 3, 1, 2)
+
+    def send1(b, o):
+        p = 0 if b < 2 else b - 1
+        t, (l0, w, dims) = T[p], PARTS[p]
         index = (me[dims[0]] + o) % 4
-        t["s1"][o - 1] = pick(Pacc, NAT.index(dims[0]), index, slice(l0, l0 + w), 3).astype(BF16)
-        t["c1"].append(cp.remote(t["s1"].at[o - 1], t["r1"].at[o - 1], peer(dims[0], o)))
+        s = b % 2 * 3 + o - 1 if p == 0 else o - 1
+        t["s1"][s] = pick(Pacc, NAT.index(dims[0]), index, slice(BLOCK * b, BLOCK * b + BLOCK), 3).astype(BF16)
+        t["c1"].append(cp.remote(t["s1"].at[s], t["r1"].at[s], peer(dims[0], o)))
 
     for t in T:
         t["c1"] = []
-    with scope("last1"):
-        last_group(2, 512, 512)
+    with scope("zy1"):
+        A[1].from_z(3, 1)
+    with scope("c00"):
+        A[0].complete(0, 3, 1)
+    with scope("early0"):
+        early(0, ALL[:3])
+    with scope("zo1"):
+        A[1].from_z(2)
+    with scope("zy2"):
+        A[2].from_z(3, 1)
+    with scope("c0"):
+        A[0].complete(2)
+    with scope("late0"):
         for o in (2, 1, 3):
-            send1(T[0], *PARTS[0], o)
+            late_rows(0, ALL[3:], (x + o) % 4)
+            send1(0, o)
+        late_rows(0, ALL[3:], x)
+    with scope("B_z0"):
+        B.to_z(0)
+        B.to_core(0, False)
+        B.from_y(3, 1)
+    with scope("zo2"):
+        A[2].from_z(2)
+    with scope("c1"):
+        A[1].complete(0, 3, 1, 2)
+    with scope("late1"):
+        for o in (2, 1, 3):
+            late_rows(1, ALL, (x + o) % 4)
+            send1(1, o)
+        late_rows(1, ALL, x)
+    with scope("zy3"):
+        A[3].from_z(3, 1)
+    with scope("zo3"):
+        A[3].from_z(2)
+    with scope("c2"):
+        A[2].complete(0, 3, 1, 2)
+    with scope("late2"):
+        late(2, ALL)
+        for o in (2, 1, 3):
+            send1(2, o)
+    with scope("c3"):
+        A[3].complete(0, 3, 1, 2)
+    with scope("late3"):
+        late(3, ALL)
+        for o in (2, 1, 3):
+            send1(3, o)
     with scope("B_o"):
-        B.opposite()
-    with scope("last0"):
-        for o in (2, 1, 3):
-            index = (x + o) % 4
-            Pacc[index, :, :, :, 0:512] = last_rows(2, 0, 512, index).reshape(4, 4, 8, 512)
-            send1(T[1], *PARTS[1], o)
-        Pacc[x, :, :, :, 0:512] = last_rows(2, 0, 512, x).reshape(4, 4, 8, 512)
-        for o in (2, 1, 3):
-            send1(T[2], *PARTS[2], o)
+        B.from_y(2)
     with scope("stats1"):
         stats1()
     with scope("B_z"):
-        B.z_both(0)
-        B.z_wave(True)
-        B.z_wave(False)
-        B.z_both(2)
+        B.from_z(0, 3, 1, 2)
 
     for t, (l0, w, dims) in zip(T, PARTS):
-        own = pick(Pacc, NAT.index(dims[0]), me[dims[0]], slice(l0, l0 + w), 3)
-        total = t["ax1"][0] * own
-        with scope("w_c1"):
-            for k in t["c1"]:
-                k.wait_recv()
-        for o in range(3):
-            total = total + t["ax1"][o + 1] * t["r1"][o].astype(F32)
-        t["m1"][...] = total.reshape(4, 4, 8, w)
+        for s in range(w // BLOCK):
+            with scope("w_c1"):
+                for k in t["c1"][3 * s : 3 * s + 3]:
+                    k.wait_recv()
+            cols = slice(BLOCK * s, BLOCK * s + BLOCK)
+            own = pick(Pacc, NAT.index(dims[0]), me[dims[0]], slice(l0 + BLOCK * s, l0 + BLOCK * s + BLOCK), 3)
+            total = t["ax1"][0, :, cols] * own
+            for o in range(3):
+                total = total + t["ax1"][o + 1, :, cols] * t["r1"][3 * s + o].astype(F32)
+            t["m1"][:, :, :, cols] = total.reshape(4, 4, 8, BLOCK)
         left = [d for d in NAT if d != dims[0]]
         axis = left.index(dims[1])
         t["c2"] = []
         for o in (2, 1, 3):
             t["s2"][o - 1] = pick(t["m1"], axis, (me[dims[1]] + o) % 4, slice(None), 2).astype(BF16)
             t["c2"].append(cp.remote(t["s2"].at[o - 1], t["r2"].at[o - 1], peer(dims[1], o)))
-
     with scope("stats2"):
         stats2()
 
@@ -516,7 +531,7 @@
     part = []
     for _, w, _ in PARTS:
         part += [
-            V((3, 128, w), BF16), V((3, 128, w), BF16),
+            V((w // BLOCK * 3, 128, BLOCK), BF16), V((w // BLOCK * 3, 128, BLOCK), BF16),
             V((3, 32, w), BF16), V((3, 32, w), BF16),
             V((3, 8, w), F32), V((3, 8, w), F32),
             V((4, 4, 8, w), F32), V((4, 8, w), F32),
@@ -531,11 +546,12 @@
         in_specs=[hbm, hbm, vm, hbm, hbm, hbm, vm],
         out_specs=vm,
         scratch_shapes=[
-            V((91, D), BF16), V((128, D), BF16), V((2, 64, 8, D), BF16), V((1024, D), BF16), V((D, D), BF16), V((D, D), BF16),
+            V((91, D), BF16), V((128, D), BF16), V((2, 64, 8, D), BF16), V((1024, D), BF16),
+            V((4, D, BLOCK), BF16), V((D, D), BF16),
             V((1024, D), F32), V((4, 4, 4, 8, D), F32), V((4, 4, 4, 8, 128), F32),
             V((8, 128), F32), V((16, 8, 128), F32), V((128, D), BF16), V((8, D), F32), V((8, 128), F32), V((1024, 128), F32),
             *part,
-            pltpu.SemaphoreType.DMA((SEND_SEMS,)), pltpu.SemaphoreType.DMA((SEND_SEMS,)), pltpu.SemaphoreType.DMA((8,)),
+            pltpu.SemaphoreType.DMA((SEND_SEMS,)), pltpu.SemaphoreType.DMA((SEND_SEMS,)), pltpu.SemaphoreType.DMA((10,)),
         ],
         compiler_params=pltpu.CompilerParams(
             collective_id=0, has_side_effects=True, vmem_limit_bytes=60 * 1024 * 1024

time: 44.3 us -> 48.6 us (1.097)
  Pallas kernels: 42.8 us -> 47.1 us
    pallas_call x1, Pallas kernels: 42.8 us -> 47.1 us  [shards(): pl.pallas_call(kernel, out_shape=jax.ShapeDtypeStruct((8, D), BF16), in_s...]
where the time goes in v4:
time: 48.6 us; the launch traced here: 48.4 us
  Pallas kernels  47.1 us (97%)
  local copies, waits for them, and re-layouts  1.32 us (3%)
    pallas_call x1, Pallas kernels, shards(): pl.pallas_call(kernel, out_shape=jax.ShapeDtypeStruct((8, D), BF16), in_s...  47.1 us
    unnamed x1, local copies, waits for them, and re-layouts  1.32 us

profile of v4, /device:TPU:0, one launch (start us, length us, event | category | flops | bytes accessed | tf_op | source)
XLA Modules:
  0.0 48.4 jit_solution(10435777403986286862)
XLA Ops:
  0.0 47.1 %shard_map.73 = bf16[8,1024]{1,0:T(8,128)(2,1)} custom-call(bf16[64,2,8,1024]{3,2,1,0:T(8,128)(2,1)} %bitcast.4, bf16[91,1024]{1,0:T(8,128)(2,1)} %emb_h.1, bf16[8,128]{1,0:T(8,128)(2,1)} %bitcast.6, bf16[64,1024]{1,0:T(8,128)(2,1)} %wk.1, bf16[64,1024]{1,0:T(8,128)(2,1)} %wv.1, bf16[64,1024]{1,0:T(8,128)(2,1)} %wo.1, s32[1,91]{1,0:T(1,128)} %bitcast.7), custom_call_target="tpu_custom_call" | custom-call | tf_op jit(solution)/shard_map/pallas_call | solution.py:543
  47.1 1.3 %copy.9 = bf16[1,8,1024]{2,1,0:T(8,128)(2,1)} copy(bf16[1,8,1024]{2,1,0:T(8,128)(2,1)} %bitcast.5) | data formatting | bytes 32768

commit v5 on v4

--- a/solution.py
+++ b/solution.py
@@ -101,7 +101,7 @@
     return got.reshape(-1, got.shape[-1])
 
 
-def kernel(tok, emb_h, query, wk, wv, wo, vslot, out, emb, wk_v, tokv, mixed, gv, go, V, Pacc, st0, qk_o, qkg, qkt,
+def kernel(tok, emb_h, query_h, wk, wv, wo, vslot_h, out, emb, query, vslot, wk_v, tokv, mixed, gv, go, V, Pacc, st0, qk_o, qkg, qkt,
            er, used, sc, *rest):
     ssem, rsem, lsem = rest[-3:]
     per_part = [rest[i * 17 : (i + 1) * 17] for i in range(len(PARTS))]
@@ -131,6 +131,8 @@
     for p in partners:
         pl.semaphore_signal(barrier, inc=1, device_id=p, device_id_type=MESH)
     load_wk = cp.here(wk, wk_v.at[pl.ds(0, 64), :])
+    load_query = cp.here(query_h, query)
+    load_slot = cp.here(vslot_h, vslot)
     load_emb = cp.here(emb_h, emb)
     load_tok = cp.here(tok.at[:, c], tokv.at[0])
 
@@ -145,6 +147,7 @@
     head_row = lax.broadcasted_iota(jnp.int32, (HEADS, D), 0)
     own_head = head_lane == head_row
     wk_v[64:128, :] = jnp.zeros((64, D), BF16)
+    load_query.wait()
     q8 = query[...].astype(F32)
     q_row = jnp.concatenate([q8[k : k + 1, :] for k in range(8)], axis=1)
     q_matrix = jnp.where(own_head, q_row, 0.0).astype(BF16)
@@ -156,6 +159,7 @@
 
     position = vx * 16 + vy
     partner_pos = position + 1 - 2 * c
+    load_slot.wait()
     n_vars = vslot.shape[1]
     row8 = lax.broadcasted_iota(jnp.int32, (8, n_vars), 0)
     slot_id = jnp.where(row8 == 0, position, jnp.where(row8 == 1, partner_pos, -1))
@@ -220,6 +224,8 @@
         tok_copy = cp.remote(tok.at[:, 1 - c], tokv.at[1], other)
         for b in range(1, 4):
             A[b].start()
+        B = Gather(go, load_wo)
+        B.start()
 
     def mix(k):
         def step(i, carry):
@@ -301,17 +307,17 @@
         A[0].from_z(2)
     with scope("o3"):
         A[3].from_y(2)
-    with scope("gatherB"):
-        B = Gather(go, load_wo)
-        B.to_y()
-
-    for t, (l0, w, dims) in zip(T, PARTS):
-        axis = NAT.index(dims[0])
-        t["sc1"] = []
-        for o in (1, 2, 3):
-            rows = pick(st0, axis, (me[dims[0]] + o) % 4, slice(None), 3)
-            t["ts1"][o - 1] = fold(rows)
-            t["sc1"].append(cp.remote(t["ts1"].at[o - 1], t["tr1"].at[o - 1], peer(dims[0], o)))
+
+    def stats0():
+        for t, (l0, w, dims) in zip(T, PARTS):
+            axis = NAT.index(dims[0])
+            t["sc1"] = []
+            for o in (1, 2, 3):
+                rows = pick(st0, axis, (me[dims[0]] + o) % 4, slice(None), 3)
+                t["ts1"][o - 1] = fold(rows)
+        for t, (l0, w, dims) in zip(T, PARTS):
+            for o in (1, 2, 3):
+                t["sc1"].append(cp.remote(t["ts1"].at[o - 1], t["tr1"].at[o - 1], peer(dims[0], o)))
 
     def stats1():
         for t, (l0, w, dims) in zip(T, PARTS):
@@ -382,18 +388,23 @@
 
         lax.fori_loop(0, 4, step, 0)
 
+    def weighted(b, groups, starts, rows):
+        cols = slice(BLOCK * b, BLOCK * b + BLOCK)
+        spans = [pl.ds(pl.multiple_of(k * 512 + start, rows), rows) for k in range(2) for start in starts]
+        lhs = jnp.concatenate(
+            [jnp.concatenate([mixed[at, pl.ds(a, 128)] for o in groups for a in offsets(o)], axis=1) for at in spans], axis=0
+        )
+        r = jnp.dot(lhs, right_rows(b, groups), preferred_element_type=F32)
+        if len(groups) < 4:
+            r = r + jnp.concatenate([V[at, cols] for at in spans], axis=0)
+        r = r * expand(jnp.concatenate([sc[at, :] for at in spans], axis=0), BLOCK * b, BLOCK)
+        return r[:128] + r[128:]
+
     def late_rows(b, groups, i):
-        cols = slice(BLOCK * b, BLOCK * b + BLOCK)
-        total = None
-        for k in range(2):
-            start = k * 512 + i * 128
-            at = pl.ds(pl.multiple_of(start, 128), 128)
-            r = jnp.dot(left_cols(start, 128, groups), right_rows(b, groups), preferred_element_type=F32)
-            if len(groups) < 4:
-                r = r + V[at, cols]
-            part = r * expand(sc[at, :], BLOCK * b, BLOCK)
-            total = part if total is None else total + part
-        Pacc[i, :, :, :, cols] = total.reshape(4, 4, 8, BLOCK)
+        Pacc[i, :, :, :, BLOCK * b : BLOCK * b + BLOCK] = weighted(b, groups, [i * 128], 128).reshape(4, 4, 8, BLOCK)
+
+    def late_by_z(b, groups, i):
+        return weighted(b, groups, [k * 128 + i * 32 for k in range(4)], 32)
 
     def late(b, groups):
         def step(i, carry):
@@ -431,10 +442,10 @@
             late_rows(0, ALL[3:], (x + o) % 4)
             send1(0, o)
         late_rows(0, ALL[3:], x)
+    with scope("stats0"):
+        stats0()
     with scope("B_z0"):
-        B.to_z(0)
-        B.to_core(0, False)
-        B.from_y(3, 1)
+        B.from_z(0)
     with scope("zo2"):
         A[2].from_z(2)
     with scope("c1"):
@@ -454,20 +465,24 @@
         late(2, ALL)
         for o in (2, 1, 3):
             send1(2, o)
+    with scope("B_y"):
+        B.from_y(3, 1, 2)
     with scope("c3"):
         A[3].complete(0, 3, 1, 2)
     with scope("late3"):
-        late(3, ALL)
         for o in (2, 1, 3):
-            send1(3, o)
-    with scope("B_o"):
-        B.from_y(2)
+            T[2]["s1"][o - 1] = late_by_z(3, ALL, (z + o) % 4).astype(BF16)
+            T[2]["c1"].append(cp.remote(T[2]["s1"].at[o - 1], T[2]["r1"].at[o - 1], peer("z", o)))
+        own_z = late_by_z(3, ALL, z).reshape(4, 4, 8, BLOCK)
+        for i in range(4):
+            Pacc[i, z, :, :, 768:1024] = own_z[i]
     with scope("stats1"):
         stats1()
-    with scope("B_z"):
-        B.from_z(0, 3, 1, 2)
 
     for t, (l0, w, dims) in zip(T, PARTS):
+        if t is T[2]:
+            with scope("stats2"):
+                stats2()
         for s in range(w // BLOCK):
             with scope("w_c1"):
                 for k in t["c1"][3 * s : 3 * s + 3]:
@@ -484,8 +499,8 @@
         for o in (2, 1, 3):
             t["s2"][o - 1] = pick(t["m1"], axis, (me[dims[1]] + o) % 4, slice(None), 2).astype(BF16)
             t["c2"].append(cp.remote(t["s2"].at[o - 1], t["r2"].at[o - 1], peer(dims[1], o)))
-    with scope("stats2"):
-        stats2()
+    with scope("B_z"):
+        B.from_z(3, 1, 2)
 
     for t, (l0, w, dims) in zip(T, PARTS):
         left = [d for d in NAT if d != dims[0]]
@@ -499,9 +514,13 @@
         t["m2"][...] = total.reshape(4, 8, w)
         t["c3"] = []
         for o in (2, 1, 3):
-            t["s3"][o - 1] = t["m2"][(me[dims[2]] + o) % 4]
+            t["s3"][o - 1] = t["m2"][(me[dims[2]] + o) % 4].astype(BF16)
             t["c3"].append(cp.remote(t["s3"].at[o - 1], t["r3"].at[o - 1], peer(dims[2], o)))
 
+    with scope("w_sends0"):
+        early_sends, cp.open = cp.open[:-40], cp.open[-40:]
+        for k in early_sends:
+            k.wait_send()
     with scope("stats3"):
         stats3()
     context = []
@@ -511,7 +530,7 @@
             for k in t["c3"]:
                 k.wait_recv()
         for o in range(3):
-            total = total + t["ax3"][o + 1] * t["r3"][o]
+            total = total + t["ax3"][o + 1] * t["r3"][o].astype(F32)
         context.append(total)
     with scope("B_c"):
         for o in (0, 3, 1, 2):
@@ -533,7 +552,7 @@
         part += [
             V((w // BLOCK * 3, 128, BLOCK), BF16), V((w // BLOCK * 3, 128, BLOCK), BF16),
             V((3, 32, w), BF16), V((3, 32, w), BF16),
-            V((3, 8, w), F32), V((3, 8, w), F32),
+            V((3, 8, w), BF16), V((3, 8, w), BF16),
             V((4, 4, 8, w), F32), V((4, 8, w), F32),
             V((3, 32, 128), F32), V((3, 32, 128), F32),
             V((3, 8, 128), F32), V((3, 8, 128), F32),
@@ -543,15 +562,15 @@
     result = pl.pallas_call(
         kernel,
         out_shape=jax.ShapeDtypeStruct((8, D), BF16),
-        in_specs=[hbm, hbm, vm, hbm, hbm, hbm, vm],
+        in_specs=[hbm] * 7,
         out_specs=vm,
         scratch_shapes=[
-            V((91, D), BF16), V((128, D), BF16), V((2, 64, 8, D), BF16), V((1024, D), BF16),
+            V((91, D), BF16), V((8, 128), BF16), V((1, 91), jnp.int32), V((128, D), BF16), V((2, 64, 8, D), BF16), V((1024, D), BF16),
             V((4, D, BLOCK), BF16), V((D, D), BF16),
             V((1024, D), F32), V((4, 4, 4, 8, D), F32), V((4, 4, 4, 8, 128), F32),
             V((8, 128), F32), V((16, 8, 128), F32), V((128, D), BF16), V((8, D), F32), V((8, 128), F32), V((1024, 128), F32),
             *part,
-            pltpu.SemaphoreType.DMA((SEND_SEMS,)), pltpu.SemaphoreType.DMA((SEND_SEMS,)), pltpu.SemaphoreType.DMA((10,)),
+            pltpu.SemaphoreType.DMA((SEND_SEMS,)), pltpu.SemaphoreType.DMA((SEND_SEMS,)), pltpu.SemaphoreType.DMA((12,)),
         ],
         compiler_params=pltpu.CompilerParams(
             collective_id=0, has_side_effects=True, vmem_limit_bytes=60 * 1024 * 1024

time: 48.6 us -> 46.8 us (0.963)
  Pallas kernels: 47.1 us -> 45.3 us
    pallas_call x1, Pallas kernels: 47.1 us -> 45.3 us  [shards(): pl.pallas_call(kernel, out_shape=jax.ShapeDtypeStruct((8, D), BF16), in_s...]
where the time goes in v5:
time: 46.8 us; the launch traced here: 46.6 us
  Pallas kernels  45.3 us (97%)
  local copies, waits for them, and re-layouts  1.32 us (3%)
    pallas_call x1, Pallas kernels, shards(): pl.pallas_call(kernel, out_shape=jax.ShapeDtypeStruct((8, D), BF16), in_s...  45.3 us
    unnamed x1, local copies, waits for them, and re-layouts  1.32 us

profile of v5, /device:TPU:0, one launch (start us, length us, event | category | flops | bytes accessed | tf_op | source)
XLA Modules:
  0.0 46.6 jit_solution(11161051584750709682)
XLA Ops:
  0.0 45.3 %shard_map.73 = bf16[8,1024]{1,0:T(8,128)(2,1)} custom-call(bf16[64,2,8,1024]{3,2,1,0:T(8,128)(2,1)} %bitcast.4, bf16[91,1024]{1,0:T(8,128)(2,1)} %emb_h.1, bf16[8,128]{1,0:T(8,128)(2,1)} %bitcast.6, bf16[64,1024]{1,0:T(8,128)(2,1)} %wk.1, bf16[64,1024]{1,0:T(8,128)(2,1)} %wv.1, bf16[64,1024]{1,0:T(8,128)(2,1)} %wo.1, s32[1,91]{1,0:T(1,128)} %bitcast.7), custom_call_target="tpu_custom_call" | custom-call | tf_op jit(solution)/shard_map/pallas_call | solution.py:562
  45.3 1.3 %copy.9 = bf16[1,8,1024]{2,1,0:T(8,128)(2,1)} copy(bf16[1,8,1024]{2,1,0:T(8,128)(2,1)} %bitcast.5) | data formatting | bytes 32768

commit v6 on v5

--- a/solution.py
+++ b/solution.py
@@ -15,7 +15,8 @@
 BIG = -1e30
 
 NAT = ("x", "z", "y")
-PARTS = ((0, 512, ("x", "y", "z")), (512, 256, ("y", "z", "x")), (768, 256, ("z", "x", "y")))
+PARTS = ((0, 512, ("x", "y", "z")), (512, 512, ("y", "x", "z")))
+SEQUENCE = (0, 2, 1, 3)
 BLOCK = 256
 SEND_SEMS = 200
 
@@ -101,12 +102,11 @@
     return got.reshape(-1, got.shape[-1])
 
 
-def kernel(tok, emb_h, query_h, wk, wv, wo, vslot_h, out, emb, query, vslot, wk_v, tokv, mixed, gv, go, V, Pacc, st0, qk_o, qkg, qkt,
-           er, used, sc, *rest):
+def kernel(tok, emb_h, query_h, wk, wv, wo, vslot_h, out, emb, query, vslot, wk_v, tokv, mixed, mixed_y,
+           gv, go, V, own1, st0, qk_o, qkg, qkt, er, used, sc, s1, r1, s2, r2, s3, r3, m1, m2, *rest):
     ssem, rsem, lsem = rest[-3:]
-    per_part = [rest[i * 17 : (i + 1) * 17] for i in range(len(PARTS))]
-    names = ("s1", "r1", "s2", "r2", "s3", "r3", "m1", "m2", "ts1", "tr1", "ts2", "tr2", "ts3", "tr3", "ax1", "ax2", "ax3")
-    T = [dict(zip(names, p)) for p in per_part]
+    names = ("ts1", "tr1", "ts2", "tr2", "ts3", "tr3", "ax1", "ax2", "ax3")
+    T = [dict(zip(names, rest[i * 9 : (i + 1) * 9])) for i in range(len(PARTS))]
     cp = Copies(ssem, rsem, lsem)
 
     vx, vy = lax.axis_index("vx"), lax.axis_index("vy")
@@ -134,13 +134,13 @@
     load_query = cp.here(query_h, query)
     load_slot = cp.here(vslot_h, vslot)
     load_emb = cp.here(emb_h, emb)
-    load_tok = cp.here(tok.at[:, c], tokv.at[0])
+    load_tok = cp.here(tok.at[:, :, :, c], tokv.at[0])
 
     def row_of(yy, zz, cc):
         return pl.multiple_of(((zz * 4 + yy) * 2 + cc) * 64, 64)
 
     own_rows = pl.ds(row_of(y, zl, c), 64)
-    load_wv = [cp.here(wv.at[:, BLOCK * b : BLOCK * b + BLOCK], gv.at[b, own_rows, :]) for b in range(4)]
+    load_wv = [cp.here(wv.at[:, BLOCK * b : BLOCK * b + BLOCK], gv.at[j, own_rows, :]) for j, b in enumerate(SEQUENCE)]
     load_wo = cp.here(wo, go.at[own_rows, :])
 
     head_lane = lax.broadcasted_iota(jnp.int32, (HEADS, D), 1) // 64
@@ -221,7 +221,7 @@
     with scope("gatherA"):
         A = [Gather(gv.at[b], load_wv[b]) for b in range(4)]
         A[0].start()
-        tok_copy = cp.remote(tok.at[:, 1 - c], tokv.at[1], other)
+        tok_copy = cp.remote(tok.at[:, :, :, 1 - c], tokv.at[1], other)
         for b in range(1, 4):
             A[b].start()
         B = Gather(go, load_wo)
@@ -229,27 +229,29 @@
 
     def mix(k):
         def step(i, carry):
-            t = tokv[k, pl.ds(i * 8, 8)].astype(F32).reshape(64, D)
-            mixed[pl.ds(pl.multiple_of(k * 512 + i * 64, 64), 64), :] = (t + er[k : k + 1, :]).astype(BF16)
+            at = pl.ds(pl.multiple_of(k * 512 + i * 64, 64), 64)
+            half = pl.ds(2 * (i % 2), 2)
+            t = tokv[k, i // 2, half].astype(F32).reshape(64, D)
+            mixed[at, :] = (t + er[k : k + 1, :]).astype(BF16)
+            t = tokv[k, half, :, i // 2].astype(F32).reshape(64, D)
+            mixed_y[at, :] = (t + er[k : k + 1, :]).astype(BF16)
             return carry
 
         lax.fori_loop(0, 8, step, 0)
 
     def score(k):
-        rows = slice(k * 512, k * 512 + 512)
-        d = lax.dot_general(mixed[rows, :], qkt[...], nt, preferred_element_type=F32)
+        d = lax.dot_general(mixed[k * 512 : k * 512 + 512, :], qkt[...], nt, preferred_element_type=F32)
         d = d + pltpu.roll(d, 112, axis=1)
-        sc[rows, :] = jnp.where(used[k : k + 1, :] > 0, d, BIG)
+        sc[k] = jnp.where(used[k : k + 1, :] > 0, d, BIG).reshape(4, 4, 4, 8, 128)
 
     def pair_stats(i, carry):
-        low, high = pl.ds(pl.multiple_of(i * 128, 128), 128), pl.ds(pl.multiple_of(512 + i * 128, 128), 128)
-        s0, s1 = sc[low, :], sc[high, :]
-        m = jnp.maximum(s0, s1)
+        s0, s1_ = sc[0, i].reshape(128, 128), sc[1, i].reshape(128, 128)
+        m = jnp.maximum(s0, s1_)
         w0 = used[0:1, :] * jnp.exp(s0 - m)
-        w1 = used[1:2, :] * jnp.exp(s1 - m)
+        w1 = used[1:2, :] * jnp.exp(s1_ - m)
         st0[i] = pack_stats(m, w0 + w1).reshape(4, 4, 8, 128)
-        sc[low, :] = w0
-        sc[high, :] = w1
+        sc[0, i] = w0.reshape(4, 4, 8, 128)
+        sc[1, i] = w1.reshape(4, 4, 8, 128)
         return carry
 
     with scope("mix0"):
@@ -371,60 +373,42 @@
         yy = (y + o) % 4
         return pl.multiple_of(yy * 128, 128), pl.multiple_of((4 + yy) * 128, 128)
 
-    def left_cols(start, rows, groups):
+    def product(j, groups, source, start, rows):
         at = pl.ds(pl.multiple_of(start, rows), rows)
-        return jnp.concatenate([mixed[at, pl.ds(a, 128)] for o in groups for a in offsets(o)], axis=1)
-
-    def right_rows(b, groups):
-        return jnp.concatenate([gv[b, pl.ds(a, 128), :] for o in groups for a in offsets(o)], axis=0)
-
-    def early(b, groups):
-        cols = slice(BLOCK * b, BLOCK * b + BLOCK)
-
+        lhs = jnp.concatenate([source[at, pl.ds(a, 128)] for o in groups for a in offsets(o)], axis=1)
+        rhs = jnp.concatenate([gv[j, pl.ds(a, 128), :] for o in groups for a in offsets(o)], axis=0)
+        return jnp.dot(lhs, rhs, preferred_element_type=F32)
+
+    def early(j, groups):
         def step(i, carry):
-            at = pl.ds(pl.multiple_of(i * 256, 256), 256)
-            V[at, cols] = jnp.dot(left_cols(i * 256, 256, groups), right_rows(b, groups), preferred_element_type=F32)
+            V[pl.ds(pl.multiple_of(i * 256, 256), 256), :] = product(j, groups, mixed, i * 256, 256)
             return carry
 
         lax.fori_loop(0, 4, step, 0)
 
-    def weighted(b, groups, starts, rows):
-        cols = slice(BLOCK * b, BLOCK * b + BLOCK)
-        spans = [pl.ds(pl.multiple_of(k * 512 + start, rows), rows) for k in range(2) for start in starts]
-        lhs = jnp.concatenate(
-            [jnp.concatenate([mixed[at, pl.ds(a, 128)] for o in groups for a in offsets(o)], axis=1) for at in spans], axis=0
-        )
-        r = jnp.dot(lhs, right_rows(b, groups), preferred_element_type=F32)
-        if len(groups) < 4:
-            r = r + jnp.concatenate([V[at, cols] for at in spans], axis=0)
-        r = r * expand(jnp.concatenate([sc[at, :] for at in spans], axis=0), BLOCK * b, BLOCK)
-        return r[:128] + r[128:]
-
-    def late_rows(b, groups, i):
-        Pacc[i, :, :, :, BLOCK * b : BLOCK * b + BLOCK] = weighted(b, groups, [i * 128], 128).reshape(4, 4, 8, BLOCK)
-
-    def late_by_z(b, groups, i):
-        return weighted(b, groups, [k * 128 + i * 32 for k in range(4)], 32)
-
-    def late(b, groups):
-        def step(i, carry):
-            late_rows(b, groups, i)
-            return carry
-
-        lax.fori_loop(0, 4, step, 0)
+    def weighted(j, groups, dim, index):
+        total = None
+        for k in range(2):
+            start = k * 512 + index * 128
+            r = product(j, groups, mixed if dim == "x" else mixed_y, start, 128)
+            if len(groups) < 4:
+                r = r + V[pl.ds(pl.multiple_of(start, 128), 128), :]
+            w = (sc[k, index] if dim == "x" else sc[k, :, :, index]).reshape(128, 128)
+            r = r * expand(w, BLOCK * SEQUENCE[j], BLOCK)
+            total = r if total is None else total + r
+        return total
+
+    c1 = [[] for _ in range(4)]
+
+    def reduce1(j, groups):
+        dim = PARTS[SEQUENCE[j] // 2][2][0]
+        for o in (2, 1, 3):
+            s1[j, o - 1] = weighted(j, groups, dim, (me[dim] + o) % 4).astype(BF16)
+            c1[j].append(cp.remote(s1.at[j, o - 1], r1.at[j, o - 1], peer(dim, o)))
+        own1[j] = weighted(j, groups, dim, me[dim])
 
     ALL = (0, 3, 1, 2)
 
-    def send1(b, o):
-        p = 0 if b < 2 else b - 1
-        t, (l0, w, dims) = T[p], PARTS[p]
-        index = (me[dims[0]] + o) % 4
-        s = b % 2 * 3 + o - 1 if p == 0 else o - 1
-        t["s1"][s] = pick(Pacc, NAT.index(dims[0]), index, slice(BLOCK * b, BLOCK * b + BLOCK), 3).astype(BF16)
-        t["c1"].append(cp.remote(t["s1"].at[s], t["r1"].at[s], peer(dims[0], o)))
-
-    for t in T:
-        t["c1"] = []
     with scope("zy1"):
         A[1].from_z(3, 1)
     with scope("c00"):
@@ -438,10 +422,7 @@
     with scope("c0"):
         A[0].complete(2)
     with scope("late0"):
-        for o in (2, 1, 3):
-            late_rows(0, ALL[3:], (x + o) % 4)
-            send1(0, o)
-        late_rows(0, ALL[3:], x)
+        reduce1(0, ALL[3:])
     with scope("stats0"):
         stats0()
     with scope("B_z0"):
@@ -451,10 +432,7 @@
     with scope("c1"):
         A[1].complete(0, 3, 1, 2)
     with scope("late1"):
-        for o in (2, 1, 3):
-            late_rows(1, ALL, (x + o) % 4)
-            send1(1, o)
-        late_rows(1, ALL, x)
+        reduce1(1, ALL)
     with scope("zy3"):
         A[3].from_z(3, 1)
     with scope("zo3"):
@@ -462,81 +440,85 @@
     with scope("c2"):
         A[2].complete(0, 3, 1, 2)
     with scope("late2"):
-        late(2, ALL)
-        for o in (2, 1, 3):
-            send1(2, o)
+        reduce1(2, ALL)
     with scope("B_y"):
         B.from_y(3, 1, 2)
     with scope("c3"):
         A[3].complete(0, 3, 1, 2)
     with scope("late3"):
-        for o in (2, 1, 3):
-            T[2]["s1"][o - 1] = late_by_z(3, ALL, (z + o) % 4).astype(BF16)
-            T[2]["c1"].append(cp.remote(T[2]["s1"].at[o - 1], T[2]["r1"].at[o - 1], peer("z", o)))
-        own_z = late_by_z(3, ALL, z).reshape(4, 4, 8, BLOCK)
-        for i in range(4):
-            Pacc[i, z, :, :, 768:1024] = own_z[i]
+        reduce1(3, ALL)
     with scope("stats1"):
         stats1()
 
-    for t, (l0, w, dims) in zip(T, PARTS):
-        if t is T[2]:
-            with scope("stats2"):
-                stats2()
-        for s in range(w // BLOCK):
-            with scope("w_c1"):
-                for k in t["c1"][3 * s : 3 * s + 3]:
-                    k.wait_recv()
-            cols = slice(BLOCK * s, BLOCK * s + BLOCK)
-            own = pick(Pacc, NAT.index(dims[0]), me[dims[0]], slice(l0 + BLOCK * s, l0 + BLOCK * s + BLOCK), 3)
-            total = t["ax1"][0, :, cols] * own
-            for o in range(3):
-                total = total + t["ax1"][o + 1, :, cols] * t["r1"][3 * s + o].astype(F32)
-            t["m1"][:, :, :, cols] = total.reshape(4, 4, 8, BLOCK)
-        left = [d for d in NAT if d != dims[0]]
-        axis = left.index(dims[1])
-        t["c2"] = []
+    c2, c3 = [[] for _ in range(4)], [[] for _ in range(4)]
+
+    def part_of(j):
+        b = SEQUENCE[j]
+        t, (l0, _, dims) = T[b // 2], PARTS[b // 2]
+        return t, dims, slice(BLOCK * b - l0, BLOCK * b - l0 + BLOCK)
+
+    def reduce2(j):
+        t, dims, cols = part_of(j)
+        axis = [d for d in NAT if d != dims[0]].index(dims[1])
+        with scope("w_c1"):
+            for k in c1[j]:
+                k.wait_recv()
+        total = t["ax1"][0, :, cols] * own1[j]
+        for o in range(3):
+            total = total + t["ax1"][o + 1, :, cols] * r1[j, o].astype(F32)
+        m1[j] = total.reshape(4, 4, 8, BLOCK)
         for o in (2, 1, 3):
-            t["s2"][o - 1] = pick(t["m1"], axis, (me[dims[1]] + o) % 4, slice(None), 2).astype(BF16)
-            t["c2"].append(cp.remote(t["s2"].at[o - 1], t["r2"].at[o - 1], peer(dims[1], o)))
+            s2[j, o - 1] = pick(m1.at[j], axis, (me[dims[1]] + o) % 4, slice(None), 2).astype(BF16)
+        for o in (2, 1, 3):
+            c2[j].append(cp.remote(s2.at[j, o - 1], r2.at[j, o - 1], peer(dims[1], o)))
+
+    def reduce3(j):
+        t, dims, cols = part_of(j)
+        axis = [d for d in NAT if d != dims[0]].index(dims[1])
+        with scope("w_c2"):
+            for k in c2[j]:
+                k.wait_recv()
+        total = t["ax2"][0, :, cols] * pick(m1.at[j], axis, me[dims[1]], slice(None), 2)
+        for o in range(3):
+            total = total + t["ax2"][o + 1, :, cols] * r2[j, o].astype(F32)
+        m2[j] = total.reshape(4, 8, BLOCK)
+        for o in (2, 1, 3):
+            s3[j, o - 1] = m2[j, (me[dims[2]] + o) % 4].astype(BF16)
+        for o in (2, 1, 3):
+            c3[j].append(cp.remote(s3.at[j, o - 1], r3.at[j, o - 1], peer(dims[2], o)))
+
+    def result(j):
+        t, dims, cols = part_of(j)
+        with scope("w_c3"):
+            for k in c3[j]:
+                k.wait_recv()
+        total = t["ax3"][0, :, cols] * m2[j, me[dims[2]]]
+        for o in range(3):
+            total = total + t["ax3"][o + 1, :, cols] * r3[j, o].astype(F32)
+        return total
+
+    for j in (0, 1, 2):
+        reduce2(j)
+    with scope("stats2"):
+        stats2()
+    reduce2(3)
     with scope("B_z"):
         B.from_z(3, 1, 2)
-
-    for t, (l0, w, dims) in zip(T, PARTS):
-        left = [d for d in NAT if d != dims[0]]
-        own = pick(t["m1"], left.index(dims[1]), me[dims[1]], slice(None), 2)
-        total = t["ax2"][0] * own
-        with scope("w_c2"):
-            for k in t["c2"]:
-                k.wait_recv()
-        for o in range(3):
-            total = total + t["ax2"][o + 1] * t["r2"][o].astype(F32)
-        t["m2"][...] = total.reshape(4, 8, w)
-        t["c3"] = []
-        for o in (2, 1, 3):
-            t["s3"][o - 1] = t["m2"][(me[dims[2]] + o) % 4].astype(BF16)
-            t["c3"].append(cp.remote(t["s3"].at[o - 1], t["r3"].at[o - 1], peer(dims[2], o)))
-
+    for j in (0, 1, 2):
+        reduce3(j)
+    with scope("stats3"):
+        stats3()
+    reduce3(3)
+    context = [result(j) for j in (0, 1, 2)]
+    with scope("B_c"):
+        B.complete(0, 3, 1, 2)
     with scope("w_sends0"):
-        early_sends, cp.open = cp.open[:-40], cp.open[-40:]
+        early_sends, cp.open = cp.open[:-6], cp.open[-6:]
         for k in early_sends:
             k.wait_send()
-    with scope("stats3"):
-        stats3()
-    context = []
-    for t, (l0, w, dims) in sorted(zip(T, PARTS), key=lambda tp: tp[1][0]):
-        total = t["ax3"][0] * t["m2"][me[dims[2]]]
-        with scope("w_c3"):
-            for k in t["c3"]:
-                k.wait_recv()
-        for o in range(3):
-            total = total + t["ax3"][o + 1] * t["r3"][o].astype(F32)
-        context.append(total)
-    with scope("B_c"):
-        for o in (0, 3, 1, 2):
-            B.complete(o)
+    context.append(result(3))
     with scope("tail"):
-        context = jnp.concatenate(context, axis=1).astype(BF16)
+        context = jnp.concatenate([context[SEQUENCE.index(b)] for b in range(4)], axis=1).astype(BF16)
         out[...] = jnp.dot(context, go[...], preferred_element_type=F32).astype(BF16)
     with scope("w_sends"):
         for k in cp.open:
@@ -550,10 +532,6 @@
     part = []
     for _, w, _ in PARTS:
         part += [
-            V((w // BLOCK * 3, 128, BLOCK), BF16), V((w // BLOCK * 3, 128, BLOCK), BF16),
-            V((3, 32, w), BF16), V((3, 32, w), BF16),
-            V((3, 8, w), BF16), V((3, 8, w), BF16),
-            V((4, 4, 8, w), F32), V((4, 8, w), F32),
             V((3, 32, 128), F32), V((3, 32, 128), F32),
             V((3, 8, 128), F32), V((3, 8, 128), F32),
             V((3, 8, 128), F32), V((3, 8, 128), F32),
@@ -565,10 +543,15 @@
         in_specs=[hbm] * 7,
         out_specs=vm,
         scratch_shapes=[
-            V((91, D), BF16), V((8, 128), BF16), V((1, 91), jnp.int32), V((128, D), BF16), V((2, 64, 8, D), BF16), V((1024, D), BF16),
-            V((4, D, BLOCK), BF16), V((D, D), BF16),
-            V((1024, D), F32), V((4, 4, 4, 8, D), F32), V((4, 4, 4, 8, 128), F32),
-            V((8, 128), F32), V((16, 8, 128), F32), V((128, D), BF16), V((8, D), F32), V((8, 128), F32), V((1024, 128), F32),
+            V((91, D), BF16), V((8, 128), BF16), V((1, 91), jnp.int32), V((128, D), BF16), V((2, 4, 4, 4, 8, D), BF16),
+            V((1024, D), BF16), V((1024, D), BF16), V((4, D, BLOCK), BF16), V((D, D), BF16),
+            V((1024, BLOCK), F32), V((4, 128, BLOCK), F32), V((4, 4, 4, 8, 128), F32),
+            V((8, 128), F32), V((16, 8, 128), F32), V((128, D), BF16), V((8, D), F32), V((8, 128), F32),
+            V((2, 4, 4, 4, 8, 128), F32),
+            V((4, 3, 128, BLOCK), BF16), V((4, 3, 128, BLOCK), BF16),
+            V((4, 3, 32, BLOCK), BF16), V((4, 3, 32, BLOCK), BF16),
+            V((4, 3, 8, BLOCK), BF16), V((4, 3, 8, BLOCK), BF16),
+            V((4, 4, 4, 8, BLOCK), F32), V((4, 4, 8, BLOCK), F32),
             *part,
             pltpu.SemaphoreType.DMA((SEND_SEMS,)), pltpu.SemaphoreType.DMA((SEND_SEMS,)), pltpu.SemaphoreType.DMA((12,)),
         ],
@@ -576,7 +559,7 @@
             collective_id=0, has_side_effects=True, vmem_limit_bytes=60 * 1024 * 1024
         ),
     )(
-        tokens.reshape(64, 2, 8, D), var_embed, query.reshape(8, 128), key_weight, value_weight, out_weight,
+        tokens.reshape(4, 4, 4, 2, 8, D), var_embed, query.reshape(8, 128), key_weight, value_weight, out_weight,
         var_slot.reshape(1, -1),
     )
     return result.reshape(1, 8, D)

time: 46.8 us -> 43.4 us (0.927)
  Pallas kernels: 45.3 us -> 41.9 us
    pallas_call x1, Pallas kernels: 45.3 us -> 41.9 us  [shards(): pl.pallas_call(kernel, out_shape=jax.ShapeDtypeStruct((8, D), BF16), in_s...]
where the time goes in v6:
time: 43.4 us; the launch traced here: 43.2 us
  Pallas kernels  41.9 us (97%)
  local copies, waits for them, and re-layouts  1.32 us (3%)
    pallas_call x1, Pallas kernels, shards(): pl.pallas_call(kernel, out_shape=jax.ShapeDtypeStruct((8, D), BF16), in_s...  41.9 us
    unnamed x1, local copies, waits for them, and re-layouts  1.32 us

profile of v6, /device:TPU:0, one launch (start us, length us, event | category | flops | bytes accessed | tf_op | source)
XLA Modules:
  0.0 43.2 jit_solution(12157357569748514050)
XLA Ops:
  0.0 41.9 %shard_map.73 = bf16[8,1024]{1,0:T(8,128)(2,1)} custom-call(bf16[4,4,4,2,8,1024]{5,4,3,2,1,0:T(8,128)(2,1)} %bitcast.4, bf16[91,1024]{1,0:T(8,128)(2,1)} %emb_h.1, bf16[8,128]{1,0:T(8,128)(2,1)} %bitcast.6, bf16[64,1024]{1,0:T(8,128)(2,1)} %wk.1, bf16[64,1024]{1,0:T(8,128)(2,1)} %wv.1, bf16[64,1024]{1,0:T(8,128)(2,1)} %wo.1, s32[1,91]{1,0:T(1,128)} %bitcast.7), custom_call_target="tpu_custom_call" | custom-call | tf_op jit(solution)/shard_map/pallas_call | solution.py:540
  41.9 1.3 %copy.9 = bf16[1,8,1024]{2,1,0:T(8,128)(2,1)} copy(bf16[1,8,1024]{2,1,0:T(8,128)(2,1)} %bitcast.5) | data formatting | bytes 32768

commit v7 on v6

--- a/solution.py
+++ b/solution.py
@@ -18,7 +18,7 @@
 PARTS = ((0, 512, ("x", "y", "z")), (512, 512, ("y", "x", "z")))
 SEQUENCE = (0, 2, 1, 3)
 BLOCK = 256
-SEND_SEMS = 200
+SEND_SEMS = 264
 
 
 def scope(name):
@@ -103,10 +103,10 @@
 
 
 def kernel(tok, emb_h, query_h, wk, wv, wo, vslot_h, out, emb, query, vslot, wk_v, tokv, mixed, mixed_y,
-           gv, go, V, own1, st0, qk_o, qkg, qkt, er, used, sc, s1, r1, s2, r2, s3, r3, m1, m2, *rest):
+           gv, go, V, own1, st0, qk_o, qkg, qkt, er, used, sc, s1, r1, s2, r2, m1, *rest):
     ssem, rsem, lsem = rest[-3:]
-    names = ("ts1", "tr1", "ts2", "tr2", "ts3", "tr3", "ax1", "ax2", "ax3")
-    T = [dict(zip(names, rest[i * 9 : (i + 1) * 9])) for i in range(len(PARTS))]
+    names = ("ts1", "tr1", "tr2", "ax1", "ax2", "st1")
+    T = [dict(zip(names, rest[i * 6 : (i + 1) * 6])) for i in range(len(PARTS))]
     cp = Copies(ssem, rsem, lsem)
 
     vx, vy = lax.axis_index("vx"), lax.axis_index("vy")
@@ -126,22 +126,73 @@
     for o in (1, 2, 3):
         group_peers += [device_of(x, (y + o) % 4, zz, cc) for zz in (z, zmate) for cc in (c, 1 - c)]
 
-    barrier = pltpu.get_barrier_semaphore()
-    partners = group_peers + [peer("x", o) for o in (1, 2, 3)] + [device_of(x, y, (zmate + 2) % 4, c), peer("z", 2)]
-    for p in partners:
-        pl.semaphore_signal(barrier, inc=1, device_id=p, device_id_type=MESH)
+    def row_of(yy, zz, cc):
+        return pl.multiple_of(((zz * 4 + yy) * 2 + cc) * 64, 64)
+
+    class Gather:
+        def __init__(self, g, local):
+            self.g = g
+            local.wait()
+            self.y, self.z, self.core = {}, {}, {}
+
+        def put(self, o, half, zz, device):
+            rows = 64 if half is None else 32
+            start = row_of((y + o) % 4, zz, c) + (half or 0) * 32
+            ref = self.g.at[pl.ds(pl.multiple_of(start, 32), rows), :]
+            return cp.remote(ref, ref, device)
+
+        def to_y(self):
+            for o in (1, 3, 2):
+                self.y[4 - o] = self.put(0, None, zl, peer("y", o))
+
+        def to_z(self, o):
+            self.z[o] = [self.put(o, half, zl, peer("z", 1 + 2 * half)) for half in (0, 1)]
+
+        def to_core(self, o, far):
+            self.core.setdefault(o, []).append(self.put(o, None, 1 - zl if far else zl, other))
+
+        def start(self):
+            self.to_y()
+            self.to_z(0)
+            self.to_core(0, False)
+
+        def from_y(self, *order):
+            for o in order:
+                self.y[o].wait_recv()
+                self.to_z(o)
+                self.to_core(o, False)
+
+        def from_z(self, *order):
+            for o in order:
+                for k in self.z[o]:
+                    k.wait_recv()
+                self.to_core(o, True)
+
+        def complete(self, *order):
+            for o in order:
+                for k in self.core[o]:
+                    k.wait_recv()
+
+    with scope("signals"):
+        barrier = pltpu.get_barrier_semaphore()
+        partners = group_peers + [peer("x", o) for o in (1, 2, 3)] + [device_of(x, y, (zmate + 2) % 4, c), peer("z", 2)]
+        for p in partners:
+            pl.semaphore_signal(barrier, inc=1, device_id=p, device_id_type=MESH)
+    own_rows = pl.ds(row_of(y, zl, c), 64)
+    load_wv = [cp.here(wv.at[:, BLOCK * b : BLOCK * b + BLOCK], gv.at[j, own_rows, :]) for j, b in enumerate(SEQUENCE)]
+    load_wo = cp.here(wo, go.at[own_rows, :])
     load_wk = cp.here(wk, wk_v.at[pl.ds(0, 64), :])
     load_query = cp.here(query_h, query)
     load_slot = cp.here(vslot_h, vslot)
     load_emb = cp.here(emb_h, emb)
     load_tok = cp.here(tok.at[:, :, :, c], tokv.at[0])
 
-    def row_of(yy, zz, cc):
-        return pl.multiple_of(((zz * 4 + yy) * 2 + cc) * 64, 64)
-
-    own_rows = pl.ds(row_of(y, zl, c), 64)
-    load_wv = [cp.here(wv.at[:, BLOCK * b : BLOCK * b + BLOCK], gv.at[j, own_rows, :]) for j, b in enumerate(SEQUENCE)]
-    load_wo = cp.here(wo, go.at[own_rows, :])
+    with scope("w_barrier"):
+        pl.semaphore_wait(barrier, len(partners))
+
+    with scope("gatherA"):
+        A = [Gather(gv.at[0], load_wv[0])]
+        A[0].start()
 
     head_lane = lax.broadcasted_iota(jnp.int32, (HEADS, D), 1) // 64
     head_row = lax.broadcasted_iota(jnp.int32, (HEADS, D), 0)
@@ -157,6 +208,16 @@
     qk = lax.dot_general(q_matrix, wk_v[...], nt, preferred_element_type=F32) * 0.125
     qk_o[...] = qk[:8] + pltpu.roll(qk[8:], 64, axis=1)
 
+    mine = (zl * 4 + y) * 2 + c
+    qk_copies = [cp.remote(qk_o, qkg.at[mine], p) for p in group_peers]
+    with scope("gatherA2"):
+        tok_copy = cp.remote(tok.at[:, :, :, 1 - c], tokv.at[1], other)
+        for b in range(1, 4):
+            A.append(Gather(gv.at[b], load_wv[b]))
+            A[b].start()
+        B = Gather(go, load_wo)
+        B.start()
+
     position = vx * 16 + vy
     partner_pos = position + 1 - 2 * c
     load_slot.wait()
@@ -167,65 +228,6 @@
     load_emb.wait()
     er[...] = jnp.dot(match.astype(BF16), emb[...], preferred_element_type=F32)
     used[...] = jnp.broadcast_to(jnp.sum(match, axis=1, keepdims=True), (8, 128))
-
-    with scope("w_barrier"):
-        pl.semaphore_wait(barrier, len(partners))
-
-    mine = (zl * 4 + y) * 2 + c
-    qk_copies = [cp.remote(qk_o, qkg.at[mine], p) for p in group_peers]
-
-    class Gather:
-        def __init__(self, g, local):
-            self.g = g
-            local.wait()
-            self.y, self.z, self.core = {}, {}, {}
-
-        def put(self, o, half, zz, device):
-            rows = 64 if half is None else 32
-            start = row_of((y + o) % 4, zz, c) + (half or 0) * 32
-            ref = self.g.at[pl.ds(pl.multiple_of(start, 32), rows), :]
-            return cp.remote(ref, ref, device)
-
-        def to_y(self):
-            for o in (1, 3, 2):
-                self.y[4 - o] = self.put(0, None, zl, peer("y", o))
-
-        def to_z(self, o):
-            self.z[o] = [self.put(o, half, zl, peer("z", 1 + 2 * half)) for half in (0, 1)]
-
-        def to_core(self, o, far):
-            self.core.setdefault(o, []).append(self.put(o, None, 1 - zl if far else zl, other))
-
-        def start(self):
-            self.to_y()
-            self.to_z(0)
-            self.to_core(0, False)
-
-        def from_y(self, *order):
-            for o in order:
-                self.y[o].wait_recv()
-                self.to_z(o)
-                self.to_core(o, False)
-
-        def from_z(self, *order):
-            for o in order:
-                for k in self.z[o]:
-                    k.wait_recv()
-                self.to_core(o, True)
-
-        def complete(self, *order):
-            for o in order:
-                for k in self.core[o]:
-                    k.wait_recv()
-
-    with scope("gatherA"):
-        A = [Gather(gv.at[b], load_wv[b]) for b in range(4)]
-        A[0].start()
-        tok_copy = cp.remote(tok.at[:, :, :, 1 - c], tokv.at[1], other)
-        for b in range(1, 4):
-            A[b].start()
-        B = Gather(go, load_wo)
-        B.start()
 
     def mix(k):
         def step(i, carry):
@@ -321,53 +323,40 @@
             for o in (1, 2, 3):
                 t["sc1"].append(cp.remote(t["ts1"].at[o - 1], t["tr1"].at[o - 1], peer(dims[0], o)))
 
+    plane = [(o, p) for o in range(4) for p in range(4) if o or p]
+
+    def rest_of(dims):
+        return [d for d in NAT if d != dims[0]]
+
+    def plane_peer(dims, o, p):
+        at = dict(me)
+        first, second = rest_of(dims)
+        at[first], at[second] = (me[first] + o) % 4, (me[second] + p) % 4
+        return at[first], at[second], device_of(at["x"], at["y"], at["z"], c)
+
     def stats1():
         for t, (l0, w, dims) in zip(T, PARTS):
             for k in t["sc1"]:
                 k.wait_recv()
             own = pick(st0, NAT.index(dims[0]), me[dims[0]], slice(None), 3)
             m, l, scales = merge_stats([own] + [unfold(t["tr1"][o]) for o in range(3)])
+            t["st1"][...] = pack_stats(m, l).reshape(4, 4, 8, 128)
             for k, a in enumerate(scales):
                 t["ax1"][k] = expand(a, l0, w)
-            left = [d for d in NAT if d != dims[0]]
-            axis = left.index(dims[1])
-            t["st1"] = pack_stats(m, l).reshape(4, 4, 8, 128)
-            stats = t["st1"]
-            pieces = [(stats[i] if axis == 0 else stats[:, i]).reshape(32, 128) for i in range(4)]
-            t["own1"] = choose(pieces, me[dims[1]])
+        for t, (l0, w, dims) in zip(T, PARTS):
             t["sc2"] = []
-            for o in (1, 2, 3):
-                t["ts2"][o - 1] = fold(choose(pieces, (me[dims[1]] + o) % 4))
-                t["sc2"].append(cp.remote(t["ts2"].at[o - 1], t["tr2"].at[o - 1], peer(dims[1], o)))
-
-    def choose(pieces, index):
-        got = pieces[3]
-        for i in (2, 1, 0):
-            got = jnp.where(index == i, pieces[i], got)
-        return got
+            for n, (o, p) in enumerate(plane):
+                i, k, device = plane_peer(dims, o, p)
+                t["sc2"].append(cp.remote(t["st1"].at[i, k], t["tr2"].at[n], device))
 
     def stats2():
         for t, (l0, w, dims) in zip(T, PARTS):
             for k in t["sc2"]:
                 k.wait_recv()
-            m, l, scales = merge_stats([t["own1"]] + [unfold(t["tr2"][o]) for o in range(3)])
+            first, second = rest_of(dims)
+            m, l, scales = merge_stats([t["st1"][me[first], me[second]]] + [t["tr2"][n] for n in range(15)])
             for k, a in enumerate(scales):
-                t["ax2"][k] = expand(a, l0, w)
-            stats = pack_stats(m, l)
-            pieces = [stats[8 * i : 8 * i + 8] for i in range(4)]
-            t["own2"] = choose(pieces, me[dims[2]])
-            t["sc3"] = []
-            for o in (1, 2, 3):
-                t["ts3"][o - 1] = choose(pieces, (me[dims[2]] + o) % 4)
-                t["sc3"].append(cp.remote(t["ts3"].at[o - 1], t["tr3"].at[o - 1], peer(dims[2], o)))
-
-    def stats3():
-        for t, (l0, w, dims) in zip(T, PARTS):
-            for k in t["sc3"]:
-                k.wait_recv()
-            m, l, scales = merge_stats([t["own2"]] + [t["tr3"][o] for o in range(3)])
-            for k, a in enumerate(scales):
-                t["ax3"][k] = expand(a / l, l0, w)
+                t["ax2"][k] = expand(a / l, l0, w)
 
     def offsets(o):
         yy = (y + o) % 4
@@ -450,7 +439,7 @@
     with scope("stats1"):
         stats1()
 
-    c2, c3 = [[] for _ in range(4)], [[] for _ in range(4)]
+    c2 = [[] for _ in range(4)]
 
     def part_of(j):
         b = SEQUENCE[j]
@@ -459,61 +448,41 @@
 
     def reduce2(j):
         t, dims, cols = part_of(j)
-        axis = [d for d in NAT if d != dims[0]].index(dims[1])
         with scope("w_c1"):
             for k in c1[j]:
                 k.wait_recv()
         total = t["ax1"][0, :, cols] * own1[j]
         for o in range(3):
             total = total + t["ax1"][o + 1, :, cols] * r1[j, o].astype(F32)
-        m1[j] = total.reshape(4, 4, 8, BLOCK)
-        for o in (2, 1, 3):
-            s2[j, o - 1] = pick(m1.at[j], axis, (me[dims[1]] + o) % 4, slice(None), 2).astype(BF16)
-        for o in (2, 1, 3):
-            c2[j].append(cp.remote(s2.at[j, o - 1], r2.at[j, o - 1], peer(dims[1], o)))
-
-    def reduce3(j):
+        total = total.reshape(4, 4, 8, BLOCK)
+        m1[j] = total
+        s2[j] = total.astype(BF16)
+        for n, (o, p) in enumerate(plane):
+            i, k, device = plane_peer(dims, o, p)
+            c2[j].append(cp.remote(s2.at[j, i, k], r2.at[j, n], device))
+
+    def result(j):
         t, dims, cols = part_of(j)
-        axis = [d for d in NAT if d != dims[0]].index(dims[1])
+        first, second = rest_of(dims)
         with scope("w_c2"):
             for k in c2[j]:
                 k.wait_recv()
-        total = t["ax2"][0, :, cols] * pick(m1.at[j], axis, me[dims[1]], slice(None), 2)
-        for o in range(3):
-            total = total + t["ax2"][o + 1, :, cols] * r2[j, o].astype(F32)
-        m2[j] = total.reshape(4, 8, BLOCK)
-        for o in (2, 1, 3):
-            s3[j, o - 1] = m2[j, (me[dims[2]] + o) % 4].astype(BF16)
-        for o in (2, 1, 3):
-            c3[j].append(cp.remote(s3.at[j, o - 1], r3.at[j, o - 1], peer(dims[2], o)))
-
-    def result(j):
-        t, dims, cols = part_of(j)
-        with scope("w_c3"):
-            for k in c3[j]:
-                k.wait_recv()
-        total = t["ax3"][0, :, cols] * m2[j, me[dims[2]]]
-        for o in range(3):
-            total = total + t["ax3"][o + 1, :, cols] * r3[j, o].astype(F32)
+        total = t["ax2"][0, :, cols] * m1[j, me[first], me[second]]
+        for n in range(15):
+            total = total + t["ax2"][n + 1, :, cols] * r2[j, n].astype(F32)
         return total
 
-    for j in (0, 1, 2):
+    for j in range(4):
         reduce2(j)
+    with scope("B_z"):
+        B.from_z(3, 1, 2)
     with scope("stats2"):
         stats2()
-    reduce2(3)
-    with scope("B_z"):
-        B.from_z(3, 1, 2)
-    for j in (0, 1, 2):
-        reduce3(j)
-    with scope("stats3"):
-        stats3()
-    reduce3(3)
     context = [result(j) for j in (0, 1, 2)]
     with scope("B_c"):
         B.complete(0, 3, 1, 2)
     with scope("w_sends0"):
-        early_sends, cp.open = cp.open[:-6], cp.open[-6:]
+        early_sends, cp.open = cp.open[:-15], cp.open[-15:]
         for k in early_sends:
             k.wait_send()
     context.append(result(3))
@@ -532,10 +501,8 @@
     part = []
     for _, w, _ in PARTS:
         part += [
-            V((3, 32, 128), F32), V((3, 32, 128), F32),
-            V((3, 8, 128), F32), V((3, 8, 128), F32),
-            V((3, 8, 128), F32), V((3, 8, 128), F32),
-            V((4, 128, w), F32), V((4, 32, w), F32), V((4, 8, w), F32),
+            V((3, 32, 128), F32), V((3, 32, 128), F32), V((15, 8, 128), F32),
+            V((4, 128, w), F32), V((16, 8, w), F32), V((4, 4, 8, 128), F32),
         ]
     result = pl.pallas_call(
         kernel,
@@ -549,9 +516,7 @@
             V((8, 128), F32), V((16, 8, 128), F32), V((128, D), BF16), V((8, D), F32), V((8, 128), F32),
             V((2, 4, 4, 4, 8, 128), F32),
             V((4, 3, 128, BLOCK), BF16), V((4, 3, 128, BLOCK), BF16),
-            V((4, 3, 32, BLOCK), BF16), V((4, 3, 32, BLOCK), BF16),
-            V((4, 3, 8, BLOCK), BF16), V((4, 3, 8, BLOCK), BF16),
-            V((4, 4, 4, 8, BLOCK), F32), V((4, 4, 8, BLOCK), F32),
+            V((4, 4, 4, 8, BLOCK), BF16), V((4, 15, 8, BLOCK), BF16), V((4, 4, 4, 8, BLOCK), F32),
             *part,
             pltpu.SemaphoreType.DMA((SEND_SEMS,)), pltpu.SemaphoreType.DMA((SEND_SEMS,)), pltpu.SemaphoreType.DMA((12,)),
         ],

time: 43.4 us -> 41.4 us (0.954)
  Pallas kernels: 41.9 us -> 39.9 us
    pallas_call x1, Pallas kernels: 41.9 us -> 39.9 us  [shards(): pl.pallas_call(kernel, out_shape=jax.ShapeDtypeStruct((8, D), BF16), in_s...]
where the time goes in v7:
time: 41.4 us; the launch traced here: 41.2 us
  Pallas kernels  39.9 us (96%)
  local copies, waits for them, and re-layouts  1.32 us (3%)
    pallas_call x1, Pallas kernels, shards(): pl.pallas_call(kernel, out_shape=jax.ShapeDtypeStruct((8, D), BF16), in_s...  39.9 us
    unnamed x1, local copies, waits for them, and re-layouts  1.32 us

profile of v7, /device:TPU:0, one launch (start us, length us, event | category | flops | bytes accessed | tf_op | source)
XLA Modules:
  0.0 41.2 jit_solution(16153587499586402997)
XLA Ops:
  0.0 39.9 %shard_map.73 = bf16[8,1024]{1,0:T(8,128)(2,1)} custom-call(bf16[4,4,4,2,8,1024]{5,4,3,2,1,0:T(8,128)(2,1)} %bitcast.4, bf16[91,1024]{1,0:T(8,128)(2,1)} %emb_h.1, bf16[8,128]{1,0:T(8,128)(2,1)} %bitcast.6, bf16[64,1024]{1,0:T(8,128)(2,1)} %wk.1, bf16[64,1024]{1,0:T(8,128)(2,1)} %wv.1, bf16[64,1024]{1,0:T(8,128)(2,1)} %wo.1, s32[1,91]{1,0:T(1,128)} %bitcast.7), custom_call_target="tpu_custom_call" | custom-call | tf_op jit(solution)/shard_map/pallas_call | solution.py:507
  39.9 1.3 %copy.9 = bf16[1,8,1024]{2,1,0:T(8,128)(2,1)} copy(bf16[1,8,1024]{2,1,0:T(8,128)(2,1)} %bitcast.5) | data formatting | bytes 32768

commit v8 on v7

--- a/solution.py
+++ b/solution.py
@@ -18,7 +18,7 @@
 PARTS = ((0, 512, ("x", "y", "z")), (512, 512, ("y", "x", "z")))
 SEQUENCE = (0, 2, 1, 3)
 BLOCK = 256
-SEND_SEMS = 264
+SENDS, RECVS = 13, 54
 
 
 def scope(name):
@@ -31,28 +31,26 @@
 
 class Copies:
     def __init__(self, send, recv, local):
-        self.send, self.recv, self.local = send, recv, local
-        self.n, self.k, self.open = 0, 0, []
-
-    def remote(self, src, dst, device):
-        copy = pltpu.make_async_remote_copy(
-            src_ref=src,
-            dst_ref=dst,
-            send_sem=self.send.at[self.n],
-            recv_sem=self.recv.at[self.n],
-            device_id=device,
-            device_id_type=MESH,
-        )
-        self.n += 1
-        copy.start()
-        self.open.append(copy)
-        return copy
+        self.sems = {"send": send, "recv": recv}
+        self.local, self.k, self.used = local, 0, {"send": 0, "recv": 0}
+
+    def new(self, side):
+        self.used[side] += 1
+        return self.sems[side].at[self.used[side] - 1]
+
+    def remote(self, src, dst, device, send, recv):
+        pltpu.make_async_remote_copy(
+            src_ref=src, dst_ref=dst, send_sem=send, recv_sem=recv, device_id=device, device_id_type=MESH
+        ).start()
 
     def here(self, src, dst):
         copy = pltpu.make_async_copy(src, dst, self.local.at[self.k])
         self.k += 1
         copy.start()
         return copy
+
+    def wait(self, like, sem):
+        pltpu.make_async_copy(like, like, sem).wait()
 
 
 def lanes_iota(rows):
@@ -105,8 +103,8 @@
 def kernel(tok, emb_h, query_h, wk, wv, wo, vslot_h, out, emb, query, vslot, wk_v, tokv, mixed, mixed_y,
            gv, go, V, own1, st0, qk_o, qkg, qkt, er, used, sc, s1, r1, s2, r2, m1, *rest):
     ssem, rsem, lsem = rest[-3:]
-    names = ("ts1", "tr1", "tr2", "ax1", "ax2", "st1")
-    T = [dict(zip(names, rest[i * 6 : (i + 1) * 6])) for i in range(len(PARTS))]
+    names = ("ts1", "tr1", "tr2", "ax1", "ax2", "st1", "a1")
+    T = [dict(zip(names, rest[i * 7 : (i + 1) * 7])) for i in range(len(PARTS))]
     cp = Copies(ssem, rsem, lsem)
 
     vx, vy = lax.axis_index("vx"), lax.axis_index("vy")
@@ -129,49 +127,54 @@
     def row_of(yy, zz, cc):
         return pl.multiple_of(((zz * 4 + yy) * 2 + cc) * 64, 64)
 
+    kinds = {"own": (0,), "near": (3, 1), "far": (2,)}
+    kind_of = {0: "own", 1: "near", 2: "far", 3: "near"}
+
     class Gather:
         def __init__(self, g, local):
             self.g = g
             local.wait()
-            self.y, self.z, self.core = {}, {}, {}
-
-        def put(self, o, half, zz, device):
+            self.send = cp.new("send")
+            self.recv = {way + kind: cp.new("recv") for way in "yzc" for kind in kinds if way + kind != "yown"}
+
+        def put(self, o, half, zz, device, recv):
             rows = 64 if half is None else 32
             start = row_of((y + o) % 4, zz, c) + (half or 0) * 32
             ref = self.g.at[pl.ds(pl.multiple_of(start, 32), rows), :]
-            return cp.remote(ref, ref, device)
-
-        def to_y(self):
+            cp.remote(ref, ref, device, self.send, self.recv[recv])
+
+        def to_z(self, o):
+            for half in (0, 1):
+                self.put(o, half, zl, peer("z", 1 + 2 * half), "z" + kind_of[o])
+
+        def to_core(self, o, far):
+            self.put(o, None, 1 - zl if far else zl, other, "c" + kind_of[o])
+
+        def start(self):
             for o in (1, 3, 2):
-                self.y[4 - o] = self.put(0, None, zl, peer("y", o))
-
-        def to_z(self, o):
-            self.z[o] = [self.put(o, half, zl, peer("z", 1 + 2 * half)) for half in (0, 1)]
-
-        def to_core(self, o, far):
-            self.core.setdefault(o, []).append(self.put(o, None, 1 - zl if far else zl, other))
-
-        def start(self):
-            self.to_y()
+                self.put(0, None, zl, peer("y", o), "y" + kind_of[o])
             self.to_z(0)
             self.to_core(0, False)
 
-        def from_y(self, *order):
-            for o in order:
-                self.y[o].wait_recv()
+        def wait(self, way, kind, rows):
+            cp.wait(self.g.at[pl.ds(0, rows * len(kinds[kind])), :], self.recv[way + kind])
+
+        def from_y(self, kind):
+            self.wait("y", kind, 64)
+            for o in kinds[kind]:
                 self.to_z(o)
                 self.to_core(o, False)
 
-        def from_z(self, *order):
-            for o in order:
-                for k in self.z[o]:
-                    k.wait_recv()
+        def from_z(self, kind):
+            self.wait("z", kind, 64)
+            for o in kinds[kind]:
                 self.to_core(o, True)
 
-        def complete(self, *order):
-            for o in order:
-                for k in self.core[o]:
-                    k.wait_recv()
+        def complete(self, kind):
+            self.wait("c", kind, 128)
+
+        def finish(self):
+            cp.wait(self.g.at[pl.ds(0, 960), :], self.send)
 
     with scope("signals"):
         barrier = pltpu.get_barrier_semaphore()
@@ -209,9 +212,12 @@
     qk_o[...] = qk[:8] + pltpu.roll(qk[8:], 64, axis=1)
 
     mine = (zl * 4 + y) * 2 + c
-    qk_copies = [cp.remote(qk_o, qkg.at[mine], p) for p in group_peers]
+    qk_send, qk_recv = cp.new("send"), cp.new("recv")
+    for p in group_peers:
+        cp.remote(qk_o, qkg.at[mine], p, qk_send, qk_recv)
     with scope("gatherA2"):
-        tok_copy = cp.remote(tok.at[:, :, :, 1 - c], tokv.at[1], other)
+        tok_send, tok_recv = cp.new("send"), cp.new("recv")
+        cp.remote(tok.at[:, :, :, 1 - c], tokv.at[1], other, tok_send, tok_recv)
         for b in range(1, 4):
             A.append(Gather(gv.at[b], load_wv[b]))
             A[b].start()
@@ -256,26 +262,75 @@
         sc[1, i] = w1.reshape(4, 4, 8, 128)
         return carry
 
+    def offsets(o):
+        yy = (y + o) % 4
+        return pl.multiple_of(yy * 128, 128), pl.multiple_of((4 + yy) * 128, 128)
+
+    def product(j, groups, source, start, rows):
+        at = pl.ds(pl.multiple_of(start, rows), rows)
+        lhs = jnp.concatenate([source[at, pl.ds(a, 128)] for o in groups for a in offsets(o)], axis=1)
+        rhs = jnp.concatenate([gv[j, pl.ds(a, 128), :] for o in groups for a in offsets(o)], axis=0)
+        return jnp.dot(lhs, rhs, preferred_element_type=F32)
+
+    def early(j, groups, fresh):
+        def step(i, carry):
+            at = pl.ds(pl.multiple_of(i * 256, 256), 256)
+            r = product(j, groups, mixed if SEQUENCE[j] < 2 else mixed_y, i * 256, 256)
+            V[j, at, :] = r if fresh else V[j, at, :] + r
+            return carry
+
+        lax.fori_loop(0, 4, step, 0)
+
+    def first_products():
+        a, b = offsets(0)
+
+        def step(i, carry):
+            at = pl.ds(pl.multiple_of(i * 512, 512), 512)
+            for source, blocks in ((mixed, (0, 2)), (mixed_y, (1, 3))):
+                lhs = jnp.concatenate([source[at, pl.ds(a, 128)], source[at, pl.ds(b, 128)]], axis=1)
+                rhs = jnp.concatenate(
+                    [jnp.concatenate([gv[j, pl.ds(a, 128), :], gv[j, pl.ds(b, 128), :]], axis=0) for j in blocks], axis=1
+                )
+                r = jnp.dot(lhs, rhs, preferred_element_type=F32)
+                for n, j in enumerate(blocks):
+                    V[j, at, :] = r[:, BLOCK * n : BLOCK * n + BLOCK]
+            return carry
+
+        lax.fori_loop(0, 2, step, 0)
+
+    def weighted(j, groups, dim, index):
+        total = None
+        for k in range(2):
+            start = k * 512 + index * 128
+            r = product(j, groups, mixed if dim == "x" else mixed_y, start, 128)
+            r = r + V[j, pl.ds(pl.multiple_of(start, 128), 128), :]
+            w = (sc[k, index] if dim == "x" else sc[k, :, :, index]).reshape(128, 128)
+            r = r * expand(w, BLOCK * SEQUENCE[j], BLOCK)
+            total = r if total is None else total + r
+        return total
+
     with scope("mix0"):
         load_tok.wait()
         mix(0)
     with scope("y0"):
-        A[0].from_y(3, 1)
+        A[0].from_y("near")
     with scope("z00"):
-        A[0].from_z(0)
+        for b in range(4):
+            A[b].from_z("own")
     with scope("w_tok"):
-        tok_copy.wait_recv()
+        cp.wait(tokv.at[1], tok_recv)
     with scope("mix1"):
         mix(1)
     with scope("o0"):
-        A[0].from_y(2)
-    with scope("z01"):
-        A[1].from_z(0)
+        A[0].from_y("far")
+    with scope("g00"):
+        for b in range(4):
+            A[b].complete("own")
+        first_products()
     with scope("y1"):
-        A[1].from_y(3, 1)
+        A[1].from_y("near")
     with scope("w_qk"):
-        for k in qk_copies:
-            k.wait_recv()
+        cp.wait(qkg.at[0:15], qk_recv)
     with scope("qkt"):
         qkg[mine] = qk_o[...]
         left = lax.broadcasted_iota(jnp.int32, (8, 128), 1) < 64
@@ -292,36 +347,32 @@
     with scope("score0"):
         score(0)
     with scope("o1"):
-        A[1].from_y(2)
+        A[1].from_y("far")
     with scope("y2"):
-        A[2].from_z(0)
-        A[2].from_y(3, 1)
-    with scope("zy0"):
-        A[0].from_z(3, 1)
+        A[2].from_y("near")
     with scope("score1"):
         score(1)
     with scope("o2"):
-        A[2].from_y(2)
-    with scope("y3"):
-        A[3].from_z(0)
-        A[3].from_y(3, 1)
+        A[2].from_y("far")
     with scope("pair_stats"):
         lax.fori_loop(0, 4, pair_stats, 0)
+    with scope("y3"):
+        A[3].from_y("near")
+    with scope("zy0"):
+        A[0].from_z("near")
     with scope("zo0"):
-        A[0].from_z(2)
-    with scope("o3"):
-        A[3].from_y(2)
+        A[0].from_z("far")
 
     def stats0():
         for t, (l0, w, dims) in zip(T, PARTS):
             axis = NAT.index(dims[0])
-            t["sc1"] = []
             for o in (1, 2, 3):
                 rows = pick(st0, axis, (me[dims[0]] + o) % 4, slice(None), 3)
                 t["ts1"][o - 1] = fold(rows)
         for t, (l0, w, dims) in zip(T, PARTS):
+            t["send1"], t["recv1"] = cp.new("send"), cp.new("recv")
             for o in (1, 2, 3):
-                t["sc1"].append(cp.remote(t["ts1"].at[o - 1], t["tr1"].at[o - 1], peer(dims[0], o)))
+                cp.remote(t["ts1"].at[o - 1], t["tr1"].at[o - 1], peer(dims[0], o), t["send1"], t["recv1"])
 
     plane = [(o, p) for o in range(4) for p in range(4) if o or p]
 
@@ -336,110 +387,94 @@
 
     def stats1():
         for t, (l0, w, dims) in zip(T, PARTS):
-            for k in t["sc1"]:
-                k.wait_recv()
+            cp.wait(t["tr1"], t["recv1"])
             own = pick(st0, NAT.index(dims[0]), me[dims[0]], slice(None), 3)
             m, l, scales = merge_stats([own] + [unfold(t["tr1"][o]) for o in range(3)])
             t["st1"][...] = pack_stats(m, l).reshape(4, 4, 8, 128)
             for k, a in enumerate(scales):
-                t["ax1"][k] = expand(a, l0, w)
+                t["a1"][k] = a
         for t, (l0, w, dims) in zip(T, PARTS):
-            t["sc2"] = []
+            t["send2"], t["recv2"] = cp.new("send"), cp.new("recv")
             for n, (o, p) in enumerate(plane):
                 i, k, device = plane_peer(dims, o, p)
-                t["sc2"].append(cp.remote(t["st1"].at[i, k], t["tr2"].at[n], device))
+                cp.remote(t["st1"].at[i, k], t["tr2"].at[n], device, t["send2"], t["recv2"])
+
+    def expand1():
+        for t, (l0, w, dims) in zip(T, PARTS):
+            for k in range(4):
+                t["ax1"][k] = expand(t["a1"][k], l0, w)
 
     def stats2():
         for t, (l0, w, dims) in zip(T, PARTS):
-            for k in t["sc2"]:
-                k.wait_recv()
+            cp.wait(t["tr2"], t["recv2"])
             first, second = rest_of(dims)
             m, l, scales = merge_stats([t["st1"][me[first], me[second]]] + [t["tr2"][n] for n in range(15)])
+            inverse = 1.0 / l
             for k, a in enumerate(scales):
-                t["ax2"][k] = expand(a / l, l0, w)
-
-    def offsets(o):
-        yy = (y + o) % 4
-        return pl.multiple_of(yy * 128, 128), pl.multiple_of((4 + yy) * 128, 128)
-
-    def product(j, groups, source, start, rows):
-        at = pl.ds(pl.multiple_of(start, rows), rows)
-        lhs = jnp.concatenate([source[at, pl.ds(a, 128)] for o in groups for a in offsets(o)], axis=1)
-        rhs = jnp.concatenate([gv[j, pl.ds(a, 128), :] for o in groups for a in offsets(o)], axis=0)
-        return jnp.dot(lhs, rhs, preferred_element_type=F32)
-
-    def early(j, groups):
-        def step(i, carry):
-            V[pl.ds(pl.multiple_of(i * 256, 256), 256), :] = product(j, groups, mixed, i * 256, 256)
-            return carry
-
-        lax.fori_loop(0, 4, step, 0)
-
-    def weighted(j, groups, dim, index):
-        total = None
-        for k in range(2):
-            start = k * 512 + index * 128
-            r = product(j, groups, mixed if dim == "x" else mixed_y, start, 128)
-            if len(groups) < 4:
-                r = r + V[pl.ds(pl.multiple_of(start, 128), 128), :]
-            w = (sc[k, index] if dim == "x" else sc[k, :, :, index]).reshape(128, 128)
-            r = r * expand(w, BLOCK * SEQUENCE[j], BLOCK)
-            total = r if total is None else total + r
-        return total
-
-    c1 = [[] for _ in range(4)]
+                t["ax2"][k] = expand(a * inverse, l0, w)
+
+    send1, recv1 = cp.new("send"), [cp.new("recv") for _ in range(4)]
 
     def reduce1(j, groups):
         dim = PARTS[SEQUENCE[j] // 2][2][0]
         for o in (2, 1, 3):
             s1[j, o - 1] = weighted(j, groups, dim, (me[dim] + o) % 4).astype(BF16)
-            c1[j].append(cp.remote(s1.at[j, o - 1], r1.at[j, o - 1], peer(dim, o)))
+            cp.remote(s1.at[j, o - 1], r1.at[j, o - 1], peer(dim, o), send1, recv1[j])
         own1[j] = weighted(j, groups, dim, me[dim])
 
     ALL = (0, 3, 1, 2)
 
-    with scope("zy1"):
-        A[1].from_z(3, 1)
-    with scope("c00"):
-        A[0].complete(0, 3, 1)
-    with scope("early0"):
-        early(0, ALL[:3])
-    with scope("zo1"):
-        A[1].from_z(2)
-    with scope("zy2"):
-        A[2].from_z(3, 1)
-    with scope("c0"):
-        A[0].complete(2)
-    with scope("late0"):
-        reduce1(0, ALL[3:])
     with scope("stats0"):
         stats0()
+    with scope("o3"):
+        A[3].from_y("far")
+    with scope("zy1"):
+        A[1].from_z("near")
+    with scope("c00"):
+        A[0].complete("near")
+    with scope("early0"):
+        early(0, (3, 1), False)
+    with scope("zo1"):
+        A[1].from_z("far")
+    with scope("zy2"):
+        A[2].from_z("near")
+    with scope("c0"):
+        A[0].complete("far")
+    with scope("late0"):
+        reduce1(0, (2,))
     with scope("B_z0"):
-        B.from_z(0)
+        B.from_z("own")
     with scope("zo2"):
-        A[2].from_z(2)
+        A[2].from_z("far")
+    with scope("B_y"):
+        B.from_y("near")
     with scope("c1"):
-        A[1].complete(0, 3, 1, 2)
+        A[1].complete("near")
+        A[1].complete("far")
     with scope("late1"):
-        reduce1(1, ALL)
+        reduce1(1, ALL[1:])
     with scope("zy3"):
-        A[3].from_z(3, 1)
+        A[3].from_z("near")
     with scope("zo3"):
-        A[3].from_z(2)
+        A[3].from_z("far")
     with scope("c2"):
-        A[2].complete(0, 3, 1, 2)
+        A[2].complete("near")
+        A[2].complete("far")
     with scope("late2"):
-        reduce1(2, ALL)
-    with scope("B_y"):
-        B.from_y(3, 1, 2)
-    with scope("c3"):
-        A[3].complete(0, 3, 1, 2)
-    with scope("late3"):
-        reduce1(3, ALL)
+        reduce1(2, ALL[1:])
+    with scope("B_o"):
+        B.from_y("far")
     with scope("stats1"):
         stats1()
-
-    c2 = [[] for _ in range(4)]
+    with scope("c3"):
+        A[3].complete("near")
+        A[3].complete("far")
+    with scope("late3"):
+        reduce1(3, ALL[1:])
+    with scope("expand1"):
+        expand1()
+
+    send2, recv2 = cp.new("send"), [cp.new("recv") for _ in range(4)]
 
     def part_of(j):
         b = SEQUENCE[j]
@@ -449,8 +484,7 @@
     def reduce2(j):
         t, dims, cols = part_of(j)
         with scope("w_c1"):
-            for k in c1[j]:
-                k.wait_recv()
+            cp.wait(r1.at[j], recv1[j])
         total = t["ax1"][0, :, cols] * own1[j]
         for o in range(3):
             total = total + t["ax1"][o + 1, :, cols] * r1[j, o].astype(F32)
@@ -459,39 +493,46 @@
         s2[j] = total.astype(BF16)
         for n, (o, p) in enumerate(plane):
             i, k, device = plane_peer(dims, o, p)
-            c2[j].append(cp.remote(s2.at[j, i, k], r2.at[j, n], device))
+            cp.remote(s2.at[j, i, k], r2.at[j, n], device, send2, recv2[j])
 
     def result(j):
         t, dims, cols = part_of(j)
         first, second = rest_of(dims)
         with scope("w_c2"):
-            for k in c2[j]:
-                k.wait_recv()
+            cp.wait(r2.at[j], recv2[j])
         total = t["ax2"][0, :, cols] * m1[j, me[first], me[second]]
         for n in range(15):
             total = total + t["ax2"][n + 1, :, cols] * r2[j, n].astype(F32)
         return total
 
-    for j in range(4):
+    for j in range(3):
         reduce2(j)
     with scope("B_z"):
-        B.from_z(3, 1, 2)
+        B.from_z("near")
+    reduce2(3)
     with scope("stats2"):
         stats2()
+    with scope("B_z2"):
+        B.from_z("far")
     context = [result(j) for j in (0, 1, 2)]
     with scope("B_c"):
-        B.complete(0, 3, 1, 2)
+        for kind in kinds:
+            B.complete(kind)
     with scope("w_sends0"):
-        early_sends, cp.open = cp.open[:-15], cp.open[-15:]
-        for k in early_sends:
-            k.wait_send()
+        for gather in A + [B]:
+            gather.finish()
+        cp.wait(qkg.at[0:15], qk_send)
+        cp.wait(tokv.at[1], tok_send)
+        cp.wait(s1, send1)
+        for t in T:
+            cp.wait(t["ts1"], t["send1"])
+            cp.wait(t["tr2"], t["send2"])
     context.append(result(3))
     with scope("tail"):
         context = jnp.concatenate([context[SEQUENCE.index(b)] for b in range(4)], axis=1).astype(BF16)
         out[...] = jnp.dot(context, go[...], preferred_element_type=F32).astype(BF16)
     with scope("w_sends"):
-        for k in cp.open:
-            k.wait_send()
+        cp.wait(r2, send2)
 
 
 def shards(tokens, var_embed, query, key_weight, value_weight, out_weight, var_slot):
@@ -502,7 +543,7 @@
     for _, w, _ in PARTS:
         part += [
             V((3, 32, 128), F32), V((3, 32, 128), F32), V((15, 8, 128), F32),
-            V((4, 128, w), F32), V((16, 8, w), F32), V((4, 4, 8, 128), F32),
+            V((4, 128, w), F32), V((16, 8, w), F32), V((4, 4, 8, 128), F32), V((4, 128, 128), F32),
         ]
     result = pl.pallas_call(
         kernel,
@@ -512,13 +553,13 @@
         scratch_shapes=[
             V((91, D), BF16), V((8, 128), BF16), V((1, 91), jnp.int32), V((128, D), BF16), V((2, 4, 4, 4, 8, D), BF16),
             V((1024, D), BF16), V((1024, D), BF16), V((4, D, BLOCK), BF16), V((D, D), BF16),
-            V((1024, BLOCK), F32), V((4, 128, BLOCK), F32), V((4, 4, 4, 8, 128), F32),
+            V((4, 1024, BLOCK), F32), V((4, 128, BLOCK), F32), V((4, 4, 4, 8, 128), F32),
             V((8, 128), F32), V((16, 8, 128), F32), V((128, D), BF16), V((8, D), F32), V((8, 128), F32),
             V((2, 4, 4, 4, 8, 128), F32),
             V((4, 3, 128, BLOCK), BF16), V((4, 3, 128, BLOCK), BF16),
             V((4, 4, 4, 8, BLOCK), BF16), V((4, 15, 8, BLOCK), BF16), V((4, 4, 4, 8, BLOCK), F32),
             *part,
-            pltpu.SemaphoreType.DMA((SEND_SEMS,)), pltpu.SemaphoreType.DMA((SEND_SEMS,)), pltpu.SemaphoreType.DMA((12,)),
+            pltpu.SemaphoreType.DMA((SENDS,)), pltpu.SemaphoreType.DMA((RECVS,)), pltpu.SemaphoreType.DMA((10,)),
         ],
         compiler_params=pltpu.CompilerParams(
             collective_id=0, has_side_effects=True, vmem_limit_bytes=60 * 1024 * 1024

time: 41.4 us -> 37.7 us (0.911)
  Pallas kernels: 39.9 us -> 36.2 us
    pallas_call x1, Pallas kernels: 39.9 us -> 36.2 us  [shards(): pl.pallas_call(kernel, out_shape=jax.ShapeDtypeStruct((8, D), BF16), in_s...]
where the time goes in v8:
time: 37.7 us; the launch traced here: 37.6 us
  Pallas kernels  36.2 us (96%)
  local copies, waits for them, and re-layouts  1.32 us (4%)
    pallas_call x1, Pallas kernels, shards(): pl.pallas_call(kernel, out_shape=jax.ShapeDtypeStruct((8, D), BF16), in_s...  36.2 us
    unnamed x1, local copies, waits for them, and re-layouts  1.32 us

profile of v8, /device:TPU:0, one launch (start us, length us, event | category | flops | bytes accessed | tf_op | source)
XLA Modules:
  0.0 37.6 jit_solution(7982865788005098086)
XLA Ops:
  0.0 36.2 %shard_map.73 = bf16[8,1024]{1,0:T(8,128)(2,1)} custom-call(bf16[4,4,4,2,8,1024]{5,4,3,2,1,0:T(8,128)(2,1)} %bitcast.4, bf16[91,1024]{1,0:T(8,128)(2,1)} %emb_h.1, bf16[8,128]{1,0:T(8,128)(2,1)} %bitcast.6, bf16[64,1024]{1,0:T(8,128)(2,1)} %wk.1, bf16[64,1024]{1,0:T(8,128)(2,1)} %wv.1, bf16[64,1024]{1,0:T(8,128)(2,1)} %wo.1, s32[1,91]{1,0:T(1,128)} %bitcast.7), custom_call_target="tpu_custom_call" | custom-call | tf_op jit(solution)/shard_map/pallas_call | solution.py:548
  36.2 1.3 %copy.9 = bf16[1,8,1024]{2,1,0:T(8,128)(2,1)} copy(bf16[1,8,1024]{2,1,0:T(8,128)(2,1)} %bitcast.5) | data formatting | bytes 32768

commit v9 on v8

--- a/solution.py
+++ b/solution.py
@@ -18,7 +18,7 @@
 PARTS = ((0, 512, ("x", "y", "z")), (512, 512, ("y", "x", "z")))
 SEQUENCE = (0, 2, 1, 3)
 BLOCK = 256
-SENDS, RECVS = 13, 54
+SENDS, RECVS = 13, 49
 
 
 def scope(name):
@@ -135,7 +135,7 @@
             self.g = g
             local.wait()
             self.send = cp.new("send")
-            self.recv = {way + kind: cp.new("recv") for way in "yzc" for kind in kinds if way + kind != "yown"}
+            self.recv = {name: cp.new("recv") for name in ("ynear", "yfar", "zown", "znear", "zfar", "same", "cross")}
 
         def put(self, o, half, zz, device, recv):
             rows = 64 if half is None else 32
@@ -148,11 +148,14 @@
                 self.put(o, half, zl, peer("z", 1 + 2 * half), "z" + kind_of[o])
 
         def to_core(self, o, far):
-            self.put(o, None, 1 - zl if far else zl, other, "c" + kind_of[o])
-
-        def start(self):
-            for o in (1, 3, 2):
+            self.put(o, None, 1 - zl if far else zl, other, "cross" if far else "same")
+
+        def to_y(self, *order):
+            for o in order:
                 self.put(0, None, zl, peer("y", o), "y" + kind_of[o])
+
+        def start(self, *order):
+            self.to_y(*order)
             self.to_z(0)
             self.to_core(0, False)
 
@@ -170,8 +173,8 @@
             for o in kinds[kind]:
                 self.to_core(o, True)
 
-        def complete(self, kind):
-            self.wait("c", kind, 128)
+        def complete(self, half):
+            cp.wait(self.g.at[0:256, :], self.recv[half])
 
         def finish(self):
             cp.wait(self.g.at[pl.ds(0, 960), :], self.send)
@@ -195,7 +198,7 @@
 
     with scope("gatherA"):
         A = [Gather(gv.at[0], load_wv[0])]
-        A[0].start()
+        A[0].start(1, 3, 2)
 
     head_lane = lax.broadcasted_iota(jnp.int32, (HEADS, D), 1) // 64
     head_row = lax.broadcasted_iota(jnp.int32, (HEADS, D), 0)
@@ -220,9 +223,9 @@
         cp.remote(tok.at[:, :, :, 1 - c], tokv.at[1], other, tok_send, tok_recv)
         for b in range(1, 4):
             A.append(Gather(gv.at[b], load_wv[b]))
-            A[b].start()
+            A[b].start(1, 3, 2)
         B = Gather(go, load_wo)
-        B.start()
+        B.start(1, 3)
 
     position = vx * 16 + vy
     partner_pos = position + 1 - 2 * c
@@ -262,47 +265,24 @@
         sc[1, i] = w1.reshape(4, 4, 8, 128)
         return carry
 
-    def offsets(o):
-        yy = (y + o) % 4
-        return pl.multiple_of(yy * 128, 128), pl.multiple_of((4 + yy) * 128, 128)
-
-    def product(j, groups, source, start, rows):
+    def product(j, half, source, start, rows):
         at = pl.ds(pl.multiple_of(start, rows), rows)
-        lhs = jnp.concatenate([source[at, pl.ds(a, 128)] for o in groups for a in offsets(o)], axis=1)
-        rhs = jnp.concatenate([gv[j, pl.ds(a, 128), :] for o in groups for a in offsets(o)], axis=0)
-        return jnp.dot(lhs, rhs, preferred_element_type=F32)
-
-    def early(j, groups, fresh):
-        def step(i, carry):
-            at = pl.ds(pl.multiple_of(i * 256, 256), 256)
-            r = product(j, groups, mixed if SEQUENCE[j] < 2 else mixed_y, i * 256, 256)
-            V[j, at, :] = r if fresh else V[j, at, :] + r
-            return carry
-
-        lax.fori_loop(0, 4, step, 0)
-
-    def first_products():
-        a, b = offsets(0)
-
+        features = pl.ds(pl.multiple_of(half * 512, 512), 512)
+        return jnp.dot(source[at, features], gv[j, features, :], preferred_element_type=F32)
+
+    def early(j):
         def step(i, carry):
             at = pl.ds(pl.multiple_of(i * 512, 512), 512)
-            for source, blocks in ((mixed, (0, 2)), (mixed_y, (1, 3))):
-                lhs = jnp.concatenate([source[at, pl.ds(a, 128)], source[at, pl.ds(b, 128)]], axis=1)
-                rhs = jnp.concatenate(
-                    [jnp.concatenate([gv[j, pl.ds(a, 128), :], gv[j, pl.ds(b, 128), :]], axis=0) for j in blocks], axis=1
-                )
-                r = jnp.dot(lhs, rhs, preferred_element_type=F32)
-                for n, j in enumerate(blocks):
-                    V[j, at, :] = r[:, BLOCK * n : BLOCK * n + BLOCK]
+            V[j, at, :] = product(j, zl, mixed if SEQUENCE[j] < 2 else mixed_y, i * 512, 512)
             return carry
 
         lax.fori_loop(0, 2, step, 0)
 
-    def weighted(j, groups, dim, index):
+    def weighted(j, dim, index):
         total = None
         for k in range(2):
             start = k * 512 + index * 128
-            r = product(j, groups, mixed if dim == "x" else mixed_y, start, 128)
+            r = product(j, 1 - zl, mixed if dim == "x" else mixed_y, start, 128)
             r = r + V[j, pl.ds(pl.multiple_of(start, 128), 128), :]
             w = (sc[k, index] if dim == "x" else sc[k, :, :, index]).reshape(128, 128)
             r = r * expand(w, BLOCK * SEQUENCE[j], BLOCK)
@@ -314,21 +294,17 @@
         mix(0)
     with scope("y0"):
         A[0].from_y("near")
-    with scope("z00"):
-        for b in range(4):
-            A[b].from_z("own")
     with scope("w_tok"):
         cp.wait(tokv.at[1], tok_recv)
     with scope("mix1"):
         mix(1)
     with scope("o0"):
         A[0].from_y("far")
-    with scope("g00"):
-        for b in range(4):
-            A[b].complete("own")
-        first_products()
+    with scope("z00"):
+        A[0].from_z("own")
     with scope("y1"):
         A[1].from_y("near")
+        A[1].from_z("own")
     with scope("w_qk"):
         cp.wait(qkg.at[0:15], qk_recv)
     with scope("qkt"):
@@ -348,8 +324,13 @@
         score(0)
     with scope("o1"):
         A[1].from_y("far")
+    with scope("s0"):
+        A[0].complete("same")
+    with scope("early0"):
+        early(0)
     with scope("y2"):
         A[2].from_y("near")
+        A[2].from_z("own")
     with scope("score1"):
         score(1)
     with scope("o2"):
@@ -358,6 +339,7 @@
         lax.fori_loop(0, 4, pair_stats, 0)
     with scope("y3"):
         A[3].from_y("near")
+        A[3].from_z("own")
     with scope("zy0"):
         A[0].from_z("near")
     with scope("zo0"):
@@ -415,62 +397,76 @@
 
     send1, recv1 = cp.new("send"), [cp.new("recv") for _ in range(4)]
 
-    def reduce1(j, groups):
+    def reduce1(j):
         dim = PARTS[SEQUENCE[j] // 2][2][0]
-        for o in (2, 1, 3):
-            s1[j, o - 1] = weighted(j, groups, dim, (me[dim] + o) % 4).astype(BF16)
-            cp.remote(s1.at[j, o - 1], r1.at[j, o - 1], peer(dim, o), send1, recv1[j])
-        own1[j] = weighted(j, groups, dim, me[dim])
-
-    ALL = (0, 3, 1, 2)
+
+        def send(*offsets):
+            for o in offsets:
+                cp.remote(s1.at[j, o - 1], r1.at[j, o - 1], peer(dim, o), send1, recv1[j])
+
+        for o in (2, 1):
+            s1[j, o - 1] = weighted(j, dim, (me[dim] + o) % 4).astype(BF16)
+        if j == 3:
+            send(2, 1)
+        s1[j, 2] = weighted(j, dim, (me[dim] + 3) % 4).astype(BF16)
+        own1[j] = weighted(j, dim, me[dim])
+        if j == 3:
+            send(3)
+        else:
+            send(2, 1, 3)
 
     with scope("stats0"):
         stats0()
+        B.to_y(2)
+    with scope("s1"):
+        A[1].complete("same")
+    with scope("early1"):
+        early(1)
     with scope("o3"):
         A[3].from_y("far")
     with scope("zy1"):
         A[1].from_z("near")
-    with scope("c00"):
-        A[0].complete("near")
-    with scope("early0"):
-        early(0, (3, 1), False)
+    with scope("s2"):
+        A[2].complete("same")
+    with scope("early2"):
+        early(2)
     with scope("zo1"):
         A[1].from_z("far")
+    with scope("c0"):
+        A[0].complete("cross")
+    with scope("late0"):
+        reduce1(0)
     with scope("zy2"):
         A[2].from_z("near")
-    with scope("c0"):
-        A[0].complete("far")
-    with scope("late0"):
-        reduce1(0, (2,))
-    with scope("B_z0"):
-        B.from_z("own")
+    with scope("s3"):
+        A[3].complete("same")
+    with scope("early3"):
+        early(3)
     with scope("zo2"):
         A[2].from_z("far")
-    with scope("B_y"):
-        B.from_y("near")
     with scope("c1"):
-        A[1].complete("near")
-        A[1].complete("far")
+        A[1].complete("cross")
     with scope("late1"):
-        reduce1(1, ALL[1:])
+        reduce1(1)
     with scope("zy3"):
         A[3].from_z("near")
+    with scope("B_y"):
+        B.from_z("own")
+        B.from_y("near")
+    with scope("c2"):
+        A[2].complete("cross")
+    with scope("late2"):
+        reduce1(2)
     with scope("zo3"):
         A[3].from_z("far")
-    with scope("c2"):
-        A[2].complete("near")
-        A[2].complete("far")
-    with scope("late2"):
-        reduce1(2, ALL[1:])
-    with scope("B_o"):
-        B.from_y("far")
     with scope("stats1"):
         stats1()
     with scope("c3"):
-        A[3].complete("near")
-        A[3].complete("far")
+        A[3].complete("cross")
     with scope("late3"):
-        reduce1(3, ALL[1:])
+        reduce1(3)
+    with scope("B_o"):
+        B.from_y("far")
     with scope("expand1"):
         expand1()
 
@@ -516,8 +512,8 @@
         B.from_z("far")
     context = [result(j) for j in (0, 1, 2)]
     with scope("B_c"):
-        for kind in kinds:
-            B.complete(kind)
+        B.complete("same")
+        B.complete("cross")
     with scope("w_sends0"):
         for gather in A + [B]:
             gather.finish()

time: 37.7 us -> 37.4 us (level)
  no operation moved by 1% of the time
where the time goes in v9:
time: 37.4 us; the launch traced here: 37.3 us
  Pallas kernels  35.9 us (96%)
  local copies, waits for them, and re-layouts  1.32 us (4%)
    pallas_call x1, Pallas kernels, shards(): pl.pallas_call(kernel, out_shape=jax.ShapeDtypeStruct((8, D), BF16), in_s...  35.9 us
    unnamed x1, local copies, waits for them, and re-layouts  1.32 us

profile of v9, /device:TPU:0, one launch (start us, length us, event | category | flops | bytes accessed | tf_op | source)
XLA Modules:
  0.0 37.3 jit_solution(11021384085024143040)
XLA Ops:
  0.0 35.9 %shard_map.73 = bf16[8,1024]{1,0:T(8,128)(2,1)} custom-call(bf16[4,4,4,2,8,1024]{5,4,3,2,1,0:T(8,128)(2,1)} %bitcast.4, bf16[91,1024]{1,0:T(8,128)(2,1)} %emb_h.1, bf16[8,128]{1,0:T(8,128)(2,1)} %bitcast.6, bf16[64,1024]{1,0:T(8,128)(2,1)} %wk.1, bf16[64,1024]{1,0:T(8,128)(2,1)} %wv.1, bf16[64,1024]{1,0:T(8,128)(2,1)} %wo.1, s32[1,91]{1,0:T(1,128)} %bitcast.7), custom_call_target="tpu_custom_call" | custom-call | tf_op jit(solution)/shard_map/pallas_call | solution.py:544
  35.9 1.3 %copy.9 = bf16[1,8,1024]{2,1,0:T(8,128)(2,1)} copy(bf16[1,8,1024]{2,1,0:T(8,128)(2,1)} %bitcast.5) | data formatting | bytes 32768

commit v10 on v9

--- a/solution.py
+++ b/solution.py
@@ -198,7 +198,7 @@
 
     with scope("gatherA"):
         A = [Gather(gv.at[0], load_wv[0])]
-        A[0].start(1, 3, 2)
+        A[0].start(2, 1, 3)
 
     head_lane = lax.broadcasted_iota(jnp.int32, (HEADS, D), 1) // 64
     head_row = lax.broadcasted_iota(jnp.int32, (HEADS, D), 0)
@@ -223,7 +223,7 @@
         cp.remote(tok.at[:, :, :, 1 - c], tokv.at[1], other, tok_send, tok_recv)
         for b in range(1, 4):
             A.append(Gather(gv.at[b], load_wv[b]))
-            A[b].start(1, 3, 2)
+            A[b].start(2, 1, 3)
         B = Gather(go, load_wo)
         B.start(1, 3)
 
@@ -305,6 +305,12 @@
     with scope("y1"):
         A[1].from_y("near")
         A[1].from_z("own")
+    with scope("o1"):
+        A[1].from_y("far")
+    with scope("s0"):
+        A[0].complete("same")
+    with scope("early0"):
+        early(0)
     with scope("w_qk"):
         cp.wait(qkg.at[0:15], qk_recv)
     with scope("qkt"):
@@ -322,28 +328,24 @@
         qkt[...] = jnp.concatenate([q_high, q_low, jnp.zeros((96, D), BF16)], axis=0)
     with scope("score0"):
         score(0)
-    with scope("o1"):
-        A[1].from_y("far")
-    with scope("s0"):
-        A[0].complete("same")
-    with scope("early0"):
-        early(0)
     with scope("y2"):
         A[2].from_y("near")
         A[2].from_z("own")
+    with scope("o2"):
+        A[2].from_y("far")
+    with scope("zy0"):
+        A[0].from_z("near")
     with scope("score1"):
         score(1)
-    with scope("o2"):
-        A[2].from_y("far")
+    with scope("zo0"):
+        A[0].from_z("far")
     with scope("pair_stats"):
         lax.fori_loop(0, 4, pair_stats, 0)
     with scope("y3"):
         A[3].from_y("near")
         A[3].from_z("own")
-    with scope("zy0"):
-        A[0].from_z("near")
-    with scope("zo0"):
-        A[0].from_z("far")
+    with scope("o3"):
+        A[3].from_y("far")
 
     def stats0():
         for t, (l0, w, dims) in zip(T, PARTS):
@@ -418,55 +420,53 @@
     with scope("stats0"):
         stats0()
         B.to_y(2)
+    with scope("zy1"):
+        A[1].from_z("near")
     with scope("s1"):
         A[1].complete("same")
     with scope("early1"):
         early(1)
-    with scope("o3"):
-        A[3].from_y("far")
-    with scope("zy1"):
-        A[1].from_z("near")
-    with scope("s2"):
-        A[2].complete("same")
-    with scope("early2"):
-        early(2)
     with scope("zo1"):
         A[1].from_z("far")
     with scope("c0"):
         A[0].complete("cross")
     with scope("late0"):
         reduce1(0)
+    with scope("s2"):
+        A[2].complete("same")
+    with scope("early2"):
+        early(2)
     with scope("zy2"):
         A[2].from_z("near")
-    with scope("s3"):
-        A[3].complete("same")
-    with scope("early3"):
-        early(3)
     with scope("zo2"):
         A[2].from_z("far")
     with scope("c1"):
         A[1].complete("cross")
     with scope("late1"):
         reduce1(1)
+    with scope("s3"):
+        A[3].complete("same")
+    with scope("early3"):
+        early(3)
     with scope("zy3"):
         A[3].from_z("near")
-    with scope("B_y"):
-        B.from_z("own")
-        B.from_y("near")
+    with scope("zo3"):
+        A[3].from_z("far")
     with scope("c2"):
         A[2].complete("cross")
     with scope("late2"):
         reduce1(2)
-    with scope("zo3"):
-        A[3].from_z("far")
-    with scope("stats1"):
-        stats1()
+    with scope("B_y"):
+        B.from_z("own")
+        B.from_y("near")
     with scope("c3"):
         A[3].complete("cross")
     with scope("late3"):
         reduce1(3)
     with scope("B_o"):
         B.from_y("far")
+    with scope("stats1"):
+        stats1()
     with scope("expand1"):
         expand1()
 
@@ -506,10 +506,10 @@
     with scope("B_z"):
         B.from_z("near")
     reduce2(3)
+    with scope("B_z2"):
+        B.from_z("far")
     with scope("stats2"):
         stats2()
-    with scope("B_z2"):
-        B.from_z("far")
     context = [result(j) for j in (0, 1, 2)]
     with scope("B_c"):
         B.complete("same")

time: 37.4 us -> 36.7 us (0.981)
  Pallas kernels: 35.9 us -> 35.1 us
    pallas_call x1, Pallas kernels: 35.9 us -> 35.1 us  [shards(): pl.pallas_call(kernel, out_shape=jax.ShapeDtypeStruct((8, D), BF16), in_s...]
where the time goes in v10:
time: 36.7 us; the launch traced here: 36.5 us
  Pallas kernels  35.1 us (96%)
  local copies, waits for them, and re-layouts  1.32 us (4%)
    pallas_call x1, Pallas kernels, shards(): pl.pallas_call(kernel, out_shape=jax.ShapeDtypeStruct((8, D), BF16), in_s...  35.1 us
    unnamed x1, local copies, waits for them, and re-layouts  1.32 us

profile of v10, /device:TPU:0, one launch (start us, length us, event | category | flops | bytes accessed | tf_op | source)
XLA Modules:
  0.0 36.5 jit_solution(2973182922401651194)
XLA Ops:
  0.0 35.1 %shard_map.73 = bf16[8,1024]{1,0:T(8,128)(2,1)} custom-call(bf16[4,4,4,2,8,1024]{5,4,3,2,1,0:T(8,128)(2,1)} %bitcast.4, bf16[91,1024]{1,0:T(8,128)(2,1)} %emb_h.1, bf16[8,128]{1,0:T(8,128)(2,1)} %bitcast.6, bf16[64,1024]{1,0:T(8,128)(2,1)} %wk.1, bf16[64,1024]{1,0:T(8,128)(2,1)} %wv.1, bf16[64,1024]{1,0:T(8,128)(2,1)} %wo.1, s32[1,91]{1,0:T(1,128)} %bitcast.7), custom_call_target="tpu_custom_call" | custom-call | tf_op jit(solution)/shard_map/pallas_call | solution.py:544
  35.1 1.3 %copy.9 = bf16[1,8,1024]{2,1,0:T(8,128)(2,1)} copy(bf16[1,8,1024]{2,1,0:T(8,128)(2,1)} %bitcast.5) | data formatting | bytes 32768

commit v11 on v10

--- a/solution.py
+++ b/solution.py
@@ -18,7 +18,7 @@
 PARTS = ((0, 512, ("x", "y", "z")), (512, 512, ("y", "x", "z")))
 SEQUENCE = (0, 2, 1, 3)
 BLOCK = 256
-SENDS, RECVS = 13, 49
+SENDS, RECVS = 10, 49
 
 
 def scope(name):
@@ -101,7 +101,7 @@
 
 
 def kernel(tok, emb_h, query_h, wk, wv, wo, vslot_h, out, emb, query, vslot, wk_v, tokv, mixed, mixed_y,
-           gv, go, V, own1, st0, qk_o, qkg, qkt, er, used, sc, s1, r1, s2, r2, m1, *rest):
+           gv, go, V, own1, st0, qk_o, qkg, qkt, er, used, sc, s1, r1, s2, r2, m1, partial, *rest):
     ssem, rsem, lsem = rest[-3:]
     names = ("ts1", "tr1", "tr2", "ax1", "ax2", "st1", "a1")
     T = [dict(zip(names, rest[i * 7 : (i + 1) * 7])) for i in range(len(PARTS))]
@@ -131,10 +131,9 @@
     kind_of = {0: "own", 1: "near", 2: "far", 3: "near"}
 
     class Gather:
-        def __init__(self, g, local):
-            self.g = g
+        def __init__(self, g, local, send):
+            self.g, self.send = g, send
             local.wait()
-            self.send = cp.new("send")
             self.recv = {name: cp.new("recv") for name in ("ynear", "yfar", "zown", "znear", "zfar", "same", "cross")}
 
         def put(self, o, half, zz, device, recv):
@@ -175,9 +174,6 @@
 
         def complete(self, half):
             cp.wait(self.g.at[0:256, :], self.recv[half])
-
-        def finish(self):
-            cp.wait(self.g.at[pl.ds(0, 960), :], self.send)
 
     with scope("signals"):
         barrier = pltpu.get_barrier_semaphore()
@@ -197,7 +193,8 @@
         pl.semaphore_wait(barrier, len(partners))
 
     with scope("gatherA"):
-        A = [Gather(gv.at[0], load_wv[0])]
+        send_v, send_o = cp.new("send"), cp.new("send")
+        A = [Gather(gv.at[0], load_wv[0], send_v)]
         A[0].start(2, 1, 3)
 
     head_lane = lax.broadcasted_iota(jnp.int32, (HEADS, D), 1) // 64
@@ -222,9 +219,9 @@
         tok_send, tok_recv = cp.new("send"), cp.new("recv")
         cp.remote(tok.at[:, :, :, 1 - c], tokv.at[1], other, tok_send, tok_recv)
         for b in range(1, 4):
-            A.append(Gather(gv.at[b], load_wv[b]))
+            A.append(Gather(gv.at[b], load_wv[b], send_v))
             A[b].start(2, 1, 3)
-        B = Gather(go, load_wo)
+        B = Gather(go, load_wo, send_o)
         B.start(1, 3)
 
     position = vx * 16 + vy
@@ -358,7 +355,7 @@
             for o in (1, 2, 3):
                 cp.remote(t["ts1"].at[o - 1], t["tr1"].at[o - 1], peer(dims[0], o), t["send1"], t["recv1"])
 
-    plane = [(o, p) for o in range(4) for p in range(4) if o or p]
+    plane = sorted([(o, p) for o in range(4) for p in range(4) if o or p], key=lambda q: -sum(min(k, 4 - k) for k in q))
 
     def rest_of(dims):
         return [d for d in NAT if d != dims[0]]
@@ -463,10 +460,10 @@
         A[3].complete("cross")
     with scope("late3"):
         reduce1(3)
+    with scope("stats1"):
+        stats1()
     with scope("B_o"):
         B.from_y("far")
-    with scope("stats1"):
-        stats1()
     with scope("expand1"):
         expand1()
 
@@ -503,30 +500,35 @@
 
     for j in range(3):
         reduce2(j)
+    reduce2(3)
     with scope("B_z"):
         B.from_z("near")
-    reduce2(3)
     with scope("B_z2"):
         B.from_z("far")
     with scope("stats2"):
         stats2()
+    def projected(j, context):
+        rows = slice(BLOCK * SEQUENCE[j], BLOCK * SEQUENCE[j] + BLOCK)
+        return jnp.dot(context.astype(BF16), go[rows, :], preferred_element_type=F32)
+
     context = [result(j) for j in (0, 1, 2)]
     with scope("B_c"):
         B.complete("same")
         B.complete("cross")
+    with scope("tail0"):
+        partial[...] = sum(projected(j, context[j]) for j in (0, 1, 2))
     with scope("w_sends0"):
-        for gather in A + [B]:
-            gather.finish()
+        cp.wait(gv.at[:, 0:960, :], send_v)
+        cp.wait(go.at[0:960, :], send_o)
         cp.wait(qkg.at[0:15], qk_send)
         cp.wait(tokv.at[1], tok_send)
         cp.wait(s1, send1)
         for t in T:
             cp.wait(t["ts1"], t["send1"])
             cp.wait(t["tr2"], t["send2"])
-    context.append(result(3))
+    last = result(3)
     with scope("tail"):
-        context = jnp.concatenate([context[SEQUENCE.index(b)] for b in range(4)], axis=1).astype(BF16)
-        out[...] = jnp.dot(context, go[...], preferred_element_type=F32).astype(BF16)
+        out[...] = (partial[...] + projected(3, last)).astype(BF16)
     with scope("w_sends"):
         cp.wait(r2, send2)
 
@@ -554,7 +556,7 @@
             V((2, 4, 4, 4, 8, 128), F32),
             V((4, 3, 128, BLOCK), BF16), V((4, 3, 128, BLOCK), BF16),
             V((4, 4, 4, 8, BLOCK), BF16), V((4, 15, 8, BLOCK), BF16), V((4, 4, 4, 8, BLOCK), F32),
-            *part,
+            V((8, D), F32), *part,
             pltpu.SemaphoreType.DMA((SENDS,)), pltpu.SemaphoreType.DMA((RECVS,)), pltpu.SemaphoreType.DMA((10,)),
         ],
         compiler_params=pltpu.CompilerParams(

time: 36.7 us -> 36.3 us (0.989)
  Pallas kernels: 35.1 us -> 34.7 us
    pallas_call x1, Pallas kernels: 35.1 us -> 34.7 us  [shards(): pl.pallas_call(kernel, out_shape=jax.ShapeDtypeStruct((8, D), BF16), in_s...]
where the time goes in v11:
time: 36.3 us; the launch traced here: 36 us
  Pallas kernels  34.7 us (96%)
  local copies, waits for them, and re-layouts  1.32 us (4%)
    pallas_call x1, Pallas kernels, shards(): pl.pallas_call(kernel, out_shape=jax.ShapeDtypeStruct((8, D), BF16), in_s...  34.7 us
    unnamed x1, local copies, waits for them, and re-layouts  1.32 us

profile of v11, /device:TPU:0, one launch (start us, length us, event | category | flops | bytes accessed | tf_op | source)
XLA Modules:
  0.0 36.0 jit_solution(10837990182989972431)
XLA Ops:
  0.0 34.7 %shard_map.73 = bf16[8,1024]{1,0:T(8,128)(2,1)} custom-call(bf16[4,4,4,2,8,1024]{5,4,3,2,1,0:T(8,128)(2,1)} %bitcast.4, bf16[91,1024]{1,0:T(8,128)(2,1)} %emb_h.1, bf16[8,128]{1,0:T(8,128)(2,1)} %bitcast.6, bf16[64,1024]{1,0:T(8,128)(2,1)} %wk.1, bf16[64,1024]{1,0:T(8,128)(2,1)} %wv.1, bf16[64,1024]{1,0:T(8,128)(2,1)} %wo.1, s32[1,91]{1,0:T(1,128)} %bitcast.7), custom_call_target="tpu_custom_call" | custom-call | tf_op jit(solution)/shard_map/pallas_call | solution.py:546
  34.7 1.3 %copy.9 = bf16[1,8,1024]{2,1,0:T(8,128)(2,1)} copy(bf16[1,8,1024]{2,1,0:T(8,128)(2,1)} %bitcast.5) | data formatting | bytes 32768

commit v12 on v11

--- a/solution.py
+++ b/solution.py
@@ -18,7 +18,7 @@
 PARTS = ((0, 512, ("x", "y", "z")), (512, 512, ("y", "x", "z")))
 SEQUENCE = (0, 2, 1, 3)
 BLOCK = 256
-SENDS, RECVS = 10, 49
+SENDS, RECVS = 10, 47
 
 
 def scope(name):
@@ -43,9 +43,9 @@
             src_ref=src, dst_ref=dst, send_sem=send, recv_sem=recv, device_id=device, device_id_type=MESH
         ).start()
 
-    def here(self, src, dst):
-        copy = pltpu.make_async_copy(src, dst, self.local.at[self.k])
-        self.k += 1
+    def here(self, src, dst, again=False):
+        self.k += 0 if again else 1
+        copy = pltpu.make_async_copy(src, dst, self.local.at[self.k - 1])
         copy.start()
         return copy
 
@@ -133,7 +133,8 @@
     class Gather:
         def __init__(self, g, local, send):
             self.g, self.send = g, send
-            local.wait()
+            if local is not None:
+                local.wait()
             self.recv = {name: cp.new("recv") for name in ("ynear", "yfar", "zown", "znear", "zfar", "same", "cross")}
 
         def put(self, o, half, zz, device, recv):
@@ -181,7 +182,8 @@
         for p in partners:
             pl.semaphore_signal(barrier, inc=1, device_id=p, device_id_type=MESH)
     own_rows = pl.ds(row_of(y, zl, c), 64)
-    load_wv = [cp.here(wv.at[:, BLOCK * b : BLOCK * b + BLOCK], gv.at[j, own_rows, :]) for j, b in enumerate(SEQUENCE)]
+    _ = [cp.here(wv.at[:, BLOCK * b : BLOCK * b + BLOCK], gv.at[j, own_rows, :], j > 0) for j, b in enumerate(SEQUENCE)]
+    wv_sem = lsem.at[cp.k - 1]
     load_wo = cp.here(wo, go.at[own_rows, :])
     load_wk = cp.here(wk, wk_v.at[pl.ds(0, 64), :])
     load_query = cp.here(query_h, query)
@@ -194,7 +196,8 @@
 
     with scope("gatherA"):
         send_v, send_o = cp.new("send"), cp.new("send")
-        A = [Gather(gv.at[0], load_wv[0], send_v)]
+        cp.wait(gv.at[:, 0:64, :], wv_sem)
+        A = [Gather(gv.at[0], None, send_v)]
         A[0].start(2, 1, 3)
 
     head_lane = lax.broadcasted_iota(jnp.int32, (HEADS, D), 1) // 64
@@ -219,7 +222,7 @@
         tok_send, tok_recv = cp.new("send"), cp.new("recv")
         cp.remote(tok.at[:, :, :, 1 - c], tokv.at[1], other, tok_send, tok_recv)
         for b in range(1, 4):
-            A.append(Gather(gv.at[b], load_wv[b], send_v))
+            A.append(Gather(gv.at[b], None, send_v))
             A[b].start(2, 1, 3)
         B = Gather(go, load_wo, send_o)
         B.start(1, 3)
@@ -467,7 +470,7 @@
     with scope("expand1"):
         expand1()
 
-    send2, recv2 = cp.new("send"), [cp.new("recv") for _ in range(4)]
+    send2, recv2 = cp.new("send"), [cp.new("recv")] * 3 + [cp.new("recv")]
 
     def part_of(j):
         b = SEQUENCE[j]
@@ -492,7 +495,10 @@
         t, dims, cols = part_of(j)
         first, second = rest_of(dims)
         with scope("w_c2"):
-            cp.wait(r2.at[j], recv2[j])
+            if j == 0:
+                cp.wait(r2.at[0:3], recv2[0])
+            elif j == 3:
+                cp.wait(r2.at[3], recv2[3])
         total = t["ax2"][0, :, cols] * m1[j, me[first], me[second]]
         for n in range(15):
             total = total + t["ax2"][n + 1, :, cols] * r2[j, n].astype(F32)
@@ -557,7 +563,7 @@
             V((4, 3, 128, BLOCK), BF16), V((4, 3, 128, BLOCK), BF16),
             V((4, 4, 4, 8, BLOCK), BF16), V((4, 15, 8, BLOCK), BF16), V((4, 4, 4, 8, BLOCK), F32),
             V((8, D), F32), *part,
-            pltpu.SemaphoreType.DMA((SENDS,)), pltpu.SemaphoreType.DMA((RECVS,)), pltpu.SemaphoreType.DMA((10,)),
+            pltpu.SemaphoreType.DMA((SENDS,)), pltpu.SemaphoreType.DMA((RECVS,)), pltpu.SemaphoreType.DMA((7,)),
         ],
         compiler_params=pltpu.CompilerParams(
             collective_id=0, has_side_effects=True, vmem_limit_bytes=60 * 1024 * 1024

time: 36.3 us -> 36.2 us (level)
  no operation moved by 1% of the time
where the time goes in v12:
time: 36.2 us; the launch traced here: 36 us
  Pallas kernels  34.7 us (96%)
  local copies, waits for them, and re-layouts  1.32 us (4%)
    pallas_call x1, Pallas kernels, shards(): pl.pallas_call(kernel, out_shape=jax.ShapeDtypeStruct((8, D), BF16), in_s...  34.7 us
    unnamed x1, local copies, waits for them, and re-layouts  1.32 us

profile of v12, /device:TPU:0, one launch (start us, length us, event | category | flops | bytes accessed | tf_op | source)
XLA Modules:
  0.0 36.0 jit_solution(7412709275958503223)
XLA Ops:
  0.0 34.7 %shard_map.73 = bf16[8,1024]{1,0:T(8,128)(2,1)} custom-call(bf16[4,4,4,2,8,1024]{5,4,3,2,1,0:T(8,128)(2,1)} %bitcast.4, bf16[91,1024]{1,0:T(8,128)(2,1)} %emb_h.1, bf16[8,128]{1,0:T(8,128)(2,1)} %bitcast.6, bf16[64,1024]{1,0:T(8,128)(2,1)} %wk.1, bf16[64,1024]{1,0:T(8,128)(2,1)} %wv.1, bf16[64,1024]{1,0:T(8,128)(2,1)} %wo.1, s32[1,91]{1,0:T(1,128)} %bitcast.7), custom_call_target="tpu_custom_call" | custom-call | tf_op jit(solution)/shard_map/pallas_call | solution.py:552
  34.7 1.3 %copy.9 = bf16[1,8,1024]{2,1,0:T(8,128)(2,1)} copy(bf16[1,8,1024]{2,1,0:T(8,128)(2,1)} %bitcast.5) | data formatting | bytes 32768

commit v13 on v11

--- a/solution.py
+++ b/solution.py
@@ -247,10 +247,12 @@
 
         lax.fori_loop(0, 8, step, 0)
 
-    def score(k):
-        d = lax.dot_general(mixed[k * 512 : k * 512 + 512, :], qkt[...], nt, preferred_element_type=F32)
+    def score():
+        d = lax.dot_general(mixed[...], qkt[...], nt, preferred_element_type=F32)
         d = d + pltpu.roll(d, 112, axis=1)
-        sc[k] = jnp.where(used[k : k + 1, :] > 0, d, BIG).reshape(4, 4, 4, 8, 128)
+        for k in range(2):
+            half = d[512 * k : 512 * k + 512]
+            sc[k] = jnp.where(used[k : k + 1, :] > 0, half, BIG).reshape(4, 4, 4, 8, 128)
 
     def pair_stats(i, carry):
         s0, s1_ = sc[0, i].reshape(128, 128), sc[1, i].reshape(128, 128)
@@ -323,8 +325,8 @@
         q_high = q_keys.astype(BF16)
         q_low = (q_keys - q_high.astype(F32)).astype(BF16)
         qkt[...] = jnp.concatenate([q_high, q_low, jnp.zeros((96, D), BF16)], axis=0)
-    with scope("score0"):
-        score(0)
+    with scope("score"):
+        score()
     with scope("y2"):
         A[2].from_y("near")
         A[2].from_z("own")
@@ -332,8 +334,6 @@
         A[2].from_y("far")
     with scope("zy0"):
         A[0].from_z("near")
-    with scope("score1"):
-        score(1)
     with scope("zo0"):
         A[0].from_z("far")
     with scope("pair_stats"):

time: 36.3 us -> 36.2 us (level)
  no operation moved by 1% of the time
where the time goes in v13:
time: 36.2 us; the launch traced here: 36 us
  Pallas kernels  34.7 us (96%)
  local copies, waits for them, and re-layouts  1.32 us (4%)
    pallas_call x1, Pallas kernels, shards(): pl.pallas_call(kernel, out_shape=jax.ShapeDtypeStruct((8, D), BF16), in_s...  34.7 us
    unnamed x1, local copies, waits for them, and re-layouts  1.32 us

profile of v13, /device:TPU:0, one launch (start us, length us, event | category | flops | bytes accessed | tf_op | source)
XLA Modules:
  0.0 36.0 jit_solution(5027471846227122046)
XLA Ops:
  0.0 34.7 %shard_map.73 = bf16[8,1024]{1,0:T(8,128)(2,1)} custom-call(bf16[4,4,4,2,8,1024]{5,4,3,2,1,0:T(8,128)(2,1)} %bitcast.4, bf16[91,1024]{1,0:T(8,128)(2,1)} %emb_h.1, bf16[8,128]{1,0:T(8,128)(2,1)} %bitcast.6, bf16[64,1024]{1,0:T(8,128)(2,1)} %wk.1, bf16[64,1024]{1,0:T(8,128)(2,1)} %wv.1, bf16[64,1024]{1,0:T(8,128)(2,1)} %wo.1, s32[1,91]{1,0:T(1,128)} %bitcast.7), custom_call_target="tpu_custom_call" | custom-call | tf_op jit(solution)/shard_map/pallas_call | solution.py:546
  34.7 1.3 %copy.9 = bf16[1,8,1024]{2,1,0:T(8,128)(2,1)} copy(bf16[1,8,1024]{2,1,0:T(8,128)(2,1)} %bitcast.5) | data formatting | bytes 32768
